TPU v7x, 32 devices: a whole 2x2x4 slice. The times are simulated.
32 devices in a mesh: seq: 8 (over z, x), batch: 4 (over y, core).
Axes of the slice: x: 2, y: 2, z: 4, core: 2. Of those that a mesh axis runs over, the one named last changes fastest.
Arguments:
- inputs: bfloat16 [4, 4096, 1024], P('batch', 'seq'), may hold values from -6 to 6
- w_key: bfloat16 [1024, 1024], replicated, may hold values from -0.1875 to 0.1875
- w_value: bfloat16 [1024, 1024], replicated, may hold values from -0.1875 to 0.1875
- w_recept: bfloat16 [1024, 1024], replicated, may hold values from -0.1875 to 0.1875
- w_output: bfloat16 [1024, 1024], replicated, may hold values from -2 to 2
- w_ffn_key: bfloat16 [1024, 4096], replicated, may hold values from -0.1875 to 0.1875
- w_ffn_value: bfloat16 [4096, 1024], replicated, may hold values from -0.09375 to 0.09375
- w_ffn_recept: bfloat16 [1024, 1024], replicated, may hold values from -0.1875 to 0.1875
- ln1_gain: float32 [1024], replicated, may hold values from 0.5 to 1.5
- ln1_bias: float32 [1024], replicated, may hold values from -0.5 to 0.5
- mix_key: float32 [1024], replicated, may hold values from 0 to 1
- mix_value: float32 [1024], replicated, may hold values from 0 to 1
- mix_recept: float32 [1024], replicated, may hold values from 0 to 1
- time_decay: float32 [1024], replicated, as said below
- time_first: float32 [1024], replicated, may hold values from -1 to 1
- ln2_gain: float32 [1024], replicated, may hold values from 0.5 to 1.5
- ln2_bias: float32 [1024], replicated, may hold values from -0.5 to 0.5
- ffn_mix_key: float32 [1024], replicated, may hold values from 0 to 1
- ffn_mix_recept: float32 [1024], replicated, may hold values from 0 to 1
- state_num: float32 [1024, 4], P(None, 'batch'), may hold values from -8 to 8
- state_den: float32 [1024, 4], P(None, 'batch'), may hold values from 1 to 8
- state_max: float32 [1024, 4], P(None, 'batch'), may hold values from 0 to 2
- prev_att: float32 [1024, 4], P(None, 'batch'), may hold values from -6 to 6
- prev_ffn: float32 [1024, 4], P(None, 'batch'), may hold values from -6 to 6
- cotangent: bfloat16 [4, 4096, 1024], P('batch', 'seq'), may hold values from -6 to 6
Outputs:
- block_out: bfloat16 [4, 4096, 1024], P('batch', 'seq')
- input_grad: bfloat16 [4, 4096, 1024], P('batch', 'seq')
- grad_w_key: float32 [1024, 1024], P('seq', 'batch')
- grad_w_value: float32 [1024, 1024], P('seq', 'batch')
- grad_w_recept: float32 [1024, 1024], P('seq', 'batch')
- grad_w_output: float32 [1024, 1024], P('seq', 'batch')
- grad_w_ffn_key: float32 [1024, 4096], P('seq', 'batch')
- grad_w_ffn_value: float32 [4096, 1024], P('seq', 'batch')
- grad_w_ffn_recept: float32 [1024, 1024], P('seq', 'batch')
- grad_ln1_gain: float32 [1024], P('seq')
- grad_ln1_bias: float32 [1024], P('seq')
- grad_mix_key: float32 [1024], P('seq')
- grad_mix_value: float32 [1024], P('seq')
- grad_mix_recept: float32 [1024], P('seq')
- grad_time_decay: float32 [1024], P('seq')
- grad_time_first: float32 [1024], P('seq')
- grad_ln2_gain: float32 [1024], P('seq')
- grad_ln2_bias: float32 [1024], P('seq')
- grad_ffn_mix_key: float32 [1024], P('seq')
- grad_ffn_mix_recept: float32 [1024], P('seq')
- grad_state_num: float32 [1024, 4], P('seq', 'batch')
- grad_state_den: float32 [1024, 4], P('seq', 'batch')
- grad_state_max: float32 [1024, 4], P('seq', 'batch')
- grad_prev_att: float32 [1024, 4], P('seq', 'batch')
- grad_prev_ffn: float32 [1024, 4], P('seq', 'batch')
Inputs may be any that keep to these rules, and one draw needn't show every extreme that they name: exp(time_decay) is at most 0.05 in every channel.
All inputs are finite; a program needn't handle non-finite values.
Results may differ from a plain program's by a relative error of at most 0.0095.
Values sent between devices are 32-bit elements; how exact they have to be, the bound alone decides.
A program may use at most 192 MiB of HBM per device.

v0:
```python
from functools import partial

import jax
import jax.numpy as jnp
from jax import lax
from jax.sharding import PartitionSpec as P

BLOCK = 64


far_below = -1e30


def from_behind(block, axis, distance):
    devices = range(lax.axis_size(axis))
    route = [(i - distance, i) for i in devices if i - distance in devices]
    return lax.ppermute(block, axis, route)


def prefix(value, axis, join, neutral, backward):
    count, mine = (lax.axis_size(axis), lax.axis_index(axis))
    pieces = jax.tree.map(lambda part: lax.all_gather(part, axis), value)
    if backward:
        pieces = jax.tree.map(lambda part: part[::-1], pieces)
        mine = count - 1 - mine
    total = jax.tree.map(
        lambda part, zero: jnp.full_like(part, 0) + jnp.asarray(zero, part.dtype), value, neutral
    )

    def turn(position, total):
        longer = join(total, jax.tree.map(lambda part: part[position], pieces))
        return jax.tree.map(lambda new, old: jnp.where(position < mine, new, old), longer, total)

    return lax.fori_loop(0, count - 1, turn, total)


def layer_norm(values, ln_gain, ln_bias):
    centred = values - jnp.mean(values, axis=-1, keepdims=True)
    spread = jnp.mean(centred * centred, axis=-1, keepdims=True)
    return centred * lax.rsqrt(spread + 1e-05) * ln_gain + ln_bias


def matmul(operand, matrix):
    return lax.dot_general(
        operand, matrix, (((operand.ndim - 1,), (0,)), ((), ())), preferred_element_type=jnp.float32
    )


def matmul_back(gradient, matrix):
    return lax.dot_general(
        gradient,
        matrix,
        (((gradient.ndim - 1,), (1,)), ((), ())),
        preferred_element_type=jnp.float32,
    )


def outer_sum(operand, gradient):
    flat_operand = operand.reshape(-1, operand.shape[-1])
    flat_gradient = gradient.reshape(-1, gradient.shape[-1])
    return lax.dot_general(
        flat_operand, flat_gradient, (((0,), (0,)), ((), ())), preferred_element_type=jnp.float32
    )


def token_mix(normed, edge_row, mix_vectors):
    earlier = jnp.concatenate([edge_row[:, None, :], normed[:, :-1, :]], axis=1)
    return tuple((normed * member + earlier * (1.0 - member) for member in mix_vectors))


def gate_rows(recept_rows, mixed_rows):
    return jax.nn.sigmoid(recept_rows) * mixed_rows


def wkv_block(decay_rate, time_first, state_in, inputs_now):
    numerator, denominator, running_max = state_in
    key_rows, value_rows = inputs_now
    length = key_rows.shape[1]
    places = jnp.arange(length, dtype=jnp.float32)[None, :, None]
    own_terms = time_first + key_rows
    anchor = jnp.maximum(
        jnp.maximum(running_max, jnp.max(key_rows, axis=1)), jnp.max(own_terms, axis=1)
    )
    scaled = jnp.exp(key_rows - anchor[:, None, :] - (places + 1.0) * decay_rate)
    running_num = jnp.cumsum(scaled * value_rows, axis=1)
    running_den = jnp.cumsum(scaled, axis=1)
    past_num = jnp.concatenate([jnp.zeros_like(running_num[:, :1]), running_num[:, :-1]], axis=1)
    past_den = jnp.concatenate([jnp.zeros_like(running_den[:, :1]), running_den[:, :-1]], axis=1)
    fading = jnp.exp(places * decay_rate)
    carried = jnp.exp(running_max[:, None, :] + places * decay_rate - anchor[:, None, :])
    own_weight = jnp.exp(own_terms - anchor[:, None, :])
    top_num = past_num * fading + own_weight * value_rows + carried * numerator[:, None, :]
    top_den = past_den * fading + own_weight + carried * denominator[:, None, :]
    outputs = top_num / top_den
    final_terms = key_rows + (length - 1.0 - places) * decay_rate
    kept_max = running_max + length * decay_rate
    new_max = jnp.maximum(kept_max, jnp.max(final_terms, axis=1))
    final_weights = jnp.exp(final_terms - new_max[:, None, :])
    kept_weight = jnp.exp(kept_max - new_max)
    new_num = jnp.sum(final_weights * value_rows, axis=1) + kept_weight * numerator
    new_den = jnp.sum(final_weights, axis=1) + kept_weight * denominator
    return ((new_num, new_den, new_max), outputs)


def wkv_local(key_rows, value_rows, time_decay, time_first, in_num, in_den, in_max):
    decay_rate = -jnp.exp(time_decay)
    block_count = key_rows.shape[1] // BLOCK

    def arrange(values):
        return jnp.moveaxis(
            values.reshape(values.shape[0], block_count, BLOCK, values.shape[2]), 1, 0
        )

    block_step = jax.checkpoint(partial(wkv_block, decay_rate, time_first))
    state_out, outputs = lax.scan(
        block_step, (in_num, in_den, in_max), (arrange(key_rows), arrange(value_rows))
    )
    outputs = jnp.moveaxis(outputs, 0, 1).reshape(key_rows.shape)
    return (outputs, state_out)


def local_summary(key_rows, value_rows, decay_rate):
    length = key_rows.shape[1]
    places = jnp.arange(length, dtype=jnp.float32)[None, :, None]
    terms = key_rows + (length - 1.0 - places) * decay_rate
    top_term = jnp.max(terms, axis=1)
    weights_now = jnp.exp(terms - top_term[:, None, :])
    return (jnp.sum(weights_now * value_rows, axis=1), jnp.sum(weights_now, axis=1), top_term)


def combine_states(earlier_one, later_one):
    earlier_num, earlier_den, earlier_max, earlier_span = earlier_one
    later_num, later_den, later_max, later_span = later_one
    shifted_max = earlier_max + later_span
    top_both = jnp.maximum(shifted_max, later_max)
    weight_early = jnp.exp(shifted_max - top_both)
    weight_late = jnp.exp(later_max - top_both)
    return (
        earlier_num * weight_early + later_num * weight_late,
        earlier_den * weight_early + later_den * weight_late,
        top_both,
        earlier_span + later_span,
    )


def combine_grads(earlier_one, later_one):
    earlier_num, earlier_den, earlier_span = earlier_one
    later_num, later_den, later_span = later_one
    factor = jnp.exp(later_span)
    return (
        later_num + factor * earlier_num,
        later_den + factor * earlier_den,
        earlier_span + later_span,
    )


def local(
    inputs,
    w_key,
    w_value,
    w_recept,
    w_output,
    w_ffn_key,
    w_ffn_value,
    w_ffn_recept,
    ln1_gain,
    ln1_bias,
    mix_key,
    mix_value,
    mix_recept,
    time_decay,
    time_first,
    ln2_gain,
    ln2_bias,
    ffn_mix_key,
    ffn_mix_recept,
    state_num,
    state_den,
    state_max,
    prev_att,
    prev_ffn,
    cotangent,
):
    position = lax.axis_index("seq")
    is_first = position == 0
    start_num = state_num.T
    start_den = state_den.T
    start_max = state_max.T
    before_att = prev_att.T
    before_ffn = prev_ffn.T
    input_rows = inputs.astype(jnp.float32)
    normed, norm_pull = jax.vjp(layer_norm, input_rows, ln1_gain, ln1_bias)
    from_left = from_behind(normed[:, -1, :], "seq", 1)
    edge_att = jnp.where(is_first, before_att, from_left)
    mixed_inputs, mix_pull = jax.vjp(token_mix, normed, edge_att, (mix_key, mix_value, mix_recept))
    key_in = mixed_inputs[0].astype(jnp.bfloat16)
    value_in = mixed_inputs[1].astype(jnp.bfloat16)
    recept_in = mixed_inputs[2].astype(jnp.bfloat16)
    key_rows = matmul(key_in, w_key)
    value_rows = matmul(value_in, w_value)
    recept_rows = matmul(recept_in, w_recept)
    decay_rate = -jnp.exp(time_decay)
    local_len = key_rows.shape[1]
    device_span = jnp.broadcast_to(local_len * decay_rate, start_num.shape)
    own_num, own_den, own_max = local_summary(key_rows, value_rows, decay_rate)
    first_element = combine_states(
        (start_num, start_den, start_max, jnp.zeros_like(device_span)),
        (own_num, own_den, own_max, device_span),
    )
    element_num = jnp.where(is_first, first_element[0], own_num)
    element_den = jnp.where(is_first, first_element[1], own_den)
    element_max = jnp.where(is_first, first_element[2], own_max)
    zero_rows = jnp.zeros_like(start_num)
    identity = (zero_rows, zero_rows, jnp.full_like(start_num, far_below), zero_rows)
    incoming = prefix(
        (element_num, element_den, element_max, device_span), "seq", combine_states, identity, False
    )
    prior_num, prior_den, prior_max = (incoming[0], incoming[1], incoming[2])
    in_num = jnp.where(is_first, start_num, prior_num)
    in_den = jnp.where(is_first, start_den, prior_den)
    in_max = jnp.where(is_first, start_max, prior_max)
    (mixed_rows, state_out), wkv_pull = jax.vjp(
        wkv_local, key_rows, value_rows, time_decay, time_first, in_num, in_den, in_max
    )
    gated, gate_pull = jax.vjp(gate_rows, recept_rows, mixed_rows)
    gated_low = gated.astype(jnp.bfloat16)
    attended = matmul(gated_low, w_output)
    middle = input_rows + attended
    normed_ffn, norm_ffn_pull = jax.vjp(layer_norm, middle, ln2_gain, ln2_bias)
    from_left_ffn = from_behind(normed_ffn[:, -1, :], "seq", 1)
    edge_ffn = jnp.where(is_first, before_ffn, from_left_ffn)
    ffn_inputs, ffn_mix_pull = jax.vjp(
        token_mix, normed_ffn, edge_ffn, (ffn_mix_key, ffn_mix_recept)
    )
    ffn_key_in = ffn_inputs[0].astype(jnp.bfloat16)
    ffn_recept_in = ffn_inputs[1].astype(jnp.bfloat16)
    hidden_pre = matmul(ffn_key_in, w_ffn_key)
    hidden = jnp.square(jax.nn.relu(hidden_pre)).astype(jnp.bfloat16)
    ffn_values = matmul(hidden, w_ffn_value)
    gate_now = jax.nn.sigmoid(matmul(ffn_recept_in, w_ffn_recept))
    block_out = (middle + gate_now * ffn_values).astype(jnp.bfloat16)
    grad_out = cotangent.astype(jnp.float32)
    grad_values = (grad_out * gate_now).astype(jnp.bfloat16)
    grad_gate = (grad_out * ffn_values * gate_now * (1.0 - gate_now)).astype(jnp.bfloat16)
    grad_hidden = matmul_back(grad_values, w_ffn_value)
    grad_pre = (grad_hidden * 2.0 * jax.nn.relu(hidden_pre)).astype(jnp.bfloat16)
    grad_w_ffn_value = outer_sum(hidden, grad_values)
    grad_w_ffn_key = outer_sum(ffn_key_in, grad_pre)
    grad_w_ffn_recept = outer_sum(ffn_recept_in, grad_gate)
    grad_normed_ffn, grad_edge_ffn, ffn_mix_grads = ffn_mix_pull(
        (matmul_back(grad_pre, w_ffn_key), matmul_back(grad_gate, w_ffn_recept))
    )
    from_right_ffn = from_behind(grad_edge_ffn, "seq", -1)
    grad_normed_ffn = grad_normed_ffn.at[:, -1, :].add(from_right_ffn)
    grad_middle, grad_ln2_gain, grad_ln2_bias = norm_ffn_pull(grad_normed_ffn)
    grad_middle = grad_middle + grad_out
    grad_attended = grad_middle.astype(jnp.bfloat16)
    grad_w_output = outer_sum(gated_low, grad_attended)
    grad_recept_full, grad_mixed = gate_pull(matmul_back(grad_attended, w_output))
    grad_recept = grad_recept_full.astype(jnp.bfloat16)
    zero_state = (zero_rows, zero_rows, zero_rows)
    first_pass = wkv_pull((grad_mixed, zero_state))
    unscale = jnp.exp(-in_max)
    local_grad_num = first_pass[4] * unscale
    local_grad_den = first_pass[5] * unscale
    later_grads = prefix(
        (local_grad_num, local_grad_den, device_span),
        "seq",
        combine_grads,
        (zero_rows, zero_rows, zero_rows),
        True,
    )
    exit_num, exit_den = (later_grads[0], later_grads[1])
    out_num, out_den, out_max = state_out
    lifting = jnp.exp(out_max)
    exit_cotangent = (
        exit_num * lifting,
        exit_den * lifting,
        (exit_num * out_num + exit_den * out_den) * lifting,
    )
    second_pass = wkv_pull((jnp.zeros_like(grad_mixed), exit_cotangent))
    grad_key_rows = (first_pass[0] + second_pass[0]).astype(jnp.bfloat16)
    grad_value_rows = (first_pass[1] + second_pass[1]).astype(jnp.bfloat16)
    grad_time_decay = first_pass[2] + second_pass[2]
    grad_time_first = first_pass[3] + second_pass[3]
    grad_start_num = first_pass[4] + second_pass[4]
    grad_start_den = first_pass[5] + second_pass[5]
    grad_start_max = first_pass[6] + second_pass[6]
    grad_w_key = outer_sum(key_in, grad_key_rows)
    grad_w_value = outer_sum(value_in, grad_value_rows)
    grad_w_recept = outer_sum(recept_in, grad_recept)
    grad_normed, grad_edge_att, mix_grads = mix_pull(
        (
            matmul_back(grad_key_rows, w_key),
            matmul_back(grad_value_rows, w_value),
            matmul_back(grad_recept, w_recept),
        )
    )
    from_right = from_behind(grad_edge_att, "seq", -1)
    grad_normed = grad_normed.at[:, -1, :].add(from_right)
    grad_input_ln, grad_ln1_gain, grad_ln1_bias = norm_pull(grad_normed)
    input_grad = (grad_input_ln + grad_middle).astype(jnp.bfloat16)
    start_num_grad = jnp.where(is_first, grad_start_num, 0.0).T
    start_den_grad = jnp.where(is_first, grad_start_den, 0.0).T
    start_max_grad = jnp.where(is_first, grad_start_max, 0.0).T
    edge_att_grad = jnp.where(is_first, grad_edge_att, 0.0).T
    edge_ffn_grad = jnp.where(is_first, grad_edge_ffn, 0.0).T
    row_parts = (
        lax.psum_scatter(grad_w_key, "seq", scatter_dimension=0, tiled=True),
        lax.psum_scatter(grad_w_value, "seq", scatter_dimension=0, tiled=True),
        lax.psum_scatter(grad_w_recept, "seq", scatter_dimension=0, tiled=True),
        lax.psum_scatter(grad_w_output, "seq", scatter_dimension=0, tiled=True),
        lax.psum_scatter(grad_w_ffn_key, "seq", scatter_dimension=0, tiled=True),
        lax.psum_scatter(grad_w_ffn_value, "seq", scatter_dimension=0, tiled=True),
        lax.psum_scatter(grad_w_ffn_recept, "seq", scatter_dimension=0, tiled=True),
        lax.psum_scatter(grad_ln1_gain, "seq", scatter_dimension=0, tiled=True),
        lax.psum_scatter(grad_ln1_bias, "seq", scatter_dimension=0, tiled=True),
        lax.psum_scatter(mix_grads[0], "seq", scatter_dimension=0, tiled=True),
        lax.psum_scatter(mix_grads[1], "seq", scatter_dimension=0, tiled=True),
        lax.psum_scatter(mix_grads[2], "seq", scatter_dimension=0, tiled=True),
        lax.psum_scatter(grad_time_decay, "seq", scatter_dimension=0, tiled=True),
        lax.psum_scatter(grad_time_first, "seq", scatter_dimension=0, tiled=True),
        lax.psum_scatter(grad_ln2_gain, "seq", scatter_dimension=0, tiled=True),
        lax.psum_scatter(grad_ln2_bias, "seq", scatter_dimension=0, tiled=True),
        lax.psum_scatter(ffn_mix_grads[0], "seq", scatter_dimension=0, tiled=True),
        lax.psum_scatter(ffn_mix_grads[1], "seq", scatter_dimension=0, tiled=True),
        lax.psum_scatter(start_num_grad, "seq", scatter_dimension=0, tiled=True),
        lax.psum_scatter(start_den_grad, "seq", scatter_dimension=0, tiled=True),
        lax.psum_scatter(start_max_grad, "seq", scatter_dimension=0, tiled=True),
        lax.psum_scatter(edge_att_grad, "seq", scatter_dimension=0, tiled=True),
        lax.psum_scatter(edge_ffn_grad, "seq", scatter_dimension=0, tiled=True),
    )
    matrix_parts = (
        lax.psum_scatter(row_parts[0], "batch", scatter_dimension=1, tiled=True),
        lax.psum_scatter(row_parts[1], "batch", scatter_dimension=1, tiled=True),
        lax.psum_scatter(row_parts[2], "batch", scatter_dimension=1, tiled=True),
        lax.psum_scatter(row_parts[3], "batch", scatter_dimension=1, tiled=True),
        lax.psum_scatter(row_parts[4], "batch", scatter_dimension=1, tiled=True),
        lax.psum_scatter(row_parts[5], "batch", scatter_dimension=1, tiled=True),
        lax.psum_scatter(row_parts[6], "batch", scatter_dimension=1, tiled=True),
    )
    vector_parts = lax.psum(
        (
            row_parts[7],
            row_parts[8],
            row_parts[9],
            row_parts[10],
            row_parts[11],
            row_parts[12],
            row_parts[13],
            row_parts[14],
            row_parts[15],
            row_parts[16],
            row_parts[17],
        ),
        "batch",
    )
    start_parts = (row_parts[18], row_parts[19], row_parts[20], row_parts[21], row_parts[22])
    return (
        block_out,
        input_grad,
        matrix_parts[0],
        matrix_parts[1],
        matrix_parts[2],
        matrix_parts[3],
        matrix_parts[4],
        matrix_parts[5],
        matrix_parts[6],
        vector_parts[0],
        vector_parts[1],
        vector_parts[2],
        vector_parts[3],
        vector_parts[4],
        vector_parts[5],
        vector_parts[6],
        vector_parts[7],
        vector_parts[8],
        vector_parts[9],
        vector_parts[10],
        start_parts[0],
        start_parts[1],
        start_parts[2],
        start_parts[3],
        start_parts[4],
    )


def solution(mesh):
    placed = (
        P("batch", "seq", None),
        P(),
        P(),
        P(),
        P(),
        P(),
        P(),
        P(),
        P(),
        P(),
        P(),
        P(),
        P(),
        P(),
        P(),
        P(),
        P(),
        P(),
        P(),
        P(None, "batch"),
        P(None, "batch"),
        P(None, "batch"),
        P(None, "batch"),
        P(None, "batch"),
        P("batch", "seq", None),
    )
    return jax.shard_map(
        local,
        mesh=mesh,
        in_specs=placed,
        out_specs=(
            P("batch", "seq", None),
            P("batch", "seq", None),
            P("seq", "batch"),
            P("seq", "batch"),
            P("seq", "batch"),
            P("seq", "batch"),
            P("seq", "batch"),
            P("seq", "batch"),
            P("seq", "batch"),
            P("seq"),
            P("seq"),
            P("seq"),
            P("seq"),
            P("seq"),
            P("seq"),
            P("seq"),
            P("seq"),
            P("seq"),
            P("seq"),
            P("seq"),
            P("seq", "batch"),
            P("seq", "batch"),
            P("seq", "batch"),
            P("seq", "batch"),
            P("seq", "batch"),
        ),
        check_vma=False,
    )
```

profile of v0, /device:TPU:0, one launch (start us, length us, event | category | flops | bytes accessed | tf_op | source)
XLA Modules:
  0.0 2055.2 jit_solution(12698908176369836961)
XLA Ops:
  11.1 5.0 collective-permute-start
  28.9 31.0 %all-gather.2 = f32[8192]{0:T(1024)S(1)} all-gather(f32[1024]{0:T(1024)S(1)} %get-tuple-element.1777), channel_id=4, replica_groups=mesh['seq'=8,'batch'=4] {'seq'}, dimensions={0}, use_global_device_ids=true | all-gather | bytes 36864 | tf_op jit(solution)/shard_map/all_gather | solution.py:22
  59.8 30.6 %all-gather.3 = f32[8192]{0:T(1024)S(1)} all-gather(f32[1024]{0:T(1024)S(1)} %get-tuple-element.1778), channel_id=5, replica_groups=mesh['seq'=8,'batch'=4] {'seq'}, dimensions={0}, use_global_device_ids=true | all-gather | bytes 36864 | tf_op jit(solution)/shard_map/all_gather | solution.py:22
  90.4 30.6 %all-gather = f32[8192]{0:T(1024)S(1)} all-gather(f32[1024]{0:T(1024)S(1)} %get-tuple-element.1775), channel_id=2, replica_groups=mesh['seq'=8,'batch'=4] {'seq'}, dimensions={0}, use_global_device_ids=true | all-gather | bytes 36864 | tf_op jit(solution)/shard_map/all_gather | solution.py:22
  121.0 30.6 %all-gather.1 = f32[8192]{0:T(1024)S(1)} all-gather(f32[1024]{0:T(1024)S(1)} %get-tuple-element.1776), channel_id=3, replica_groups=mesh['seq'=8,'batch'=4] {'seq'}, dimensions={0}, use_global_device_ids=true | all-gather | bytes 36864 | tf_op jit(solution)/shard_map/all_gather | solution.py:22
  153.7 92.8 %while.118 = (s32[]{:T(128)}, f32[1,1024]{1,0:T(1,128)S(1)}, f32[1,1024]{1,0:T(1,128)S(1)}, f32[1,1024]{1,0:T(1,128)S(1)}, f32[8,1,64,1024]{3,2,1,0:T(8,128)}, /...) while((s32[]{:T(128)}, f32[1,1024]{1,0:T(1,128)S(1)}, ...), condition=%wide.region_15.16_spmd.clone.clone, body=%wide.region_7.15_spmd.clone.clone.sunk | while | flops 10293250 | bytes 4643253 | solution.py:115
  246.4 6.0 fusion.88
  260.0 3.6 fusion.99
  263.6 10.8 fusion.136
  277.2 13.1 multiply_convert_fusion
  290.3 12.3 fusion.101
  302.6 7.2 fusion.138
  324.4 3.7 multiply_reduce_fusion.14
  338.8 95.4 %while.115 = (s32[]{:T(128)}, f32[1024]{0:T(1024)S(1)}, f32[1024]{0:T(1024)S(1)}, f32[1,1024]{1,0:T(1,128)S(1)}, f32[1,1024]{1,0:T(1,128)S(1)}, /*index=5*/f32[1...) while((s32[]{:T(128)}, f32[1024]{0:T(1024)S(1)}, ...), condition=%wide.region_42.43_spmd.clone, body=%wide.region_20.42_spmd.clone.sunk | while | flops 23723140 | bytes 14510618 | solution.py:115
  434.3 31.2 %all-gather.6 = f32[8,1,1024]{2,1,0:T(1,128)S(1)} all-gather(f32[1,1,1024]{2,1,0:T(1,128)S(1)} %get-tuple-element.1773), channel_id=6, replica_groups=mesh['seq'=8,'batch'=4] {'seq'}, dimensions={0}, use_global_device_ids=true | all-gather | bytes 36864 | tf_op jit(solution)/shard_map/all_gather | solution.py:22
  465.6 30.6 %all-gather.7 = f32[8,1,1024]{2,1,0:T(1,128)S(1)} all-gather(f32[1,1,1024]{2,1,0:T(1,128)S(1)} %get-tuple-element.1772), channel_id=7, replica_groups=mesh['seq'=8,'batch'=4] {'seq'}, dimensions={0}, use_global_device_ids=true | all-gather | bytes 36864 | tf_op jit(solution)/shard_map/all_gather | solution.py:22
  496.6 5.2 while.116
  505.0 92.2 %while.117 = (s32[]{:T(128)}, f32[1024]{0:T(1024)S(1)}, f32[1024]{0:T(1024)S(1)}, f32[1,1024]{1,0:T(1,128)S(1)}, f32[1,1024]{1,0:T(1,128)S(1)}, /*index=5*/f32[1...) while((s32[]{:T(128)}, f32[1024]{0:T(1024)S(1)}, ...), condition=%wide.region_67.68_spmd.clone, body=%wide.region_45.67_spmd.clone.sunk | while | flops 23720068 | bytes 14371364 | solution.py:115
  599.8 3.2 fusion.143
  607.6 3.3 fusion.142
  612.5 3.2 fusion.144
  617.4 4.8 fusion.117
  623.4 10.5 fusion.145
  635.1 14.5 fusion.92
  651.7 3.4 fusion.140
  664.6 3.8 multiply_reduce_fusion.15
  671.6 20.5 reduce-scatter.34.cloned.1.call-done
  692.1 91.6 %reduce-scatter.30.cloned.1.call-done = f32[128,1024]{1,0:T(8,128)} async-done(((f32[1024,1024]{1,0:T(8,128)}), f32[128,1024]{1,0:T(8,128)}) %reduce-scatter.30.cloned.1.call-update) | async-done | bytes 524304 | tf_op jit(solution)/shard_map/reduce_scatter | solution.py:309
  783.8 91.4 %reduce-scatter.42.cloned.1.call-done = f32[128,1024]{1,0:T(8,128)} async-done(((f32[1024,1024]{1,0:T(8,128)}), f32[128,1024]{1,0:T(8,128)}) %reduce-scatter.42.cloned.1.call-update) | async-done | bytes 524304 | tf_op jit(solution)/shard_map/reduce_scatter | solution.py:312
  875.3 91.4 %reduce-scatter.38.cloned.1.call-done = f32[128,1024]{1,0:T(8,128)} async-done(((f32[1024,1024]{1,0:T(8,128)}), f32[128,1024]{1,0:T(8,128)}) %reduce-scatter.38.cloned.1.call-update) | async-done | bytes 524304 | tf_op jit(solution)/shard_map/reduce_scatter | solution.py:311
  966.8 282.7 %reduce-scatter.46.cloned.1.call-done = f32[128,4096]{1,0:T(8,128)} async-done(((f32[1024,4096]{1,0:T(8,128)}), f32[128,4096]{1,0:T(8,128)}) %reduce-scatter.46.cloned.1.call-update) | async-done | bytes 2097168 | tf_op jit(solution)/shard_map/reduce_scatter | solution.py:313
  1249.6 283.1 %reduce-scatter.50.cloned.1.call-done = f32[512,1024]{1,0:T(8,128)} async-done(((f32[4096,1024]{1,0:T(8,128)}), f32[512,1024]{1,0:T(8,128)}) %reduce-scatter.50.cloned.1.call-update) | async-done | bytes 2097168 | tf_op jit(solution)/shard_map/reduce_scatter | solution.py:314
  1542.7 3.4 fusion.84
  1546.1 36.1 %all-reduce.19 = (f32[1024]{0:T(1024)S(1)}, f32[1024]{0:T(1024)S(1)}, f32[1024]{0:T(1024)S(1)}, f32[1024]{0:T(1024)S(1)}, f32[1024]{0:T(1024)S(1)}, /*index=5*/f...) all-reduce(f32[1024]{0:T(1024)S(1)} %get-tuple-element.1482, ...), channel_id=22, replica_groups=mesh['seq'=8,'batch'=4] {'seq'}, use_global_device_ids=true, to_apply=%region_85.86.clone | all-reduce | flops 11264 | bytes 90112
  1583.1 14.7 reduce-scatter.66.cloned.1.call-done
  1599.2 6.3 all-reduce.20
  1605.5 4.0 add_convert_fusion
  1609.5 53.4 %reduce-scatter.62.cloned.1.call-done = f32[128,1]{1,0:T(8,128)} async-done(((f32[1024,1]{1,0:T(8,128)}), f32[128,1]{1,0:T(8,128)}) %reduce-scatter.62.cloned.1.call-update) | async-done | bytes 528
  1664.3 63.4 %reduce-scatter.60.cloned.1.call-done = f32[128,1]{1,0:T(8,128)} async-done(((f32[1024,1]{1,0:T(8,128)}), f32[128,1]{1,0:T(8,128)}) %reduce-scatter.60.cloned.1.call-update) | async-done | bytes 528
  1729.2 63.6 %reduce-scatter.58.cloned.1.call-done = f32[128,1]{1,0:T(8,128)} async-done(((f32[1024,1]{1,0:T(8,128)}), f32[128,1]{1,0:T(8,128)}) %reduce-scatter.58.cloned.1.call-update) | async-done | bytes 528
  1794.2 63.5 %reduce-scatter.64.cloned.1.call-done = f32[128,1]{1,0:T(8,128)} async-done(((f32[1024,1]{1,0:T(8,128)}), f32[128,1]{1,0:T(8,128)}) %reduce-scatter.64.cloned.1.call-update) | async-done | bytes 528
  1859.1 22.3 %reduce-scatter.56.cloned.1.call-done = f32[128,256]{1,0:T(8,128)} async-done(((f32[128,1024]{1,0:T(8,128)}), f32[128,256]{1,0:T(8,128)}) %reduce-scatter.56.cloned.1.call-update) | async-done | bytes 131088 | tf_op jit(solution)/shard_map/reduce_scatter | solution.py:340
  1881.4 24.6 %reduce-scatter.36.cloned.1.call-done = f32[128,256]{1,0:T(8,128)} async-done(((f32[128,1024]{1,0:T(8,128)}), f32[128,256]{1,0:T(8,128)}) %reduce-scatter.36.cloned.1.call-update) | async-done | bytes 131088 | tf_op jit(solution)/shard_map/reduce_scatter | solution.py:335
  1906.0 24.6 %reduce-scatter.32.cloned.1.call-done = f32[128,256]{1,0:T(8,128)} async-done(((f32[128,1024]{1,0:T(8,128)}), f32[128,256]{1,0:T(8,128)}) %reduce-scatter.32.cloned.1.call-update) | async-done | bytes 131088 | tf_op jit(solution)/shard_map/reduce_scatter | solution.py:334
  1930.6 24.6 %reduce-scatter.44.cloned.1.call-done = f32[128,256]{1,0:T(8,128)} async-done(((f32[128,1024]{1,0:T(8,128)}), f32[128,256]{1,0:T(8,128)}) %reduce-scatter.44.cloned.1.call-update) | async-done | bytes 131088 | tf_op jit(solution)/shard_map/reduce_scatter | solution.py:337
  1955.1 24.6 %reduce-scatter.40.cloned.1.call-done = f32[128,256]{1,0:T(8,128)} async-done(((f32[128,1024]{1,0:T(8,128)}), f32[128,256]{1,0:T(8,128)}) %reduce-scatter.40.cloned.1.call-update) | async-done | bytes 131088 | tf_op jit(solution)/shard_map/reduce_scatter | solution.py:336
  1979.7 34.2 %reduce-scatter.48.cloned.1.call-done = f32[128,1024]{1,0:T(8,128)} async-done(((f32[128,4096]{1,0:T(8,128)}), f32[128,1024]{1,0:T(8,128)}) %reduce-scatter.48.cloned.1.call-update) | async-done | bytes 524304 | tf_op jit(solution)/shard_map/reduce_scatter | solution.py:338
  2013.9 34.3 %reduce-scatter.52.cloned.1.call-done = f32[512,256]{1,0:T(8,128)} async-done(((f32[512,1024]{1,0:T(8,128)}), f32[512,256]{1,0:T(8,128)}) %reduce-scatter.52.cloned.1.call-update) | async-done | bytes 524304 | tf_op jit(solution)/shard_map/reduce_scatter | solution.py:339
  (1032 shorter events, 384.3 us)
Async XLA Ops:
  7.2 245.2 %copy-start = (bf16[1024,1024]{1,0:T(8,128)(2,1)S(1)}, bf16[1024,1024]{1,0:T(8,128)(2,1)}, u32[]{:S(2)}) copy-start(bf16[1024,1024]{1,0:T(8,128)(2,1)} %param.43) | copy-start | bytes 6291460
  7.3 663.6 %reduce-scatter.54.cloned.1.call-start = ((), (), s32[]{:S(2)}) async-start(), calls=%async_computation.31 | async-start | bytes 4718592 | tf_op jit(solution)/shard_map/reduce_scatter | solution.py:315
  10.5 8.1 copy-start.71
  11.0 7.6 copy-start.55
  11.0 7.6 copy-start.69
  11.1 7.7 copy-start.78
  11.1 8.2 copy-start.61
  11.1 8.2 copy-start.63
  11.1 9.4 copy-start.86
  11.1 9.4 collective-permute-start
  28.8 124.8 %copy-start.14 = (f32[1024]{0:T(1024)S(1)}, f32[1024]{0:T(1024)}, u32[]{:S(2)}) copy-start(f32[1024]{0:T(1024)} %param.53) | copy-start | bytes 12292
  255.1 4.8 collective-permute-start.1
  263.5 10.8 copy-start.36
  263.5 10.8 copy-start.30
  263.5 10.8 copy-start.88
  277.2 13.1 copy-start.3
  290.3 12.3 copy-start.32
  316.7 5.5 collective-permute-start.2
  321.3 370.8 %reduce-scatter.34.cloned.1.call-start = ((), (), s32[]{:S(2)}) async-start(), calls=%async_computation.21 | async-start | bytes 4718592 | tf_op jit(solution)/shard_map/reduce_scatter | solution.py:310
  338.8 95.5 %copy-start.68 = (f32[1,1024]{1,0:T(1,128)S(1)}, f32[1,1024]{1,0:T(1,128)}, u32[]{:S(2)}) copy-start(f32[1,1024]{1,0:T(1,128)} %copy-done.67) | copy-start | bytes 12292
  603.1 180.6 %reduce-scatter.30.cloned.1.call-start = ((), (), s32[]{:S(2)}) async-start(), calls=%async_computation.19 | async-start | bytes 4718592 | tf_op jit(solution)/shard_map/reduce_scatter | solution.py:309
  611.0 264.2 %reduce-scatter.42.cloned.1.call-start = ((), (), s32[]{:S(2)}) async-start(), calls=%async_computation.25 | async-start | bytes 4718592 | tf_op jit(solution)/shard_map/reduce_scatter | solution.py:312
  615.8 350.9 %reduce-scatter.38.cloned.1.call-start = ((), (), s32[]{:S(2)}) async-start(), calls=%async_computation.23 | async-start | bytes 4718592 | tf_op jit(solution)/shard_map/reduce_scatter | solution.py:311
  622.2 627.3 %reduce-scatter.46.cloned.1.call-start = ((), (), s32[]{:S(2)}) async-start(), calls=%async_computation.27 | async-start | bytes 18874368 | tf_op jit(solution)/shard_map/reduce_scatter | solution.py:313
  633.9 898.8 %reduce-scatter.50.cloned.1.call-start = ((), (), s32[]{:S(2)}) async-start(), calls=%async_computation.29 | async-start | bytes 18874368 | tf_op jit(solution)/shard_map/reduce_scatter | solution.py:314
  649.6 948.2 %reduce-scatter.66.cloned.1.call-start = ((), (), s32[]{:S(2)}) async-start(), calls=%async_computation.37 | async-start | bytes 589824
  651.4 1011.5 %reduce-scatter.62.cloned.1.call-start = ((), (), s32[]{:S(2)}) async-start(), calls=%async_computation.35 | async-start | bytes 589824
  655.1 9.5 copy-start.10
  662.3 1065.5 %reduce-scatter.60.cloned.1.call-start = ((), (), s32[]{:S(2)}) async-start(), calls=%async_computation.34 | async-start | bytes 589824
  663.4 1129.4 %reduce-scatter.58.cloned.1.call-start = ((), (), s32[]{:S(2)}) async-start(), calls=%async_computation.33 | async-start | bytes 589824
  664.5 1193.1 %reduce-scatter.64.cloned.1.call-start = ((), (), s32[]{:S(2)}) async-start(), calls=%async_computation.36 | async-start | bytes 589824
  670.8 1210.6 %reduce-scatter.56.cloned.1.call-start = ((), (), s32[]{:S(2)}) async-start(), calls=%async_computation.32 | async-start | bytes 655360 | tf_op jit(solution)/shard_map/reduce_scatter | solution.py:340
  671.5 1234.5 %reduce-scatter.36.cloned.1.call-start = ((), (), s32[]{:S(2)}) async-start(), calls=%async_computation.22 | async-start | bytes 655360 | tf_op jit(solution)/shard_map/reduce_scatter | solution.py:335
  692.1 1238.5 %reduce-scatter.32.cloned.1.call-start = ((), (), s32[]{:S(2)}) async-start(), calls=%async_computation.20 | async-start | bytes 655360 | tf_op jit(solution)/shard_map/reduce_scatter | solution.py:334
  783.7 1171.4 %reduce-scatter.44.cloned.1.call-start = ((), (), s32[]{:S(2)}) async-start(), calls=%async_computation.26 | async-start | bytes 655360 | tf_op jit(solution)/shard_map/reduce_scatter | solution.py:337
  875.2 660.8 %copy-start.54 = (f32[1024]{0:T(1024)S(1)}, f32[1024]{0:T(1024)}, u32[]{:S(2)}) copy-start(f32[1024]{0:T(1024)} %param.50) | copy-start | bytes 12292
  875.2 660.8 %copy-start.56 = (f32[1024]{0:T(1024)S(1)}, f32[1024]{0:T(1024)}, u32[]{:S(2)}) copy-start(f32[1024]{0:T(1024)} %param.49) | copy-start | bytes 12292
  875.2 1104.5 %reduce-scatter.40.cloned.1.call-start = ((), (), s32[]{:S(2)}) async-start(), calls=%async_computation.24 | async-start | bytes 655360 | tf_op jit(solution)/shard_map/reduce_scatter | solution.py:336
  966.7 1047.1 %reduce-scatter.48.cloned.1.call-start = ((), (), s32[]{:S(2)}) async-start(), calls=%async_computation.28 | async-start | bytes 2621440 | tf_op jit(solution)/shard_map/reduce_scatter | solution.py:338
  1249.5 283.2 %copy-start.94 = (u32[32]{0:T(128)S(1)}, u32[32]{0:T(128)}, u32[]{:S(2)}) copy-start(u32[32]{0:T(128)} %constant.402) | copy-start | bytes 388
  1249.5 284.5 %copy-start.74 = (f32[1024]{0:T(1024)S(1)}, f32[1024]{0:T(1024)}, u32[]{:S(2)}) copy-start(f32[1024]{0:T(1024)} %get-tuple-element.1468) | copy-start | bytes 12292
  1249.5 284.5 %copy-start.76 = (f32[1024]{0:T(1024)S(1)}, f32[1024]{0:T(1024)}, u32[]{:S(2)}) copy-start(f32[1024]{0:T(1024)} %get-tuple-element.1473) | copy-start | bytes 12292
  1249.5 284.5 %copy-start.73 = (f32[1024]{0:T(1024)S(1)}, f32[1024]{0:T(1024)}, u32[]{:S(2)}) copy-start(f32[1024]{0:T(1024)} %get-tuple-element.1469) | copy-start | bytes 12292
  1249.5 284.5 %copy-start.75 = (f32[1024]{0:T(1024)S(1)}, f32[1024]{0:T(1024)}, u32[]{:S(2)}) copy-start(f32[1024]{0:T(1024)} %get-tuple-element.1474) | copy-start | bytes 12292
  1249.5 284.5 %copy-start.21 = (f32[1,512,1024]{2,1,0:T(8,128)S(1)}, f32[1,512,1024]{2,1,0:T(8,128)}, u32[]{:S(2)}) copy-start(f32[1,512,1024]{2,1,0:T(8,128)} %copy-done.20) | copy-start | bytes 6291460
  1249.5 798.6 %reduce-scatter.52.cloned.1.call-start = ((), (), s32[]{:S(2)}) async-start(), calls=%async_computation.30 | async-start | bytes 2621440 | tf_op jit(solution)/shard_map/reduce_scatter | solution.py:339
  1534.4 5.8 collective-permute-start.3
  1605.5 442.7 %copy-start.1 = (bf16[1024,1024]{1,0:T(8,128)(2,1)S(1)}, bf16[1024,1024]{1,0:T(8,128)(2,1)}, u32[]{:S(2)}) copy-start(bf16[1024,1024]{1,0:T(8,128)(2,1)} %param.43) | copy-start | bytes 6291460
  (91 other events, 225.0 us)
Sparse Core Ops, SparseCore 0:
  321.4 90.3 reduce-scatter.53
  603.2 88.8 reduce-scatter.33
  695.7 87.9 reduce-scatter.29
  787.2 87.9 reduce-scatter.41
  878.7 87.9 reduce-scatter.37
  970.3 279.1 reduce-scatter.45
  1253.3 279.3 reduce-scatter.49
  1536.0 61.7 reduce-scatter.65
  1601.2 61.6 reduce-scatter.61
  1666.1 61.6 reduce-scatter.59
  1731.1 61.6 reduce-scatter.57
  1796.0 61.6 reduce-scatter.63
  1860.7 20.6 reduce-scatter.55
  1884.3 21.6 reduce-scatter.35
  1908.9 21.6 reduce-scatter.31
  1933.5 21.6 reduce-scatter.43
  1958.0 21.6 reduce-scatter.39
  1982.7 31.1 reduce-scatter.47
  2017.0 31.1 reduce-scatter.51
where the time goes:
time: 2070 us; the launch traced here: 2060 us
  waiting for transfers between devices  1310 us (63%)
  other arithmetic  263 us (13%)
  blocking collectives  227 us (11%)
  matrix products  113 us (5%)
  local copies, waits for them, and re-layouts  110 us (5%)
    reduce_scatter x1, waiting for transfers between devices, local(): lax.psum_scatter(grad_w_ffn_value, 'seq', scatter_dimension=0, tiled=True)  283 us
    reduce_scatter x1, waiting for transfers between devices, local(): lax.psum_scatter(grad_w_ffn_key, 'seq', scatter_dimension=0, tiled=True)  283 us
    unnamed x24, waiting for transfers between devices  260 us
    all_gather x6, blocking collectives, prefix(): pieces = jax.tree.map(lambda part: lax.all_gather(part, axis), value)  185 us
    reduce_scatter x1, waiting for transfers between devices, local(): lax.psum_scatter(grad_w_key, 'seq', scatter_dimension=0, tiled=True)  91.6 us
    reduce_scatter x1, waiting for transfers between devices, local(): lax.psum_scatter(grad_w_output, 'seq', scatter_dimension=0, tiled=True)  91.4 us
    reduce_scatter x1, waiting for transfers between devices, local(): lax.psum_scatter(grad_w_recept, 'seq', scatter_dimension=0, tiled=True)  91.4 us
    another operation x40, other arithmetic, wkv_block(): running_num = jnp.cumsum(scaled * value_rows, axis=1)  53.9 us
  transfers between devices with their start and end apart: 23, of which 20 were waited for; matrix products, arithmetic and copies ran while one was open for 14% of the time, Pallas kernels for 0%

commit v1 on v0

--- a/solution.py
+++ b/solution.py
@@ -1,9 +1,507 @@
+import functools
 from functools import partial
 
 import jax
 import jax.numpy as jnp
 from jax import lax
+from jax.experimental import pallas as pl
+from jax.experimental.pallas import tpu as pltpu
 from jax.sharding import PartitionSpec as P
+
+MESH = pl.DeviceIdType.MESH
+F32 = jnp.float32
+BF = jnp.bfloat16
+
+
+def contract0(a, b):
+    return lax.dot_general(a, b, (((0,), (0,)), ((), ())), preferred_element_type=F32)
+
+
+class Place:
+    def __init__(self, nz, nx, ny):
+        s, b = lax.axis_index("seq"), lax.axis_index("batch")
+        self.nz, self.nx, self.ny = nz, nx, ny
+        self.z, self.x = s // nx, s % nx
+        self.y, self.c = b // 2, b % 2
+
+    def at(self, z=None, x=None, y=None, c=None):
+        z = self.z if z is None else z
+        x = self.x if x is None else x
+        y = self.y if y is None else y
+        c = self.c if c is None else c
+        return (z * self.nx + x, y * 2 + c)
+
+
+NZ = 4
+LAG = 4
+SLOTF = 8
+
+
+def rs_kernel(nm, *refs):
+    lhs = refs[:7]
+    rhs = refs[7:14]
+    sm_in = refs[14]
+    outs = refs[15:22]
+    sm_out = refs[22]
+    (lbuf, rbuf, acc, sbuf, rF, rS, rZ, smb, smr, lsem, rsem, s0s, s0r, sFs, sFr, sSs, sSr, sZs, sZr, osem, msem, mss, msr) = refs[23:]
+    nk = 2 * nm
+    me = Place(NZ, 2, 2)
+    z, x, y, c = me.z, me.x, me.y, me.c
+
+    bar = pltpu.get_barrier_semaphore()
+
+    def sig(dev):
+        pl.semaphore_signal(bar, inc=1, device_id=dev, device_id_type=MESH)
+
+    sig(me.at(c=1 - c))
+    sig(me.at(x=1 - x))
+    sig(me.at(y=1 - y))
+
+    @pl.when(z > 0)
+    def _():
+        sig(me.at(z=z - 1))
+
+    @pl.when(z < NZ - 1)
+    def _():
+        sig(me.at(z=z + 1))
+
+    def fs(h):
+        f = jnp.where(h == 0, x, y)
+        s = jnp.where(h == 0, y, x)
+        return f, s
+
+    def partnerF(h):
+        a, b = me.at(x=1 - x), me.at(y=1 - y)
+        return (jnp.where(h == 0, a[0], b[0]), jnp.where(h == 0, a[1], b[1]))
+
+    def partnerS(h):
+        return partnerF(1 - h)
+
+    def rcopy(src, dst, ss, rs, dev):
+        return pltpu.make_async_remote_copy(src_ref=src, dst_ref=dst, send_sem=ss, recv_sem=rs, device_id=dev, device_id_type=MESH)
+
+    def copy0(k):
+        return rcopy(sbuf.at[lax.rem(k, 3)], acc.at[k], s0s.at[k], s0r.at[k], me.at(c=1 - c))
+
+    def copyF(k):
+        h = lax.rem(k, 2)
+        f, s = fs(h)
+        return rcopy(acc.at[k, 1 - f], rF.at[lax.rem(k, SLOTF)], sFs.at[k], sFr.at[k], partnerF(h))
+
+    def copySA(k):
+        h = lax.rem(k, 2)
+        f, s = fs(h)
+        return rcopy(acc.at[k, f, 1 - s], rS.at[k], sSs.at[k], sSr.at[k], partnerS(h))
+
+    def copySE(k):
+        h = lax.rem(k, 2)
+        f, s = fs(h)
+        return rcopy(acc.at[k, f, 1 - s, z], rS.at[k, 0], sSs.at[k], sSr.at[k], partnerS(h))
+
+    def unit(k, q, late):
+        f, s = fs(lax.rem(k, 2))
+        if late:
+            return acc.at[k, f, s, q]
+        return acc.at[k, f, :, q]
+
+    def zbuf(k, slot, late):
+        if late:
+            return rZ.at[k, slot, 0]
+        return rZ.at[k, slot]
+
+    def copyR(k, q, late):
+        return rcopy(unit(k, q, late), zbuf(k, q + 1, late), sZs.at[k, q], sZr.at[k, q + 1], me.at(z=z + 1))
+
+    def copyL(k, q, late):
+        return rcopy(unit(k, q, late), zbuf(k, q, late), sZs.at[k, q], sZr.at[k, q], me.at(z=z - 1))
+
+    def add_into(dst, src):
+        dst[...] = dst[...] + src[...]
+
+    def zadd(k, q, slot, late):
+        f, s = fs(lax.rem(k, 2))
+        if late:
+            add_into(acc.at[k, f, s, q], rZ.at[k, slot, 0])
+        else:
+            for i in range(2):
+                add_into(acc.at[k, f, i, q], rZ.at[k, slot, i])
+
+    def zsub(k, tau, late):
+        n = NZ
+
+        @pl.when(z <= tau)
+        def _():
+            q = n - 1 - tau + z
+
+            @pl.when(z > 0)
+            def _():
+                copyR(k, q, late).wait_recv()
+                zadd(k, q, q + 1, late)
+
+            copyR(k, q, late).start()
+
+        @pl.when(n - 1 - z <= tau)
+        def _():
+            q = tau - (n - 1 - z)
+
+            @pl.when(z < n - 1)
+            def _():
+                copyL(k, q, late).wait_recv()
+                zadd(k, q, q, late)
+
+            copyL(k, q, late).start()
+
+    def zfin(k, late):
+        @pl.when(z > 0)
+        def _():
+            copyR(k, z, late).wait_recv()
+            zadd(k, z, z + 1, late)
+
+        @pl.when(z < NZ - 1)
+        def _():
+            copyL(k, z, late).wait_recv()
+            zadd(k, z, z, late)
+
+    def operands(m, slot):
+        return (pltpu.make_async_copy(lhs[0], lbuf.at[slot], lsem.at[slot]),
+                pltpu.make_async_copy(rhs[0], rbuf.at[slot], rsem.at[slot]))
+
+    def fetch(m, slot):
+        for j in range(4):
+            @pl.when(m == j)
+            def _(j=j):
+                for s in range(8):
+                    pltpu.make_async_copy(lhs[5].at[:, pl.ds(s * 512 + j * 128, 128)], lbuf.at[slot, :, pl.ds(s * 128, 128)], lsem.at[slot]).start()
+                pltpu.make_async_copy(rhs[5], rbuf.at[slot], rsem.at[slot]).start()
+
+            @pl.when(m == 4 + j)
+            def _(j=j):
+                for s in range(8):
+                    pltpu.make_async_copy(rhs[4].at[:, pl.ds(s * 512 + j * 128, 128)], rbuf.at[slot, :, pl.ds(s * 128, 128)], rsem.at[slot]).start()
+                pltpu.make_async_copy(lhs[4], lbuf.at[slot], lsem.at[slot]).start()
+
+        for mm, i in ((8, 6), (9, 3), (10, 2), (11, 1), (12, 0)):
+            @pl.when(m == mm)
+            def _(i=i):
+                pltpu.make_async_copy(lhs[i], lbuf.at[slot], lsem.at[slot]).start()
+                pltpu.make_async_copy(rhs[i], rbuf.at[slot], rsem.at[slot]).start()
+
+    def wait_fetch(slot):
+        for cp in operands(0, slot):
+            cp.wait()
+
+    def columns(slot, h, core):
+        parts = []
+        for yy in range(2):
+            start = pl.multiple_of((2 * yy + core) * 256 + h * 128, 128)
+            parts.append(rbuf[slot, :, pl.ds(start, 128)])
+        return jnp.concatenate(parts, axis=1)
+
+    def gradient(k, core, write):
+        h = lax.rem(k, 2)
+        slot = lax.rem(k // 2, 2)
+        cols = columns(slot, h, core)
+
+        def group(g, _):
+            rows = lbuf[slot, :, pl.ds(pl.multiple_of(g * 512, 512), 512)]
+            res = contract0(rows, cols)
+            for i in range(4):
+                zz, xx = g * 2 + i // 2, i % 2
+                for yy in range(2):
+                    f = jnp.where(h == 0, xx, yy)
+                    s = jnp.where(h == 0, yy, xx)
+                    write(f, s, zz, res[i * 128:(i + 1) * 128, yy * 128:(yy + 1) * 128])
+            return 0
+
+        lax.fori_loop(0, 2, group, 0)
+
+    def taskP(k):
+        slot = lax.rem(k, 3)
+
+        @pl.when(k >= 3)
+        def _():
+            copy0(k - 3).wait_send()
+
+        def write(f, s, zz, v):
+            sbuf[slot, f, s, zz] = v
+
+        gradient(k, 1 - c, write)
+        copy0(k).start()
+
+    def task1(k):
+        copy0(k).wait_recv()
+
+        def write(f, s, zz, v):
+            acc[k, f, s, zz] = acc[k, f, s, zz] + v
+
+        gradient(k, c, write)
+        copyF(k).start()
+
+    def is_late(k):
+        return lax.rem(k // 2, 3) == 0
+
+    def task2(k):
+        copyF(k).wait_recv()
+        f, s = fs(lax.rem(k, 2))
+        slot = lax.rem(k, SLOTF)
+
+        def body(i, _):
+            add_into(acc.at[k, f, i // NZ, lax.rem(i, NZ)], rF.at[slot, i // NZ, lax.rem(i, NZ)])
+            return 0
+
+        lax.fori_loop(0, 2 * NZ, body, 0)
+
+        @pl.when(is_late(k))
+        def _():
+            copySA(k).start()
+
+        @pl.when(jnp.logical_not(is_late(k)))
+        def _():
+            zsub(k, 0, False)
+
+    def taskSA(k):
+        @pl.when(is_late(k))
+        def _():
+            copySA(k).wait_recv()
+            f, s = fs(lax.rem(k, 2))
+
+            def body(i, _):
+                add_into(acc.at[k, f, s, i], rS.at[k, i])
+                return 0
+
+            lax.fori_loop(0, NZ, body, 0)
+            zsub(k, 0, True)
+
+    def taskZA(tau, k):
+        @pl.when(is_late(k))
+        def _():
+            zsub(k, tau, True)
+
+    def taskZE(tau, k):
+        @pl.when(jnp.logical_not(is_late(k)))
+        def _():
+            zsub(k, tau, False)
+
+    def finish(k):
+        f, s = fs(lax.rem(k, 2))
+        h = lax.rem(k, 2)
+        m = k // 2
+        src = acc.at[k, f, s, z]
+        for j in range(4):
+            @pl.when(m == j)
+            def _(j=j):
+                pltpu.make_async_copy(src, outs[5].at[pl.ds(j * 128, 128), pl.ds(pl.multiple_of(h * 128, 128), 128)], osem.at[k]).start()
+
+            @pl.when(m == 4 + j)
+            def _(j=j):
+                pltpu.make_async_copy(src, outs[4].at[:, pl.ds(pl.multiple_of(h * 512 + j * 128, 128), 128)], osem.at[k]).start()
+        for mm, i in ((8, 6), (9, 3), (10, 2), (11, 1), (12, 0)):
+            @pl.when(m == mm)
+            def _(i=i):
+                pltpu.make_async_copy(src, outs[i].at[:, pl.ds(pl.multiple_of(h * 128, 128), 128)], osem.at[k]).start()
+
+    def taskFinA(k):
+        @pl.when(is_late(k))
+        def _():
+            zfin(k, True)
+            finish(k)
+
+    def taskFinE(k):
+        @pl.when(jnp.logical_not(is_late(k)))
+        def _():
+            zfin(k, False)
+            copySE(k).start()
+
+    def taskSE(k):
+        @pl.when(jnp.logical_not(is_late(k)))
+        def _():
+            copySE(k).wait_recv()
+            f, s = fs(lax.rem(k, 2))
+            add_into(acc.at[k, f, s, z], rS.at[k, 0])
+            finish(k)
+
+    L = LAG
+    stages = [
+        (0, taskP),
+        (1, task1),
+        (1 + L, task2),
+        (1 + 2 * L, taskSA),
+        (2 + L, functools.partial(taskZE, 1)),
+        (3 + L, functools.partial(taskZE, 2)),
+        (4 + L, taskFinE),
+        (2 + 2 * L, functools.partial(taskZA, 1)),
+        (3 + 2 * L, functools.partial(taskZA, 2)),
+        (4 + 2 * L, taskFinA),
+        (5 + L, taskSE),
+    ]
+    stages = stages[::-1]
+    last = max(lag for lag, _ in stages)
+
+    def sm_copy(step):
+        if step == 0:
+            return rcopy(smb.at[0], smr.at[0], mss.at[0], msr.at[0], me.at(c=1 - c))
+        if step == 1:
+            return rcopy(smb.at[0], smr.at[1], mss.at[1], msr.at[1], me.at(y=1 - y))
+        return rcopy(smb.at[1, 1 - x], smr.at[2, 0], mss.at[2], msr.at[2], me.at(x=1 - x))
+
+    def sm_z(q, right):
+        if right:
+            return rcopy(smb.at[1, x, q], smr.at[3, 0, q], mss.at[3 + q], msr.at[3 + q], me.at(z=z + 1))
+        return rcopy(smb.at[1, x, q], smr.at[3, 1, q], mss.at[3 + q], msr.at[3 + NZ + q], me.at(z=z - 1))
+
+    vec = lax.broadcasted_iota(jnp.int32, (2, NZ, 16, 128), 2) < 11
+
+    def sm0():
+        pltpu.make_async_copy(sm_in, smb.at[0], msem).wait()
+        sm_copy(0).start()
+
+    def sm1():
+        sm_copy(0).wait_recv()
+        smb[1] = smb[0] + jnp.where(vec, smr[0], 0.0)
+        sm_copy(0).wait_send()
+        smb[0] = smb[1]
+        sm_copy(1).start()
+
+    def sm2():
+        sm_copy(1).wait_recv()
+        smb[1] = smb[0] + jnp.where(vec, smr[1], 0.0)
+        sm_copy(2).start()
+
+    def sm3():
+        sm_copy(2).wait_recv()
+        smb[1, x] = smb[1, x] + smr[2, 0]
+
+    def smz(tau):
+        n = NZ
+
+        @pl.when(z <= tau)
+        def _():
+            q = n - 1 - tau + z
+
+            @pl.when(z > 0)
+            def _():
+                sm_z(q, True).wait_recv()
+                smb[1, x, q] = smb[1, x, q] + smr[3, 0, q]
+
+            sm_z(q, True).start()
+
+        @pl.when(n - 1 - z <= tau)
+        def _():
+            q = tau - (n - 1 - z)
+
+            @pl.when(z < n - 1)
+            def _():
+                sm_z(q, False).wait_recv()
+                smb[1, x, q] = smb[1, x, q] + smr[3, 1, q]
+
+            sm_z(q, False).start()
+
+    def sm_fin():
+        @pl.when(z > 0)
+        def _():
+            sm_z(z, True).wait_recv()
+            smb[1, x, z] = smb[1, x, z] + smr[3, 0, z]
+
+        @pl.when(z < NZ - 1)
+        def _():
+            sm_z(z, False).wait_recv()
+            smb[1, x, z] = smb[1, x, z] + smr[3, 1, z]
+
+        pltpu.make_async_copy(smb.at[1, x, z], sm_out, msem).start()
+
+    small = [sm0, sm1, sm2, sm3, lambda: smz(0), lambda: smz(1), lambda: smz(2), sm_fin]
+
+    pltpu.make_async_copy(sm_in, smb.at[0], msem).start()
+    fetch(0, 0)
+    pl.semaphore_wait(bar, 3 + jnp.where(z > 0, 1, 0) + jnp.where(z < NZ - 1, 1, 0))
+
+    def tick(t, _):
+        @pl.when(jnp.logical_and(lax.rem(t, 2) == 0, t < nk))
+        def _():
+            wait_fetch(lax.rem(t // 2, 2))
+
+        for lag, task in stages:
+            k = t - lag
+
+            @pl.when(jnp.logical_and(k >= 0, k < nk))
+            def _(k=k, task=task):
+                task(k)
+
+            if task is taskP:
+                @pl.when(jnp.logical_and(lax.rem(t, 2) == 0, t + 2 < nk))
+                def _():
+                    fetch(t // 2 + 1, lax.rem(t // 2 + 1, 2))
+
+        for i, step in enumerate(small):
+            @pl.when(t == 8 + i)
+            def _(step=step):
+                step()
+        return 0
+
+    lax.fori_loop(0, nk + last, tick, 0)
+
+    def drain(k, _):
+        @pl.when(k >= nk - 3)
+        def _():
+            copy0(k).wait_send()
+
+        copyF(k).wait_send()
+        pltpu.make_async_copy(acc.at[k, 0, 0, 0], outs[0].at[:, pl.ds(0, 128)], osem.at[k]).wait()
+
+        @pl.when(is_late(k))
+        def _():
+            copySA(k).wait_send()
+            for q in range(NZ):
+                @pl.when(q != z)
+                def _(q=q):
+                    rcopy(unit(k, q, True), zbuf(k, q, True), sZs.at[k, q], sZr.at[k, q], me.at(c=1 - c)).wait_send()
+
+        @pl.when(jnp.logical_not(is_late(k)))
+        def _():
+            copySE(k).wait_send()
+            for q in range(NZ):
+                @pl.when(q != z)
+                def _(q=q):
+                    rcopy(unit(k, q, False), zbuf(k, q, False), sZs.at[k, q], sZr.at[k, q], me.at(c=1 - c)).wait_send()
+        return 0
+
+    lax.fori_loop(0, nk, drain, 0)
+    sm_copy(1).wait_send()
+    sm_copy(2).wait_send()
+    for q in range(NZ):
+        @pl.when(q != z)
+        def _(q=q):
+            sm_z(q, True).wait_send()
+    pltpu.make_async_copy(smb.at[1, x, z], sm_out, msem).wait()
+
+
+def rs_call(lhs, rhs, small):
+    nm = 13
+    nk = 26
+    anyspec = pl.BlockSpec(memory_space=pl.ANY)
+    d = [jax.ShapeDtypeStruct((128, 256), F32)] * 4 + [jax.ShapeDtypeStruct((128, 1024), F32), jax.ShapeDtypeStruct((512, 256), F32), jax.ShapeDtypeStruct((128, 256), F32)]
+    sem = pltpu.SemaphoreType.DMA
+    return pl.pallas_call(
+        functools.partial(rs_kernel, nm),
+        out_shape=d + [jax.ShapeDtypeStruct((16, 128), F32)],
+        in_specs=[anyspec] * 15,
+        out_specs=[anyspec] * 8,
+        scratch_shapes=[
+            pltpu.VMEM((2, 512, 1024), BF), pltpu.VMEM((2, 512, 1024), BF),
+            pltpu.VMEM((nk, 2, 2, NZ, 128, 128), F32),
+            pltpu.VMEM((3, 2, 2, NZ, 128, 128), F32),
+            pltpu.VMEM((SLOTF, 2, NZ, 128, 128), F32),
+            pltpu.VMEM((nk, NZ, 128, 128), F32),
+            pltpu.VMEM((nk, NZ + 1, 2, 128, 128), F32),
+            pltpu.VMEM((2, 2, NZ, 16, 128), F32), pltpu.VMEM((4, 2, NZ, 16, 128), F32),
+            sem((2,)), sem((2,)),
+            sem((nk,)), sem((nk,)), sem((nk,)), sem((nk,)), sem((nk,)), sem((nk,)),
+            sem((nk, NZ)), sem((nk, NZ + 1)), sem((nk,)), sem, sem((3 + NZ,)), sem((3 + 2 * NZ,)),
+        ],
+        compiler_params=pltpu.CompilerParams(collective_id=0, has_side_effects=True, vmem_limit_bytes=67043328),
+        name="grad_sums",
+    )(*lhs, *rhs, small)
+
 
 BLOCK = 64
 
@@ -305,6 +803,45 @@
     start_max_grad = jnp.where(is_first, grad_start_max, 0.0).T
     edge_att_grad = jnp.where(is_first, grad_edge_att, 0.0).T
     edge_ffn_grad = jnp.where(is_first, grad_edge_ffn, 0.0).T
+    if fits_kernel():
+        small = jnp.concatenate(
+            [
+                part.reshape(1, -1)
+                for part in (
+                    grad_ln1_gain,
+                    grad_ln1_bias,
+                    mix_grads[0],
+                    mix_grads[1],
+                    mix_grads[2],
+                    grad_time_decay,
+                    grad_time_first,
+                    grad_ln2_gain,
+                    grad_ln2_bias,
+                    ffn_mix_grads[0],
+                    ffn_mix_grads[1],
+                    start_num_grad,
+                    start_den_grad,
+                    start_max_grad,
+                    edge_att_grad,
+                    edge_ffn_grad,
+                )
+            ],
+            axis=0,
+        )
+        small = small.reshape(16, NZ, 2, 128).transpose(2, 1, 0, 3)
+        flat = lambda rows: rows.reshape(-1, rows.shape[-1])
+        *matrices, small_sums = rs_call(
+            [flat(v) for v in (key_in, value_in, recept_in, gated_low, ffn_key_in, hidden, ffn_recept_in)],
+            [flat(v) for v in (grad_key_rows, grad_value_rows, grad_recept, grad_attended, grad_pre, grad_values, grad_gate)],
+            small,
+        )
+        return (
+            block_out,
+            input_grad,
+            *matrices,
+            *[small_sums[i] for i in range(11)],
+            *[small_sums[i][:, None] for i in range(11, 16)],
+        )
     row_parts = (
         lax.psum_scatter(grad_w_key, "seq", scatter_dimension=0, tiled=True),
         lax.psum_scatter(grad_w_value, "seq", scatter_dimension=0, tiled=True),
@@ -385,6 +922,10 @@
     )
 
 
+def fits_kernel():
+    return (lax.axis_size("seq"), lax.axis_size("batch")) == (2 * NZ, 4)
+
+
 def solution(mesh):
     placed = (
         P("batch", "seq", None),

time: 2070 us -> 843 us (0.41)
  waiting for transfers between devices: 1310 us -> 8.17 us
  Pallas kernels: 0 us -> 243 us
  matrix products: 113 us -> 57.7 us
  blocking collectives: 227 us -> 184 us
  other arithmetic: 263 us -> 232 us
    reduce_scatter x14 -> x0, waiting for transfers between devices: 1050 us -> none  [the longest x1 283 us: local(): lax.psum_scatter(grad_w_ffn_value, 'seq', scatter_dimension=0, tiled=True)]
    unnamed x24 -> x0, waiting for transfers between devices: 260 us -> none
    pallas_call x0 -> x1, Pallas kernels: none -> 243 us  [rs_call(): pl.pallas_call(functools.partial(rs_kernel, nm), out_shape=d + [jax.Shape...]
    dot_general x7 -> x0, matrix products: 42.8 us -> none  [outer_sum(): lax.dot_general(flat_operand, flat_gradient, (((0,), (0,)), ((), ())), pr...]
    unnamed x1 -> x0, blocking collectives: 36.1 us -> none
  transfers between devices with their start and end apart: 23 -> 4, of which waited for: 20 -> 2; matrix products, arithmetic and copies ran while one was open for 14% -> 1% of each run, Pallas kernels for 0% -> 0%
where the time goes in v1:
time: 843 us; the launch traced here: 830 us
  Pallas kernels  243 us (29%)
  other arithmetic  232 us (28%)
  blocking collectives  184 us (22%)
  local copies, waits for them, and re-layouts  89.8 us (11%)
  matrix products  57.7 us (7%)
  starting transfers between devices  9.34 us (1%)
    pallas_call x1, Pallas kernels, rs_call(): pl.pallas_call(functools.partial(rs_kernel, nm), out_shape=d + [jax.Shape...  243 us
    all_gather x6, blocking collectives, prefix(): pieces = jax.tree.map(lambda part: lax.all_gather(part, axis), value)  184 us
    another operation x40, other arithmetic, wkv_block(): running_num = jnp.cumsum(scaled * value_rows, axis=1)  53.9 us
    another operation x40, other arithmetic, wkv_block(): running_den = jnp.cumsum(scaled, axis=1)  48.4 us
    squeeze x64, local copies, waits for them, and re-layouts, wkv_local(): lax.scan(block_step, (in_num, in_den, in_max), (arrange(key_rows), arrang...  47.4 us
    dynamic_update_slice x40, other arithmetic, wkv_local(): lax.scan(block_step, (in_num, in_den, in_max), (arrange(key_rows), arrang...  44.2 us
    dot_general x7, matrix products, matmul(): lax.dot_general(operand, matrix, (((operand.ndim - 1,), (0,)), ((), ())),...  30.3 us
    dot_general x7, matrix products, matmul_back(): lax.dot_general(gradient, matrix, (((gradient.ndim - 1,), (1,)), ((), ())...  27.5 us
  transfers between devices with their start and end apart: 4, of which 2 were waited for; matrix products, arithmetic and copies ran while one was open for 1% of the time, Pallas kernels for 0%

profile of v1, /device:TPU:0, one launch (start us, length us, event | category | flops | bytes accessed | tf_op | source)
XLA Modules:
  0.0 830.4 jit_solution(1268013669042418731)
XLA Ops:
  4.5 5.0 collective-permute-start
  13.4 2.9 fusion.95
  18.6 2.7 fusion.90
  21.4 31.0 %all-gather.2 = f32[8192]{0:T(1024)S(1)} all-gather(f32[1024]{0:T(1024)S(1)} %get-tuple-element.1835), channel_id=4, replica_groups=mesh['seq'=8,'batch'=4] {'seq'}, dimensions={0}, use_global_device_ids=true | all-gather | bytes 36864 | tf_op jit(solution)/shard_map/all_gather | solution.py:520
  52.3 30.6 %all-gather.3 = f32[8192]{0:T(1024)S(1)} all-gather(f32[1024]{0:T(1024)S(1)} %get-tuple-element.1836), channel_id=5, replica_groups=mesh['seq'=8,'batch'=4] {'seq'}, dimensions={0}, use_global_device_ids=true | all-gather | bytes 36864 | tf_op jit(solution)/shard_map/all_gather | solution.py:520
  82.9 30.6 %all-gather = f32[8192]{0:T(1024)S(1)} all-gather(f32[1024]{0:T(1024)S(1)} %get-tuple-element.1833), channel_id=2, replica_groups=mesh['seq'=8,'batch'=4] {'seq'}, dimensions={0}, use_global_device_ids=true | all-gather | bytes 36864 | tf_op jit(solution)/shard_map/all_gather | solution.py:520
  113.5 30.6 %all-gather.1 = f32[8192]{0:T(1024)S(1)} all-gather(f32[1024]{0:T(1024)S(1)} %get-tuple-element.1834), channel_id=3, replica_groups=mesh['seq'=8,'batch'=4] {'seq'}, dimensions={0}, use_global_device_ids=true | all-gather | bytes 36864 | tf_op jit(solution)/shard_map/all_gather | solution.py:520
  146.8 75.5 %while.118 = (s32[]{:T(128)}, f32[1,1024]{1,0:T(1,128)S(1)}, f32[1,1024]{1,0:T(1,128)S(1)}, f32[1,1024]{1,0:T(1,128)S(1)}, f32[8,1,64,1024]{3,2,1,0:T(8,128)}, /...) while((s32[]{:T(128)}, f32[1,1024]{1,0:T(1,128)S(1)}, ...), condition=%wide.region_15.16_spmd.clone.clone, body=%wide.region_7.15_spmd.clone.clone.sunk | while | flops 10293250 | bytes 4643253 | solution.py:613
  222.3 6.1 fusion.88
  232.7 2.5 slice_bitcast_fusion.20
  235.2 3.1 fusion.97
  238.4 11.3 %multiply_convert_fusion.1 = (bf16[512,4096]{1,0:T(8,128)(2,1)S(1)}, f32[512,4096]{1,0:T(8,128)}) fusion(bf16[512,1024]{1,0:T(8,128)(2,1)S(1)} %get-tuple-element.1788.refs_4_, bf16[1024,4096]{1,0:T(8,128)(2,1)} %param.44), kind=kOutput, calls=%fused_computation.225 | convolution fusion | flops 4301258752 | bytes 22020096 | tf_op jit(solution)/shard_map/dot_general | solution.py:542
  249.7 4.5 fusion.122
  254.3 3.0 fusion.99
  257.3 10.3 %multiply_convert_fusion.refs_11_ = bf16[512,4096]{1,0:T(8,128)(2,1)S(1)} fusion(f32[512,4096]{1,0:T(8,128)} %get-tuple-element.1845, bf16[512,1024]{1,0:T(8,128)(2,1)S(1)} %get-tuple-element.1799.refs_12_, bf16[4096,1024]{1,0:T(8,128)(2,1)} %param.45), kind=kOutput, calls=%fused_computation.224 | convolution fusion | flops 4303355904 | bytes 22020096 | tf_op jit(solution)/shard_map/dot_general | solution.py:548
  267.6 8.9 %fusion.124 = f32[512,1024]{1,0:T(8,128)S(1)} fusion(bf16[512,4096]{1,0:T(8,128)(2,1)S(1)} %multiply_convert_fusion.refs_11_, bf16[1024,4096]{1,0:T(8,128)(2,1)} %param.44), kind=kOutput, calls=%fused_computation.396 | convolution fusion | flops 4294967296 | bytes 14680064 | tf_op jit(solution)/shard_map/dot_general | solution.py:548
  281.5 4.1 collective-permute-done.2
  287.1 2.5 multiply_reduce_fusion.14
  294.0 3.1 fusion.120
  300.3 95.0 %while.115 = (s32[]{:T(128)}, f32[1024]{0:T(1024)S(1)}, f32[1024]{0:T(1024)S(1)}, f32[1,1024]{1,0:T(1,128)S(1)}, f32[1,1024]{1,0:T(1,128)S(1)}, /*index=5*/f32[1...) while((s32[]{:T(128)}, f32[1024]{0:T(1024)S(1)}, ...), condition=%wide.region_42.43_spmd.clone, body=%wide.region_20.42_spmd.clone.sunk | while | flops 23723140 | bytes 14379510 | solution.py:613
  305.3 2.2 reduce_window_sum.144
  317.1 2.2 reduce_window_sum.144
  329.0 2.2 reduce_window_sum.144
  340.8 2.2 reduce_window_sum.144
  352.7 2.2 reduce_window_sum.144
  364.5 2.2 reduce_window_sum.144
  376.4 2.2 reduce_window_sum.144
  388.2 2.2 reduce_window_sum.144
  395.3 30.6 %all-gather.6 = f32[8,1,1024]{2,1,0:T(1,128)S(1)} all-gather(f32[1,1,1024]{2,1,0:T(1,128)S(1)} %get-tuple-element.1831), channel_id=6, replica_groups=mesh['seq'=8,'batch'=4] {'seq'}, dimensions={0}, use_global_device_ids=true | all-gather | bytes 36864 | tf_op jit(solution)/shard_map/all_gather | solution.py:520
  426.0 30.6 %all-gather.7 = f32[8,1,1024]{2,1,0:T(1,128)S(1)} all-gather(f32[1,1,1024]{2,1,0:T(1,128)S(1)} %get-tuple-element.1830), channel_id=7, replica_groups=mesh['seq'=8,'batch'=4] {'seq'}, dimensions={0}, use_global_device_ids=true | all-gather | bytes 36864 | tf_op jit(solution)/shard_map/all_gather | solution.py:520
  460.7 87.3 %while.117 = (s32[]{:T(128)}, f32[1024]{0:T(1024)S(1)}, f32[1024]{0:T(1024)S(1)}, f32[1,1024]{1,0:T(1,128)S(1)}, f32[1,1024]{1,0:T(1,128)S(1)}, /*index=5*/f32[1...) while((s32[]{:T(128)}, f32[1024]{0:T(1024)S(1)}, ...), condition=%wide.region_67.68_spmd.clone, body=%wide.region_45.67_spmd.clone.sunk | while | flops 23720068 | bytes 14109164 | solution.py:613
  464.5 2.2 reduce_window_sum.147
  466.7 2.2 reduce_window_sum.148
  475.4 2.2 reduce_window_sum.147
  477.6 2.2 reduce_window_sum.148
  486.3 2.2 reduce_window_sum.147
  488.5 2.2 reduce_window_sum.148
  497.2 2.2 reduce_window_sum.147
  499.3 2.2 reduce_window_sum.148
  508.0 2.2 reduce_window_sum.147
  510.2 2.2 reduce_window_sum.148
  518.9 2.2 reduce_window_sum.147
  521.1 2.2 reduce_window_sum.148
  548.0 4.3 add_convert_fusion.1
  563.0 4.0 collective-permute-done.3
  569.5 4.0 fusion.84
  574.9 243.5 %grad_sums.1 = (f32[128,256]{1,0:T(8,128)}, f32[128,256]{1,0:T(8,128)}, f32[128,256]{1,0:T(8,128)}, f32[128,256]{1,0:T(8,128)}, f32[128,1024]{1,0:T(8,128)}, /*i...) custom-call(bf16[512,1024]{1,0:T(8,128)(2,1)} %copy-done.21, bf16[512,1024]{1,0:T(8,128)(2,1)} %copy-done.20, ...), custom_call_target="tpu_custom_call" | custom-call | tf_op jit(solution)/shard_map/grad_sums/pallas_call | solution.py:484
  820.7 4.3 add_convert_fusion
  (903 shorter events, 267.4 us)
Async XLA Ops:
  2.2 565.5 %copy-start.41 = (f32[512]{0:T(512)}, f32[512]{0:T(512)S(1)}, u32[]{:S(2)}) copy-start(f32[512]{0:T(512)S(1)} %broadcast_multiply_fusion.7) | copy-start | bytes 6148
  3.9 7.5 copy-start.66
  3.9 563.8 %copy-start.42 = (f32[512]{0:T(512)}, f32[512]{0:T(512)S(1)}, u32[]{:S(2)}) copy-start(f32[512]{0:T(512)S(1)} %fusion.102) | copy-start | bytes 6148
  4.4 7.5 copy-start.47
  4.4 7.5 copy-start.48
  4.4 7.5 copy-start.50
  4.4 7.5 copy-start.62
  4.4 7.6 copy-start.45
  4.4 8.1 copy-start.46
  4.5 8.9 %copy-start.71 = (f32[1024,1]{0,1:T(1,128)S(1)}, f32[1024,1]{0,1:T(1,128)}, u32[]{:S(2)}) copy-start(f32[1024,1]{0,1:T(1,128)} %param.61) | copy-start | bytes 12292
  4.5 8.8 %collective-permute-start = (f32[1,1024]{1,0:T(1,128)S(1)}, f32[1,1024]{1,0:T(1,128)S(1)}, u32[]{:S(2)}, u32[]{:S(2)}) collective-permute-start(f32[1,1024]{1,0:T(1,128)S(1)} %slice_bitcast_fusion.1), channel_id=1, source_target_pairs={{0,4},{4,8},{8,12},{12,16},{16,20},{20,24},{24,28},{1,5},{5,9},{9,... | collective-permute-start | bytes 12296 | tf_op jit(solution)/shard_map/ppermute | solution.py:515
  11.9 4.3 copy-start.52
  11.9 4.3 copy-start.54
  12.0 4.3 copy-start.56
  21.3 125.5 %copy-start.10 = (f32[1024]{0:T(1024)S(1)}, f32[1024]{0:T(1024)}, u32[]{:S(2)}) copy-start(f32[1024]{0:T(1024)} %param.53) | copy-start | bytes 12292
  222.3 6.2 copy-start.1
  222.3 6.2 copy-start.26
  230.9 4.3 copy-start.72
  230.9 4.3 copy-start.58
  230.9 4.3 copy-start.59
  230.9 4.2 collective-permute-start.1
  235.2 14.4 %slice-start = ((s8[8388608]{0:T(1024)(128)(4,1)}), s8[4194304]{0:T(1024)(128)(4,1)S(1)}, s32[]{:S(2)}) async-start(s8[8388608]{0:T(1024)(128)(4,1)} %bitcast.716), calls=%async_computation | async-start | bytes 8388608
  238.3 11.3 %copy-start.22 = (bf16[512,1024]{1,0:T(8,128)(2,1)}, bf16[512,1024]{1,0:T(8,128)(2,1)S(1)}, u32[]{:S(2)}) copy-start(bf16[512,1024]{1,0:T(8,128)(2,1)S(1)} %get-tuple-element.1788.refs_4_) | copy-start | bytes 3145732
  238.3 15.9 %copy-start.23 = (bf16[512,1024]{1,0:T(8,128)(2,1)}, bf16[512,1024]{1,0:T(8,128)(2,1)S(1)}, u32[]{:S(2)}) copy-start(bf16[512,1024]{1,0:T(8,128)(2,1)S(1)} %get-tuple-element.1789.refs_6_) | copy-start | bytes 3145732
  238.4 11.3 %slice-start.1 = ((s8[8388608]{0:T(1024)(128)(4,1)}), s8[4194304]{0:T(1024)(128)(4,1)S(1)}, s32[]{:S(2)}) async-start(s8[8388608]{0:T(1024)(128)(4,1)} %bitcast.716), calls=%async_computation.1 | async-start | bytes 8388608
  249.6 4.6 copy-start.15
  249.7 4.6 copy-start.24
  249.7 4.6 copy-start.73
  257.3 10.3 %copy-start.31 = (bf16[512,1024]{1,0:T(8,128)(2,1)}, bf16[512,1024]{1,0:T(8,128)(2,1)S(1)}, u32[]{:S(2)}) copy-start(bf16[512,1024]{1,0:T(8,128)(2,1)S(1)} %get-tuple-element.1799.refs_12_) | copy-start | bytes 3145732
  257.3 19.2 %copy-start.30 = (bf16[512,1024]{1,0:T(8,128)(2,1)}, bf16[512,1024]{1,0:T(8,128)(2,1)S(1)}, u32[]{:S(2)}) copy-start(bf16[512,1024]{1,0:T(8,128)(2,1)S(1)} %get-tuple-element.1794.refs_13_) | copy-start | bytes 3145732
  267.5 8.9 %copy-start.16 = (bf16[512,4096]{1,0:T(8,128)(2,1)}, bf16[512,4096]{1,0:T(8,128)(2,1)S(1)}, u32[]{:S(2)}) copy-start(bf16[512,4096]{1,0:T(8,128)(2,1)S(1)} %multiply_convert_fusion.refs_11_) | copy-start | bytes 12582916
  267.5 8.9 %copy-start.74 = (bf16[1024,1024]{1,0:T(8,128)(2,1)S(1)}, bf16[1024,1024]{1,0:T(8,128)(2,1)}, u32[]{:S(2)}) copy-start(bf16[1024,1024]{1,0:T(8,128)(2,1)} %param.46) | copy-start | bytes 6291460
  280.2 5.5 copy-start.3
  280.2 5.5 collective-permute-start.2
  291.6 5.5 copy-start.11
  300.3 95.0 %copy-start.61 = (f32[1,1024]{1,0:T(1,128)S(1)}, f32[1,1024]{1,0:T(1,128)}, u32[]{:S(2)}) copy-start(f32[1,1024]{1,0:T(1,128)} %copy-done.60) | copy-start | bytes 12292
  548.0 4.4 copy-start.76
  553.7 6.5 copy-start.6
  556.1 4.1 copy-start.8
  561.5 6.2 copy-start.67
  561.5 5.5 collective-permute-start.3
  567.2 6.3 copy-start.2
  820.7 4.3 copy-start.38
  820.7 5.0 copy-start.37
  820.7 5.6 copy-start.36
  820.7 6.3 copy-start.35
  820.7 6.9 copy-start.33
  825.0 4.2 copy-start.34
  (38 other events, 76.1 us)

commit v2 on v0

--- a/solution.py
+++ b/solution.py
@@ -1,9 +1,1238 @@
+import functools
 from functools import partial
 
 import jax
 import jax.numpy as jnp
 from jax import lax
+from jax.experimental import pallas as pl
+from jax.experimental.pallas import tpu as pltpu
 from jax.sharding import PartitionSpec as P
+
+MESH = pl.DeviceIdType.MESH
+F32 = jnp.float32
+BF = jnp.bfloat16
+NS = 8
+T = 512
+D = 1024
+SUB = T // 8
+
+
+def matmul_ref(out, a, b):
+    out[...] = jnp.dot(a[...], b[...], preferred_element_type=F32)
+
+
+def normalize(v, gain, bias):
+    mean = jnp.mean(v, axis=-1, keepdims=True)
+    cen = v - mean
+    var = jnp.mean(cen * cen, axis=-1, keepdims=True)
+    return cen * lax.rsqrt(var + 1e-5) * gain + bias
+
+
+def step_weights(delta):
+    e = jnp.exp(-jnp.abs(delta))
+    up = delta >= 0
+    return jnp.where(up, 1.0, e), jnp.where(up, e, 1.0)
+
+
+def join(early, late, span):
+    em, en, ed = early
+    lm, ln, ld = late
+    a, b = step_weights(em + span - lm)
+    return jnp.maximum(em + span, lm), a * en + b * ln, a * ed + b * ld
+
+
+def fwd_kernel(*refs):
+    (x_hbm, wk_h, wv_h, wr_h, wo_h, g1, b1, mk, mv, mr, td, tf, g2, b2, fmk, fmr, sn, sd, sm, pa, pf) = refs[:21]
+    (o_kin, o_vin, o_rin, o_gat, o_fk, o_fr, o_mid, o_k, o_v, o_r, o_mix, o_m, o_n, o_d, o_edge) = refs[21:36]
+    (xb, lanes, xf, xp, nb, kin, vin, rin, gat, fki, fri, wbuf, kb, vb, rb, mixb, mb, nmb, db,
+     es, er, fs, fr, ss, sr, cur, edges, insem, outsem, esem, fsem, ssem, rsem) = refs[36:]
+    s = lax.axis_index("seq")
+    b = lax.axis_index("batch")
+    bar = pltpu.get_barrier_semaphore()
+    for d in range(1, NS):
+        pl.semaphore_signal(bar, inc=1, device_id=(lax.rem(s + d, NS), b), device_id_type=MESH)
+    loads = [pltpu.make_async_copy(x_hbm, xb, insem.at[0])]
+    for i, w in enumerate((wk_h, wv_h, wr_h, wo_h)):
+        loads.append(pltpu.make_async_copy(w, wbuf.at[i], insem.at[1 + i]))
+    for cp in loads:
+        cp.start()
+    pending = []
+
+    def put(src, dst):
+        cp = pltpu.make_async_copy(src, dst, outsem.at[len(pending)])
+        cp.start()
+        pending.append(cp)
+
+    def edge(src, dst, i, sem):
+        return pltpu.make_async_remote_copy(src_ref=src, dst_ref=dst, send_sem=sem.at[0], recv_sem=sem.at[1], device_id=(i, b), device_id_type=MESH)
+
+    loads[0].wait()
+    es[...] = normalize(xb[T - 16:T, :].astype(F32), g1[...], b1[...])[8:16, :]
+    pl.semaphore_wait(bar, NS - 1)
+    to_next = edge(es, er, jnp.minimum(s + 1, NS - 1), esem)
+
+    @pl.when(s < NS - 1)
+    def _():
+        to_next.start()
+
+    def widen(i, _):
+        rows = pl.ds(pl.multiple_of(i * 64, 64), 64)
+        for g in range(8):
+            lanes[g, rows, :] = xb[rows, g * 128:g * 128 + 128].astype(F32)
+        return 0
+
+    lax.fori_loop(0, T // 64, widen, 0)
+
+    def norm1(j, _):
+        rows = pl.ds(pl.multiple_of(j * 8, 8), 8)
+        v = jnp.concatenate([lanes[g, pl.ds(j, 8, stride=SUB), :] for g in range(8)], axis=1)
+        xp[rows, :] = v
+        nb[pl.ds(pl.multiple_of(j * 8 + 8, 8), 8), :] = normalize(v, g1[...], b1[...])
+        return 0
+
+    lax.fori_loop(0, SUB, norm1, 0, unroll=4)
+    first_row = lax.broadcasted_iota(jnp.int32, (8, D), 0) == 0
+
+    def header(buf, start_row):
+        tail = pltpu.roll(buf[T:T + 8, :], 1, 0)
+        buf[0:8, :] = jnp.where(first_row, start_row, tail)
+
+    def mix(buf, pairs, i):
+        rows = pl.ds(pl.multiple_of(i * 32, 32), 32)
+        before = buf[rows, :]
+        now = buf[pl.ds(pl.multiple_of(i * 32 + 8, 8), 32), :]
+        for dst, w in pairs:
+            dst[rows, :] = (now * w[...] + before * (1.0 - w[...])).astype(BF)
+
+    @pl.when(s > 0)
+    def _():
+        to_next.wait_recv()
+
+    header(nb, jnp.where(s == 0, pa[...], er[7:8, :]))
+    edges[0:8, :] = nb[0:8, :]
+
+    def mix1(i, _):
+        mix(nb, ((kin, mk), (vin, mv), (rin, mr)), i)
+        return 0
+
+    lax.fori_loop(0, T // 32, mix1, 0)
+    put(kin, o_kin)
+    put(vin, o_vin)
+    put(rin, o_rin)
+    loads[1].wait()
+    matmul_ref(kb, kin, wbuf.at[0])
+    loads[2].wait()
+    matmul_ref(vb, vin, wbuf.at[1])
+    put(kb, o_k)
+    put(vb, o_v)
+    decay = -jnp.exp(td[...])
+
+    def own(h):
+        cols = pl.ds(h * 512, 512)
+        w = jnp.broadcast_to(decay[:, h * 512:h * 512 + 512], (8, 512))
+
+        def step(j, state):
+            rows = pl.ds(pl.multiple_of(j * 8, 8), 8)
+            m, n, d = state
+            k, v = kb[rows, cols], vb[rows, cols]
+            low = m + w
+            a, bb = step_weights(low - k)
+            return jnp.maximum(low, k), a * n + bb * v, a * d + bb
+
+        zero = jnp.zeros((8, 512), F32)
+        k, v = kb[0:8, cols], vb[0:8, cols]
+        return lax.fori_loop(1, SUB, step, (k, v, zero + 1.0), unroll=3)
+
+    halves = [own(h) for h in range(2)]
+    total = tuple(jnp.concatenate([halves[0][i], halves[1][i]], axis=1) for i in range(3))
+    row = lax.broadcasted_iota(jnp.int32, (8, D), 0)
+    span = SUB * decay
+
+    def earlier(state, dist):
+        m, n, d = (pltpu.roll(p, dist, 0) for p in state)
+        out = row < dist
+        return jnp.where(out, -1e30, m), jnp.where(out, 0.0, n), jnp.where(out, 0.0, d)
+
+    for dist in (1, 2, 4):
+        total = join(earlier(total, dist), total, dist * span)
+    before_own = earlier(total, 1)
+    m, n, d = (p[7:8, :] for p in total)
+    ss[...] = jnp.where(row == 0, m, jnp.where(row == 1, n, d))
+
+    def state_copy(src, dst):
+        return pltpu.make_async_remote_copy(src_ref=ss, dst_ref=sr.at[src], send_sem=ssem.at[dst], recv_sem=rsem.at[src], device_id=(dst, b), device_id_type=MESH)
+
+    for i in range(1, NS):
+        @pl.when(s < i)
+        def _(i=i):
+            state_copy(s, i).start()
+
+    loads[3].wait()
+    matmul_ref(rb, rin, wbuf.at[2])
+    put(rb, o_r)
+    cur[0:1, :] = sm[...]
+    cur[1:2, :] = sn[...]
+    cur[2:3, :] = sd[...]
+    for i in range(NS - 1):
+        @pl.when(i < s)
+        def _(i=i):
+            state_copy(i, NS - 1).wait_recv()
+            got = (sr[i, 0:1, :], sr[i, 1:2, :], sr[i, 2:3, :])
+            now = join((cur[0:1, :], cur[1:2, :], cur[2:3, :]), got, 8.0 * span)
+            for r in range(3):
+                cur[r:r + 1, :] = now[r]
+
+    lifted = cur[0:1, :] + row.astype(F32) * span
+    wide = tuple(jnp.broadcast_to(cur[r:r + 1, :], (8, D)) for r in (1, 2))
+    begin = join((lifted,) + wide, before_own, 0.0)
+
+    def outputs(h):
+        cols = pl.ds(h * 512, 512)
+        w = jnp.broadcast_to(decay[:, h * 512:h * 512 + 512], (8, 512))
+        bonus = jnp.broadcast_to(tf[:, h * 512:h * 512 + 512], (8, 512))
+
+        def one(j, state):
+            rows = pl.ds(pl.multiple_of(j * 8, 8), 8)
+            m, n, d = state
+            k, v = kb[rows, cols], vb[rows, cols]
+            mb[rows, cols] = m
+            nmb[rows, cols] = n
+            db[rows, cols] = d
+            p, u = step_weights(m - (bonus + k))
+            mixed = (p * n + u * v) / (p * d + u)
+            mixb[rows, cols] = mixed
+            low = m + w
+            a, bb = step_weights(low - k)
+            return (jnp.maximum(low, k), a * n + bb * v, a * d + bb), jax.nn.sigmoid(rb[rows, cols]) * mixed
+
+        def two(i, state):
+            state, ga = one(2 * i, state)
+            state, gb = one(2 * i + 1, state)
+            gat[pl.ds(pl.multiple_of(i * 16, 16), 16), cols] = jnp.concatenate([ga, gb], axis=0).astype(BF)
+            return state
+
+        lax.fori_loop(0, SUB // 2, two, tuple(p[:, h * 512:h * 512 + 512] for p in begin))
+
+    for h in range(2):
+        outputs(h)
+    put(gat, o_gat)
+    put(mixb, o_mix)
+    put(mb, o_m)
+    put(nmb, o_n)
+    put(db, o_d)
+    loads[4].wait()
+    matmul_ref(xf, gat, wbuf.at[3])
+
+    def norm2(i):
+        rows = pl.ds(pl.multiple_of(i * 32, 32), 32)
+        v = xp[rows, :] + xf[rows, :]
+        xp[rows, :] = v
+        nb[pl.ds(pl.multiple_of(i * 32 + 8, 8), 32), :] = normalize(v, g2[...], b2[...])
+
+    norm2(T // 32 - 1)
+    fs[...] = nb[T:T + 8, :]
+    to_next2 = edge(fs, fr, jnp.minimum(s + 1, NS - 1), fsem)
+
+    @pl.when(s < NS - 1)
+    def _():
+        to_next2.start()
+
+    def norm2_loop(i, _):
+        norm2(i)
+        return 0
+
+    lax.fori_loop(0, T // 32 - 1, norm2_loop, 0)
+    put(xp, o_mid)
+
+    def mix2(i, _):
+        mix(nb, ((fki, fmk), (fri, fmr)), i)
+        return 0
+
+    lax.fori_loop(1, T // 32, mix2, 0)
+
+    @pl.when(s > 0)
+    def _():
+        to_next2.wait_recv()
+
+    header(nb, jnp.where(s == 0, pf[...], fr[7:8, :]))
+    edges[8:16, :] = nb[0:8, :]
+    put(edges, o_edge)
+    mix2(0, 0)
+    put(fki, o_fk)
+    put(fri, o_fr)
+
+    @pl.when(s < NS - 1)
+    def _():
+        to_next.wait_send()
+        to_next2.wait_send()
+
+    for i in range(1, NS):
+        @pl.when(s < i)
+        def _(i=i):
+            state_copy(s, i).wait_send()
+    for cp in pending:
+        cp.wait()
+
+
+def fwd_call(x, wk, wv, wr, wo, vectors, states):
+    anyspec = pl.BlockSpec(memory_space=pl.ANY)
+    vm = pl.BlockSpec(memory_space=pltpu.VMEM)
+    low, full = jax.ShapeDtypeStruct((T, D), BF), jax.ShapeDtypeStruct((T, D), F32)
+    sem = pltpu.SemaphoreType.DMA
+    V = pltpu.VMEM
+    return pl.pallas_call(
+        fwd_kernel,
+        out_shape=[low] * 6 + [full] * 8 + [jax.ShapeDtypeStruct((16, D), F32)],
+        in_specs=[anyspec] * 5 + [vm] * 16,
+        out_specs=[anyspec] * 15,
+        scratch_shapes=[
+            V((T, D), BF), V((8, T, 128), F32), V((T, D), F32), V((T, D), F32), V((T + 8, D), F32),
+            V((T, D), BF), V((T, D), BF), V((T, D), BF), V((T, D), BF), V((T, D), BF), V((T, D), BF),
+            V((4, D, D), BF), V((T, D), F32), V((T, D), F32), V((T, D), F32), V((T, D), F32), V((T, D), F32), V((T, D), F32), V((T, D), F32),
+            V((8, D), F32), V((8, D), F32), V((8, D), F32), V((8, D), F32), V((8, D), F32), V((NS, 8, D), F32), V((8, D), F32), V((16, D), F32),
+            sem((5,)), sem((15,)), sem((2,)), sem((2,)), sem((NS,)), sem((NS,)),
+        ],
+        compiler_params=pltpu.CompilerParams(collective_id=1, has_side_effects=True, vmem_limit_bytes=67043328),
+        name="forward",
+    )(x, wk, wv, wr, wo, *vectors, *states)
+
+
+NZ = 4
+NM = 13
+NK = 2 * NM
+WIN = 12
+WINF = 4
+RA = 48
+RE = 128 - RA
+LAGS = [3, 5, 4, 5, 6, 6, 7, 8, 8]
+RETIRE = 9
+
+
+def contract0(a, b):
+    return lax.dot_general(a, b, (((0,), (0,)), ((), ())), preferred_element_type=F32)
+
+
+def contract1(a, b):
+    return lax.dot_general(a, b, (((1,), (1,)), ((), ())), preferred_element_type=F32)
+
+
+def pick(m, table):
+    out = jnp.int32(table[0])
+    for i, v in enumerate(table[1:], 1):
+        out = jnp.where(m == i, v, out)
+    return out
+
+
+LEFT = (0, 9, 1, 9, 2, 9, 3, 9, 10, 4, 5, 8, 7)
+RIGHT = (8, 4, 8, 5, 8, 6, 8, 7, 0, 1, 2, 3, 6)
+
+
+class Place:
+    def __init__(self):
+        self.s, self.b = lax.axis_index("seq"), lax.axis_index("batch")
+        self.z, self.x = self.s // 2, self.s % 2
+        self.y, self.c = self.b // 2, self.b % 2
+
+    def at(self, z=None, x=None, y=None, c=None):
+        z = self.z if z is None else z
+        x = self.x if x is None else x
+        y = self.y if y is None else y
+        c = self.c if c is None else c
+        return (z * 2 + x, y * 2 + c)
+
+
+def rcopy(src, dst, ss, rs, dev):
+    return pltpu.make_async_remote_copy(src_ref=src, dst_ref=dst, send_sem=ss, recv_sem=rs, device_id=dev, device_id_type=MESH)
+
+
+def bwd_kernel(*refs):
+    (cot_h, x_h, wfk_h, wfv_h, wfr_h, wo_h, wr_h, wv_h, wk_h,
+     kin_h, vin_h, rin_h, gat_h, fk_h, fr_h, mid_h, k_h, v_h, r_h, mix_h, m_h, n_h, d_h) = refs[:23]
+    (edges, g1, b1, mk, mv, mr, td, tf, g2, b2, fmk, fmr, sn, sd) = refs[23:37]
+    (o_blk, o_inp) = refs[37:39]
+    outs = refs[39:46]
+    sm_out = refs[46]
+    (ob, wbuf, G, V, K, X, lanes, lanes2, st, sums, RS, es, er, fs, fr, ws, wr,
+     acc, sbuf, rF, rSA, rSE, rZA, rZE, smb, smr,
+     obsem, wsem, stsem, bigsem, outsem, esem, fsem, wssem, wrsem,
+     s0s, s0r, sFs, sFr, sSs, sSr, sZs, sZr, osem, msem, mss, msr) = refs[47:]
+    me = Place()
+    z, x, y, c, s = me.z, me.x, me.y, me.c, me.s
+    left, right = (jnp.maximum(s - 1, 0), me.b), (jnp.minimum(s + 1, NS - 1), me.b)
+
+    bar = pltpu.get_barrier_semaphore()
+
+    def sig(dev):
+        pl.semaphore_signal(bar, inc=1, device_id=dev, device_id_type=MESH)
+
+    sig(me.at(c=1 - c))
+    sig(me.at(y=1 - y))
+    for i in range(1, NS):
+        sig((lax.rem(s + i, NS), me.b))
+
+    def local(src, dst, sem):
+        return pltpu.make_async_copy(src, dst, sem)
+
+    def op_load(src, slot):
+        return local(src, ob.at[slot], obsem.at[slot])
+
+    def slab_columns(src, j, dst, sem):
+        return [local(src.at[:, pl.ds(i * 512 + j * 128, 128)], dst.at[:, pl.ds(i * 128, 128)], sem) for i in range(8)]
+
+    def slab_rows(src, j, dst, sem):
+        return [local(src.at[pl.ds(i * 512 + j * 128, 128), :], dst.at[pl.ds(i * 128, 128), :], sem) for i in range(8)]
+
+    weights = [("p", wfr_h)]
+    for j in range(4):
+        weights += [("c", wfk_h, j), ("r", wfv_h, j)]
+    weights += [("p", wfr_h), ("p", wo_h), ("p", wr_h), ("p", wv_h), ("p", wk_h)]
+
+    def w_start(i):
+        if i >= len(weights):
+            return
+        kind, src, *j = weights[i]
+        dst, sem = wbuf.at[i % 3], wsem.at[i % 3]
+        if kind == "p":
+            local(src, dst, sem).start()
+        else:
+            for cp in (slab_columns if kind == "c" else slab_rows)(src, j[0], dst, sem):
+                cp.start()
+
+    def w_wait(i):
+        local(wo_h, wbuf.at[i % 3], wsem.at[i % 3]).wait()
+
+    def fs_of(k):
+        h = lax.rem(k, 2)
+        return jnp.where(h == 0, x, y), jnp.where(h == 0, y, x)
+
+    def partner(h):
+        a, b = me.at(x=1 - x), me.at(y=1 - y)
+        return (jnp.where(h == 0, a[0], b[0]), jnp.where(h == 0, a[1], b[1]))
+
+    def copy0(k):
+        return rcopy(sbuf.at[lax.rem(k, 2)], acc.at[lax.rem(k, WIN)], s0s.at[k], s0r.at[k], me.at(c=1 - c))
+
+    def copyF(k):
+        f, _ = fs_of(k)
+        return rcopy(acc.at[lax.rem(k, WIN), 1 - f], rF.at[lax.rem(k, WINF)], sFs.at[k], sFr.at[k], partner(lax.rem(k, 2)))
+
+    def copySA(k):
+        f, g = fs_of(k)
+        w = lax.rem(k, WIN)
+        return rcopy(acc.at[w, f, 1 - g, :, pl.ds(0, RA)], rSA.at[w], sSs.at[k, 0], sSr.at[k, 0], partner(1 - lax.rem(k, 2)))
+
+    def copySE(k):
+        f, g = fs_of(k)
+        w = lax.rem(k, WIN)
+        return rcopy(acc.at[w, f, 1 - g, z, pl.ds(RA, RE)], rSE.at[w], sSs.at[k, 1], sSr.at[k, 1], partner(1 - lax.rem(k, 2)))
+
+    def unit(k, q, late):
+        f, g = fs_of(k)
+        w = lax.rem(k, WIN)
+        return acc.at[w, f, g, q, pl.ds(0, RA)] if late else acc.at[w, f, :, q, pl.ds(RA, RE)]
+
+    def zbuf(k, slot, late):
+        return (rZA if late else rZE).at[lax.rem(k, WIN), slot]
+
+    def copyR(k, q, late):
+        i = int(late)
+        return rcopy(unit(k, q, late), zbuf(k, q + 1, late), sZs.at[k, i, q], sZr.at[k, i, q + 1], me.at(z=z + 1))
+
+    def copyL(k, q, late):
+        i = int(late)
+        return rcopy(unit(k, q, late), zbuf(k, q, late), sZs.at[k, i, q], sZr.at[k, i, q], me.at(z=z - 1))
+
+    def add_into(dst, src):
+        dst[...] = dst[...] + src[...]
+
+    def zsub(k, tau, late):
+        @pl.when(z <= tau)
+        def _():
+            q = NZ - 1 - tau + z
+
+            @pl.when(z > 0)
+            def _():
+                copyR(k, q, late).wait_recv()
+                add_into(unit(k, q, late), zbuf(k, q + 1, late))
+
+            copyR(k, q, late).start()
+
+        @pl.when(NZ - 1 - z <= tau)
+        def _():
+            q = tau - (NZ - 1 - z)
+
+            @pl.when(z < NZ - 1)
+            def _():
+                copyL(k, q, late).wait_recv()
+                add_into(unit(k, q, late), zbuf(k, q, late))
+
+            copyL(k, q, late).start()
+
+    def zfin(k, late):
+        @pl.when(z > 0)
+        def _():
+            copyR(k, z, late).wait_recv()
+            add_into(unit(k, z, late), zbuf(k, z + 1, late))
+
+        @pl.when(z < NZ - 1)
+        def _():
+            copyL(k, z, late).wait_recv()
+            add_into(unit(k, z, late), zbuf(k, z, late))
+
+    def gradient(k, core, write):
+        h, m = lax.rem(k, 2), k // 2
+        ls, rs = pick(m, LEFT), pick(m, RIGHT)
+        cols = jnp.concatenate(
+            [ob[rs, :, pl.ds(pl.multiple_of((2 * yy + core) * 256 + h * 128, 128), 128)] for yy in range(2)], axis=1)
+
+        def group(g, _):
+            res = contract0(ob[ls, :, pl.ds(pl.multiple_of(g * 512, 512), 512)], cols)
+            for i in range(4):
+                zz, xx = g * 2 + i // 2, i % 2
+                for yy in range(2):
+                    f = jnp.where(h == 0, xx, yy)
+                    g2_ = jnp.where(h == 0, yy, xx)
+                    write(f, g2_, zz, res[i * 128:(i + 1) * 128, yy * 128:(yy + 1) * 128])
+            return 0
+
+        lax.fori_loop(0, 2, group, 0)
+
+    def taskP(k):
+        @pl.when(k >= 2)
+        def _():
+            copy0(k - 2).wait_send()
+
+        slot = lax.rem(k, 2)
+
+        def write(f, g, zz, v):
+            sbuf[slot, f, g, zz] = v
+
+        gradient(k, 1 - c, write)
+        copy0(k).start()
+
+    def task1(k):
+        copy0(k).wait_recv()
+        w = lax.rem(k, WIN)
+
+        def write(f, g, zz, v):
+            acc[w, f, g, zz] = acc[w, f, g, zz] + v
+
+        gradient(k, c, write)
+        copyF(k).start()
+
+    def task2(k):
+        copyF(k).wait_recv()
+        f, _ = fs_of(k)
+        w = lax.rem(k, WIN)
+
+        def body(i, _):
+            add_into(acc.at[w, f, i // NZ, lax.rem(i, NZ)], rF.at[lax.rem(k, WINF), i // NZ, lax.rem(i, NZ)])
+            return 0
+
+        lax.fori_loop(0, 2 * NZ, body, 0)
+        copySA(k).start()
+        zsub(k, 0, False)
+
+    def taskSA(k):
+        copySA(k).wait_recv()
+        f, g = fs_of(k)
+        w = lax.rem(k, WIN)
+        add_into(acc.at[w, f, g, :, pl.ds(0, RA)], rSA.at[w])
+        zsub(k, 0, True)
+
+    def taskFinE(k):
+        zfin(k, False)
+        copySE(k).start()
+
+    def taskSE(k):
+        copySE(k).wait_recv()
+        f, g = fs_of(k)
+        w = lax.rem(k, WIN)
+        add_into(acc.at[w, f, g, z, pl.ds(RA, RE)], rSE.at[w])
+        src = acc.at[w, f, g, z]
+        h, m = lax.rem(k, 2), k // 2
+        half = pl.ds(pl.multiple_of(h * 128, 128), 128)
+        for j in range(4):
+            @pl.when(m == 2 * j)
+            def _(j=j):
+                local(src, outs[5].at[pl.ds(j * 128, 128), half], osem.at[k]).start()
+
+            @pl.when(m == 2 * j + 1)
+            def _(j=j):
+                local(src, outs[4].at[:, pl.ds(pl.multiple_of(h * 512 + j * 128, 128), 128)], osem.at[k]).start()
+        for mm, i in ((8, 6), (9, 3), (10, 2), (11, 1), (12, 0)):
+            @pl.when(m == mm)
+            def _(i=i):
+                local(src, outs[i].at[:, half], osem.at[k]).start()
+
+    def retire(k):
+        copyF(k).wait_send()
+        copySA(k).wait_send()
+        copySE(k).wait_send()
+        for late in (False, True):
+            for q in range(NZ):
+                @pl.when(q != z)
+                def _(q=q, late=late):
+                    rcopy(unit(k, q, late), zbuf(k, q, late), sZs.at[k, int(late), q], sZr.at[k, int(late), q], me.at(c=1 - c)).wait_send()
+        local(acc.at[lax.rem(k, WIN), 0, 0, 0], outs[0].at[:, pl.ds(0, 128)], osem.at[k]).wait()
+
+    stages = [
+        (RETIRE, retire),
+        (LAGS[7], lambda k: zfin(k, True)),
+        (LAGS[8], taskSE),
+        (LAGS[6], lambda k: zsub(k, 2, True)),
+        (LAGS[5], lambda k: zsub(k, 1, True)),
+        (LAGS[4], taskFinE),
+        (LAGS[3], lambda k: zsub(k, 2, False)),
+        (LAGS[2], lambda k: zsub(k, 1, False)),
+        (LAGS[1], taskSA),
+        (LAGS[0], task2),
+        (1, task1),
+        (0, taskP),
+    ]
+
+    def sm_copy(step):
+        if step == 0:
+            return rcopy(smb.at[0], smr.at[0], mss.at[0], msr.at[0], me.at(c=1 - c))
+        if step == 1:
+            return rcopy(smb.at[2], smr.at[1], mss.at[1], msr.at[1], me.at(y=1 - y))
+        return rcopy(smb.at[1, 1 - x], smr.at[2, 0], mss.at[2], msr.at[2], me.at(x=1 - x))
+
+    def sm_z(q, to_right):
+        if to_right:
+            return rcopy(smb.at[1, x, q], smr.at[3, 0, q], mss.at[3 + q], msr.at[3 + q], me.at(z=z + 1))
+        return rcopy(smb.at[1, x, q], smr.at[3, 1, q], mss.at[3 + q], msr.at[3 + NZ + q], me.at(z=z - 1))
+
+    vec = lax.broadcasted_iota(jnp.int32, (2, NZ, 16, 128), 2) < 11
+
+    def sm1():
+        sm_copy(0).wait_recv()
+        smb[2] = smb[0] + jnp.where(vec, smr[0], 0.0)
+        sm_copy(1).start()
+
+    def sm2():
+        sm_copy(1).wait_recv()
+        smb[1] = smb[2] + jnp.where(vec, smr[1], 0.0)
+        sm_copy(2).start()
+
+    def sm3():
+        sm_copy(2).wait_recv()
+        smb[1, x] = smb[1, x] + smr[2, 0]
+
+    def smz(tau):
+        @pl.when(z <= tau)
+        def _():
+            q = NZ - 1 - tau + z
+
+            @pl.when(z > 0)
+            def _():
+                sm_z(q, True).wait_recv()
+                smb[1, x, q] = smb[1, x, q] + smr[3, 0, q]
+
+            sm_z(q, True).start()
+
+        @pl.when(NZ - 1 - z <= tau)
+        def _():
+            q = tau - (NZ - 1 - z)
+
+            @pl.when(z < NZ - 1)
+            def _():
+                sm_z(q, False).wait_recv()
+                smb[1, x, q] = smb[1, x, q] + smr[3, 1, q]
+
+            sm_z(q, False).start()
+
+    def sm_fin():
+        @pl.when(z > 0)
+        def _():
+            sm_z(z, True).wait_recv()
+            smb[1, x, z] = smb[1, x, z] + smr[3, 0, z]
+
+        @pl.when(z < NZ - 1)
+        def _():
+            sm_z(z, False).wait_recv()
+            smb[1, x, z] = smb[1, x, z] + smr[3, 1, z]
+
+        local(smb.at[1, x, z], sm_out, msem).start()
+
+    def tiles(n, rows, body):
+        def step(i, _):
+            body(i, pl.ds(pl.multiple_of(i * rows, rows), rows))
+            return 0
+
+        lax.fori_loop(0, n, step, 0)
+
+    def widen(slot):
+        def body(i, rows):
+            for g in range(8):
+                lanes[g, rows, :] = ob[slot, rows, g * 128:g * 128 + 128].astype(F32)
+
+        tiles(T // 64, 64, body)
+
+    def spread(i, count):
+        return jnp.concatenate(
+            [jnp.concatenate([lanes[g, pl.ds(i * count + a, 8, stride=SUB), :] for g in range(8)], axis=1) for a in range(count)], axis=0)
+
+    def unspread(i, count, value):
+        for a in range(count):
+            for g in range(8):
+                lanes2[g, pl.ds(i * count + a, 8, stride=SUB), :] = value[a * 8:a * 8 + 8, g * 128:g * 128 + 128]
+
+    def narrow(slot, dst, sem):
+        def body(i, rows):
+            for g in range(8):
+                ob[slot, rows, g * 128:g * 128 + 128] = lanes2[g, rows, :].astype(BF)
+
+        tiles(T // 64, 64, body)
+        local(ob.at[slot], dst, sem).start()
+
+    def halves(body):
+        tiles(2, 512, body)
+
+    def gate_step():
+        w_wait(0)
+
+        def mm(i, cols):
+            G[:, cols] = jnp.dot(ob[10], wbuf[0, :, cols], preferred_element_type=F32)
+
+        halves(mm)
+        w_start(3)
+
+        def body(i, rows):
+            gate = jax.nn.sigmoid(G[rows, :])
+            G[rows, :] = gate
+            ob[8, rows, :] = (spread(i, 4) * gate).astype(BF)
+
+        tiles(T // 32, 32, body)
+
+    def hid(j):
+        w_wait(1 + 2 * j)
+        slot = (1 + 2 * j) % 3
+
+        def mm(i, cols):
+            up = jnp.maximum(jnp.dot(ob[9], wbuf[slot, :, cols], preferred_element_type=F32), 0.0)
+            X[pl.ds(0, T), cols] = up
+            ob[j, :, cols] = (up * up).astype(BF)
+
+        halves(mm)
+
+    def gpre(j):
+        w_wait(2 + 2 * j)
+        slot = (2 + 2 * j) % 3
+
+        def mm(i, cols):
+            back = contract1(ob[8], wbuf[slot, cols, :])
+            ob[4 + j, :, cols] = (back * 2.0 * X[pl.ds(0, T), cols]).astype(BF)
+
+        halves(mm)
+
+    def gk_step(j):
+        slot = (1 + 2 * j) % 3
+
+        def mm(i, cols):
+            part = contract1(ob[4 + j], wbuf[slot, cols, :])
+            K[pl.ds(0, T), cols] = part if j == 0 else K[pl.ds(0, T), cols] + part
+
+        halves(mm)
+        w_start(1 + 2 * j + 3)
+
+    def ffv(j):
+        slot = (2 + 2 * j) % 3
+
+        def mm(i, cols):
+            part = jnp.dot(ob[j], wbuf[slot, :, cols], preferred_element_type=F32)
+            V[pl.ds(0, T), cols] = part if j == 0 else V[pl.ds(0, T), cols] + part
+
+        halves(mm)
+        w_start(2 + 2 * j + 3)
+
+    def big_load(src, dst, i):
+        return local(src, dst.at[pl.ds(0, T)], bigsem.at[i])
+
+    def block_step():
+        big_load(mid_h, X, 0).wait()
+
+        def body(i, rows):
+            gate, values = G[rows, :], V[rows, :]
+            unspread(i, 4, X[rows, :] + gate * values)
+            ob[0, rows, :] = (spread(i, 4) * values * gate * (1.0 - gate)).astype(BF)
+
+        tiles(T // 32, 32, body)
+        narrow(5, o_blk, outsem.at[0])
+
+    row8 = lax.broadcasted_iota(jnp.int32, (8, D), 0)
+
+    def tail(buf):
+        buf[T:T + 8, :] = jnp.where(row8 == 7, 0.0, pltpu.roll(buf[0:8, :], 7, 0))
+
+    def edge(src, dst, sem, dev):
+        return rcopy(src, dst, sem.at[0], sem.at[1], dev)
+
+    def recept_back():
+        w_wait(9)
+
+        def mm(i, cols):
+            V[pl.ds(0, T), cols] = contract1(ob[0], wbuf[0, cols, :])
+
+        halves(mm)
+        w_start(12)
+        tail(K)
+        tail(V)
+        es[...] = K[0:8, :] * (1.0 - fmk[...]) + V[0:8, :] * (1.0 - fmr[...])
+
+        @pl.when(s > 0)
+        def _():
+            edge(es, er, esem, left).start()
+
+    def fold(v):
+        return v[0:8] + v[8:16] + v[16:24] + v[24:32]
+
+    row32 = lax.broadcasted_iota(jnp.int32, (32, D), 0)
+
+    def centre(v):
+        mean = jnp.mean(v, axis=-1, keepdims=True)
+        cen = v - mean
+        inv = lax.rsqrt(jnp.mean(cen * cen, axis=-1, keepdims=True) + 1e-5)
+        return cen * inv, inv
+
+    def ln_back(grad, n, inv, gain):
+        h = grad * gain[...]
+        return inv * (h - jnp.mean(h, axis=-1, keepdims=True) - n * jnp.mean(h * n, axis=-1, keepdims=True))
+
+    def ln_tile(i, rows, n, gain, bias, parts, arrived, sum_rows, ln_sums):
+        later = pl.ds(pl.multiple_of(i * 32 + 8, 8), 32)
+        normed = n * gain[...] + bias[...]
+        grad = 0.0
+        if arrived is not None:
+            grad = jnp.where(jnp.logical_and(row32 == 31, i == T // 32 - 1), arrived, 0.0)
+        for (buf, w), r in zip(parts, sum_rows):
+            now, nxt = buf[rows, :], buf[later, :]
+            grad = grad + now * w[...] + nxt * (1.0 - w[...])
+            sums[r] = sums[r] + fold(normed * (now - nxt))
+        sums[ln_sums[0]] = sums[ln_sums[0]] + fold(grad * n)
+        sums[ln_sums[1]] = sums[ln_sums[1]] + fold(grad)
+        return grad
+
+    def wait_from_right(cp):
+        @pl.when(s < NS - 1)
+        def _():
+            cp.wait_recv()
+
+    def middle_back(lo, hi):
+        arrived = jnp.where(s == NS - 1, 0.0, er[0:1, :]) if hi == T // 32 else None
+
+        def body(i, _):
+            rows = pl.ds(pl.multiple_of(i * 32, 32), 32)
+            n, inv = centre(X[rows, :])
+            grad = ln_tile(i, rows, n, g2, b2, ((K, fmk), (V, fmr)), arrived, (9, 10), (7, 8))
+            gm = spread(i, 4) + ln_back(grad, n, inv, g2)
+            G[rows, :] = gm
+            ob[1, rows, :] = gm.astype(BF)
+            return 0
+
+        lax.fori_loop(lo, hi, body, 0)
+
+    def middle_end():
+        for r, buf in ((9, K), (10, V)):
+            sums[r, 0:1, :] = sums[r, 0:1, :] - buf[0:1, :] * edges[8:9, :]
+        sums[15, 0:1, :] = es[0:1, :]
+
+    def gated_back():
+        w_wait(10)
+
+        def mm(i, cols):
+            V[pl.ds(0, T), cols] = contract1(ob[1], wbuf[1, cols, :])
+
+        halves(mm)
+        w_start(13)
+        big_load(r_h, X, 0).wait()
+        big_load(mix_h, K, 1).wait()
+
+        def body(i, rows):
+            sg = jax.nn.sigmoid(X[rows, :])
+            gg = V[rows, :]
+            ob[2, rows, :] = (gg * K[rows, :] * sg * (1.0 - sg)).astype(BF)
+            V[rows, :] = gg * sg
+
+        tiles(T // 32, 32, body)
+
+    streams = (k_h, m_h, d_h, n_h, v_h)
+
+    def st_copies(blk, slot, count):
+        rows = pl.ds(pl.multiple_of(blk * 64, 64), 64)
+        return [local(src.at[rows, :], st.at[slot, i], stsem.at[slot, i]) for i, src in enumerate(streams[:count])]
+
+    def st_start(blk, count):
+        for cp in st_copies(blk, lax.rem(blk, 2), count):
+            cp.start()
+
+    def st_next(blk, count):
+        for cp in st_copies(blk, lax.rem(blk, 2), count):
+            cp.wait()
+
+        @pl.when(blk > 0)
+        def _():
+            st_start(blk - 1, count)
+
+    decay = -jnp.exp(td[...])
+
+    def wide(v, cols):
+        return jnp.broadcast_to(v[:, cols], (8, 512))
+
+    def first_pass(lo):
+        def block(i, _):
+            blk = 7 - lo - i
+            slot = lax.rem(blk, 2)
+            st_next(blk, 3)
+            for h in range(2):
+                cols = slice(h * 512, h * 512 + 512)
+                w, bonus = wide(decay, cols), wide(tf[...], cols)
+
+                def step(jj, carry):
+                    R, S = carry
+                    j = 7 - jj
+                    at = pl.ds(pl.multiple_of(j * 8, 8), 8)
+                    rows = pl.ds(pl.multiple_of(blk * 64 + j * 8, 8), 8)
+                    k, m, d = st[slot, 0, at, cols], st[slot, 1, at, cols], st[slot, 2, at, cols]
+                    p, u = step_weights(m - (bonus + k))
+                    q = V[rows, cols] / (p * d + u)
+                    qp = p * q
+                    V[rows, cols] = qp
+                    X[rows, cols] = u * q
+                    a, _ = step_weights(m + w - k)
+                    return qp + a * R, qp * K[rows, cols] + a * S
+
+                R, S = lax.fori_loop(0, 8, step, (RS[0, :, cols], RS[1, :, cols]), unroll=2)
+                RS[0, :, cols] = R
+                RS[1, :, cols] = S
+
+                @pl.when(blk == 7)
+                def _():
+                    RS[2, :, cols] = jnp.maximum(st[slot, 1, 56:64, cols] + w, st[slot, 0, 56:64, cols])
+
+                @pl.when(blk == 0)
+                def _():
+                    RS[3, :, cols] = st[slot, 1, 0:8, cols]
+            return 0
+
+        lax.fori_loop(0, 4, block, 0)
+
+    def suffix(value, dist, fill):
+        return jnp.where(row8 >= 8 - dist, fill, pltpu.roll(value, 8 - dist, 0))
+
+    span = SUB * decay
+
+    def state_copy(src, dst):
+        return rcopy(ws, wr.at[src], wssem.at[dst], wrsem.at[src], (dst, me.b))
+
+    def first_end():
+        A = jnp.exp(jnp.minimum(RS[3] + span - RS[2], 0.0))
+        R, S = RS[0], RS[1]
+        for dist in (1, 2, 4):
+            R = R + A * suffix(R, dist, 0.0)
+            S = S + A * suffix(S, dist, 0.0)
+            A = A * suffix(A, dist, 1.0)
+        RS[0], RS[1], RS[4] = R, S, A
+        ws[...] = jnp.where(row8 == 0, R[0:1], jnp.where(row8 == 1, S[0:1], RS[3, 0:1, :]))
+        for i in range(NS - 1):
+            @pl.when(i < s)
+            def _(i=i):
+                state_copy(s, i).start()
+
+    def second_start():
+        RS[5] = jnp.zeros((8, D), F32)
+        RS[6] = jnp.zeros((8, D), F32)
+        for i in range(1, NS):
+            @pl.when(i > s)
+            def _(i=i):
+                state_copy(i, 0).wait_recv()
+                far = jnp.exp(jnp.minimum(RS[2, 7:8, :] + (i - s - 1).astype(F32) * (8.0 * span) - wr[i, 2:3, :], 0.0))
+                RS[5, 0:1, :] = RS[5, 0:1, :] + far * wr[i, 0:1, :]
+                RS[6, 0:1, :] = RS[6, 0:1, :] + far * wr[i, 1:2, :]
+        Rin, Sin = RS[5, 0:1, :], RS[6, 0:1, :]
+        A = RS[4]
+        R = RS[0] + A * Rin
+        S = RS[1] + A * Sin
+        RS[0] = jnp.where(row8 == 7, Rin, pltpu.roll(R, 7, 0))
+        RS[1] = jnp.where(row8 == 7, Sin, pltpu.roll(S, 7, 0))
+
+    def second_pass(lo, n):
+        def block(i, _):
+            blk = 7 - lo - i
+            slot = lax.rem(blk, 2)
+            st_next(blk, 5)
+            for h in range(2):
+                cols = slice(h * 512, h * 512 + 512)
+                w = wide(decay, cols)
+
+                def one(j, carry):
+                    R, S, first, slow = carry
+                    at = pl.ds(pl.multiple_of(j * 8, 8), 8)
+                    rows = pl.ds(pl.multiple_of(blk * 64 + j * 8, 8), 8)
+                    k, m, d, n_, v = (st[slot, q, at, cols] for q in range(5))
+                    mixed, qp, uq = K[rows, cols], V[rows, cols], X[rows, cols]
+                    a, b = step_weights(m + w - k)
+                    own = uq * (v - mixed)
+                    gv = uq + b * R
+                    gk = own + b * (v * R - S)
+                    first = first + own
+                    slow = slow + a * (n_ * R - d * S)
+                    return (qp + a * R, qp * mixed + a * S, first, slow), gk, gv
+
+                def step(jj, carry):
+                    j = 3 - jj
+                    carry, gk1, gv1 = one(2 * j + 1, carry)
+                    carry, gk0, gv0 = one(2 * j, carry)
+                    pair = pl.ds(pl.multiple_of(blk * 64 + j * 16, 16), 16)
+                    ob[6, pair, cols] = jnp.concatenate([gk0, gk1], axis=0).astype(BF)
+                    ob[3, pair, cols] = jnp.concatenate([gv0, gv1], axis=0).astype(BF)
+                    return carry
+
+                R, S, first, slow = lax.fori_loop(0, 4, step, (RS[0, :, cols], RS[1, :, cols], sums[6, :, cols], sums[5, :, cols]))
+                RS[0, :, cols] = R
+                RS[1, :, cols] = S
+                sums[6, :, cols] = first
+                sums[5, :, cols] = slow
+            return 0
+
+        lax.fori_loop(0, n, block, 0)
+
+    def second_end():
+        gn, gd = RS[0, 0:1, :], -RS[1, 0:1, :]
+        sums[11, 0:1, :] = gn
+        sums[12, 0:1, :] = gd
+        sums[13, 0:1, :] = sn[...] * gn + sd[...] * gd
+        sums[5] = sums[5] * decay
+
+    def input_mm(i, slot, buf):
+        w_wait(i)
+
+        def mm(_, cols):
+            buf[pl.ds(0, T), cols] = contract1(ob[slot], wbuf[i % 3, cols, :])
+
+        halves(mm)
+        tail(buf)
+
+    def input_edge():
+        fs[...] = K[0:8, :] * (1.0 - mk[...]) + V[0:8, :] * (1.0 - mv[...]) + X[0:8, :] * (1.0 - mr[...])
+
+        @pl.when(s > 0)
+        def _():
+            edge(fs, fr, fsem, left).start()
+
+    def input_back(lo, hi):
+        arrived = jnp.where(s == NS - 1, 0.0, fr[0:1, :]) if hi == T // 32 else None
+
+        def body(i, _):
+            rows = pl.ds(pl.multiple_of(i * 32, 32), 32)
+            n, inv = centre(spread(i, 4))
+            grad = ln_tile(i, rows, n, g1, b1, ((K, mk), (V, mv), (X, mr)), arrived, (2, 3, 4), (0, 1))
+            unspread(i, 4, G[rows, :] + ln_back(grad, n, inv, g1))
+            return 0
+
+        lax.fori_loop(lo, hi, body, 0)
+
+    def input_end():
+        for r, buf in ((2, K), (3, V), (4, X)):
+            sums[r, 0:1, :] = sums[r, 0:1, :] - buf[0:1, :] * edges[0:1, :]
+        sums[14, 0:1, :] = fs[0:1, :]
+        narrow(0, o_inp, outsem.at[1])
+        alone = jnp.where(s == 0, 1.0, 0.0)
+        rows = [jnp.sum(sums[r], axis=0, keepdims=True) for r in range(11)] + [jnp.where(s == 0, sums[r, 0:1, :], 0.0) for r in range(11, 16)]
+        table = jnp.concatenate(rows, axis=0)
+        for g in range(8):
+            smb[0, g % 2, g // 2] = table[:, g * 128:g * 128 + 128]
+        sm_copy(0).start()
+
+    def start_all(*copies):
+        for cp in copies:
+            cp.start()
+
+    compute = {
+        0: [lambda: gpre(0)],
+        1: [lambda: gk_step(0), lambda: hid(1)],
+        2: [lambda: ffv(0), lambda: gpre(1)],
+        3: [lambda: gk_step(1), lambda: hid(2)],
+        4: [lambda: ffv(1), lambda: gpre(2)],
+        5: [lambda: gk_step(2), lambda: hid(3), lambda: start_all(op_load(gat_h, 4))],
+        6: [lambda: ffv(2), lambda: gpre(3), lambda: big_load(mid_h, X, 0).start()],
+        7: [lambda: gk_step(3), lambda: ffv(3)],
+        8: [block_step],
+        9: [recept_back],
+        10: [lambda: middle_back(0, 8)],
+        11: [lambda: wait_from_right(edge(es, er, esem, left)), lambda: middle_back(8, 16), middle_end,
+             lambda: start_all(big_load(r_h, X, 0), big_load(mix_h, K, 1)), lambda: st_start(7, 3),
+             lambda: local(ob.at[5], o_blk, outsem.at[0]).wait(), lambda: start_all(op_load(rin_h, 5))],
+        12: [gated_back],
+        13: [lambda: first_pass(0)],
+        14: [lambda: first_pass(4), first_end, lambda: st_start(7, 5)],
+        15: [second_start, lambda: second_pass(0, 2), lambda: start_all(op_load(vin_h, 8))],
+        16: [lambda: second_pass(2, 3)],
+        17: [lambda: second_pass(5, 3), second_end, lambda: start_all(op_load(kin_h, 7), op_load(x_h, 9))],
+        18: [lambda: input_mm(11, 2, X), lambda: input_mm(12, 3, V)],
+        19: [lambda: input_mm(13, 6, K), input_edge, lambda: op_load(x_h, 9).wait(), lambda: widen(9)],
+        20: [lambda: input_back(0, 8)],
+        21: [lambda: wait_from_right(edge(fs, fr, fsem, left)), lambda: input_back(8, 16), input_end],
+        23: [sm1],
+        24: [sm2],
+        25: [sm3, lambda: smz(0)],
+        27: [lambda: smz(1)],
+        29: [lambda: smz(2)],
+        31: [sm_fin],
+    }
+    landed = {18: (gat_h, 4), 20: (rin_h, 5), 22: (vin_h, 8), 24: (kin_h, 7)}
+
+    start_all(op_load(fr_h, 10), op_load(cot_h, 1), op_load(fk_h, 9))
+    for i in range(3):
+        w_start(i)
+    sums[...] = jnp.zeros_like(sums)
+    RS[...] = jnp.zeros_like(RS)
+    op_load(cot_h, 1).wait()
+    widen(1)
+    op_load(fr_h, 10).wait()
+    gate_step()
+    op_load(fk_h, 9).wait()
+    hid(0)
+    pl.semaphore_wait(bar, NS + 1)
+
+    def tick(t, _):
+        for at, (src, slot) in landed.items():
+            @pl.when(t == at)
+            def _(src=src, slot=slot):
+                op_load(src, slot).wait()
+
+        for lag, task in stages:
+            k = t - lag
+
+            @pl.when(jnp.logical_and(k >= 0, k < NK))
+            def _(k=k, task=task):
+                task(k)
+
+        for at, steps in compute.items():
+            @pl.when(t == at)
+            def _(steps=steps):
+                for step in steps:
+                    step()
+        return 0
+
+    lax.fori_loop(0, NK + RETIRE, tick, 0)
+
+    copy0(NK - 2).wait_send()
+    copy0(NK - 1).wait_send()
+    for i in range(3):
+        sm_copy(i).wait_send()
+    for q in range(NZ):
+        @pl.when(q != z)
+        def _(q=q):
+            sm_z(q, True).wait_send()
+
+    @pl.when(s > 0)
+    def _():
+        edge(es, er, esem, left).wait_send()
+        edge(fs, fr, fsem, left).wait_send()
+
+    for i in range(NS - 1):
+        @pl.when(i < s)
+        def _(i=i):
+            state_copy(s, i).wait_send()
+    local(smb.at[1, x, z], sm_out, msem).wait()
+    local(ob.at[0], o_inp, outsem.at[1]).wait()
+
+
+def bwd_call(cot, x, mats, acts, edges, vectors, sn, sd):
+    anyspec = pl.BlockSpec(memory_space=pl.ANY)
+    vm = pl.BlockSpec(memory_space=pltpu.VMEM)
+    S = jax.ShapeDtypeStruct
+    sem = pltpu.SemaphoreType.DMA
+    M = pltpu.VMEM
+    return pl.pallas_call(
+        bwd_kernel,
+        out_shape=[S((T, D), BF)] * 2 + [S((128, 256), F32)] * 4 + [S((128, 1024), F32), S((512, 256), F32), S((128, 256), F32), S((16, 128), F32)],
+        in_specs=[anyspec] * 23 + [vm] * 14,
+        out_specs=[anyspec] * 10,
+        scratch_shapes=[
+            M((11, T, D), BF), M((3, D, D), BF), M((T, D), F32), M((T + 8, D), F32), M((T + 8, D), F32), M((T + 8, D), F32),
+            M((8, T, 128), F32), M((8, T, 128), F32), M((2, 5, 64, D), F32), M((16, 8, D), F32), M((7, 8, D), F32),
+            M((8, D), F32), M((8, D), F32), M((8, D), F32), M((8, D), F32), M((8, D), F32), M((NS, 8, D), F32),
+            M((WIN, 2, 2, NZ, 128, 128), F32), M((2, 2, 2, NZ, 128, 128), F32), M((WINF, 2, NZ, 128, 128), F32),
+            M((WIN, NZ, RA, 128), F32), M((WIN, RE, 128), F32), M((WIN, NZ + 1, RA, 128), F32), M((WIN, NZ + 1, 2, RE, 128), F32),
+            M((3, 2, NZ, 16, 128), F32), M((4, 2, NZ, 16, 128), F32),
+            sem((11,)), sem((3,)), sem((2, 5)), sem((2,)), sem((2,)), sem((2,)), sem((2,)), sem((NS,)), sem((NS,)),
+            sem((NK,)), sem((NK,)), sem((NK,)), sem((NK,)), sem((NK, 2)), sem((NK, 2)),
+            sem((NK, 2, NZ)), sem((NK, 2, NZ + 1)), sem((NK,)), sem, sem((3 + NZ,)), sem((3 + 2 * NZ,)),
+        ],
+        compiler_params=pltpu.CompilerParams(collective_id=0, has_side_effects=True, vmem_limit_bytes=67043328),
+        name="backward",
+    )(cot, x, *mats, *acts, edges, *vectors, sn, sd)
+
+def fits(mesh):
+    return (mesh.shape["seq"], mesh.shape["batch"]) == (2 * NZ, 4)
+
+
+def local(
+    inputs,
+    w_key,
+    w_value,
+    w_recept,
+    w_output,
+    w_ffn_key,
+    w_ffn_value,
+    w_ffn_recept,
+    ln1_gain,
+    ln1_bias,
+    mix_key,
+    mix_value,
+    mix_recept,
+    time_decay,
+    time_first,
+    ln2_gain,
+    ln2_bias,
+    ffn_mix_key,
+    ffn_mix_recept,
+    state_num,
+    state_den,
+    state_max,
+    prev_att,
+    prev_ffn,
+    cotangent,
+):
+    rows = inputs.reshape(T, D)
+    vectors = [
+        v.reshape(1, D)
+        for v in (
+            ln1_gain,
+            ln1_bias,
+            mix_key,
+            mix_value,
+            mix_recept,
+            time_decay,
+            time_first,
+            ln2_gain,
+            ln2_bias,
+            ffn_mix_key,
+            ffn_mix_recept,
+        )
+    ]
+    states = [v.reshape(1, D) for v in (state_num, state_den, state_max, prev_att, prev_ffn)]
+    *acts, edges = fwd_call(rows, w_key, w_value, w_recept, w_output, vectors, states)
+    block_out, input_grad, *matrices, small = bwd_call(
+        cotangent.reshape(T, D),
+        rows,
+        [w_ffn_key, w_ffn_value, w_ffn_recept, w_output, w_recept, w_value, w_key],
+        acts,
+        edges,
+        vectors,
+        states[0],
+        states[1],
+    )
+    return (
+        block_out.reshape(inputs.shape),
+        input_grad.reshape(inputs.shape),
+        *matrices,
+        *[small[i] for i in range(11)],
+        *[small[i][:, None] for i in range(11, 16)],
+    )
+
 
 BLOCK = 64
 
@@ -154,7 +1383,7 @@
     )
 
 
-def local(
+def local_plain(
     inputs,
     w_key,
     w_value,
@@ -414,7 +1643,7 @@
         P("batch", "seq", None),
     )
     return jax.shard_map(
-        local,
+        local if fits(mesh) else local_plain,
         mesh=mesh,
         in_specs=placed,
         out_specs=(

time: 2070 us -> 280 us (0.14)
  waiting for transfers between devices: 1310 us -> 0 us
  Pallas kernels: 0 us -> 269 us
  other arithmetic: 263 us -> 0 us
  blocking collectives: 227 us -> 0 us
  matrix products: 113 us -> 0 us
  local copies, waits for them, and re-layouts: 110 us -> 9.74 us
    reduce_scatter x14 -> x0, waiting for transfers between devices: 1050 us -> none  [the longest x1 283 us: local(): lax.psum_scatter(grad_w_ffn_value, 'seq', scatter_dimension=0, tiled=True)]
    pallas_call x0 -> x2, Pallas kernels: none -> 269 us  [the longest x1 242 us: bwd_call(): pl.pallas_call(bwd_kernel, out_shape=[S((T, D), BF)] * 2 + [S((128, 256),...]
    unnamed x24 -> x0, waiting for transfers between devices: 260 us -> none
    all_gather x6 -> x0, blocking collectives: 185 us -> none  [prefix(): pieces = jax.tree.map(lambda part: lax.all_gather(part, axis), value)]
    dot_general x21 -> x0, matrix products: 113 us -> none  [the longest x7 42.8 us: outer_sum(): lax.dot_general(flat_operand, flat_gradient, (((0,), (0,)), ((), ())), pr...]
    another operation x94 -> x0, other arithmetic: 109 us -> none  [the longest x40 53.9 us: wkv_block(): running_num = jnp.cumsum(scaled * value_rows, axis=1)]
    reduce_sum x82 -> x0, other arithmetic: 47.6 us -> none  [the longest x8 9.61 us: wkv_block(): new_den = jnp.sum(final_weights, axis=1) + kept_weight * denominator]
    squeeze x66 -> x0, local copies, waits for them, and re-layouts: 47.3 us -> none  [the longest x64 47.3 us: wkv_local(): lax.scan(block_step, (in_num, in_den, in_max), (arrange(key_rows), arrang...]
  transfers between devices with their start and end apart: 23 -> 0, of which waited for: 20 -> 0; matrix products, arithmetic and copies ran while one was open for 14% -> 0% of each run, Pallas kernels for 0% -> 0%
where the time goes in v2:
time: 280 us
  Pallas kernels  269 us (96%)
  local copies, waits for them, and re-layouts  9.74 us (3%)
    pallas_call x1, Pallas kernels, bwd_call(): pl.pallas_call(bwd_kernel, out_shape=[S((T, D), BF)] * 2 + [S((128, 256),...  242 us
    pallas_call x1, Pallas kernels, fwd_call(): pl.pallas_call(fwd_kernel, out_shape=[low] * 6 + [full] * 8 + [jax.ShapeD...  27.3 us
    unnamed x25, local copies, waits for them, and re-layouts  8.18 us

profile of v2, /device:TPU:0, one launch (start us, length us, event | category | flops | bytes accessed | tf_op | source)
XLA Modules:
  0.0 279.8 jit_solution(15025270160314278845)
XLA Ops:
  0.7 27.3 %forward.1 = (bf16[512,1024]{1,0:T(8,128)(2,1)}, bf16[512,1024]{1,0:T(8,128)(2,1)}, bf16[512,1024]{1,0:T(8,128)(2,1)}, bf16[512,1024]{1,0:T(8,128)(2,1)}, bf16[5...) custom-call(bf16[512,1024]{1,0:T(8,128)(2,1)} %bitcast.52, ...), custom_call_target="tpu_custom_call" | custom-call | tf_op jit(solution)/shard_map/forward/pallas_call | solution.py:283
  28.0 242.0 %backward.1 = (bf16[512,1024]{1,0:T(8,128)(2,1)}, bf16[512,1024]{1,0:T(8,128)(2,1)}, f32[128,256]{1,0:T(8,128)}, f32[128,256]{1,0:T(8,128)}, f32[128,256]{1,0:T(...) custom-call(bf16[512,1024]{1,0:T(8,128)(2,1)} %bitcast.54, ...), custom_call_target="tpu_custom_call" | custom-call | tf_op jit(solution)/shard_map/backward/pallas_call | solution.py:1148
  270.0 0.0 copy-start
  270.0 1.6 slice_bitcast_fusion
  271.5 0.0 copy-start.7
  271.6 0.0 copy-start.6
  271.6 0.0 copy-start.5
  271.6 0.0 copy-start.4
  271.6 2.3 copy.59
  273.9 0.0 copy-done
  273.9 0.0 copy-start.2
  273.9 0.0 copy-start.1
  273.9 1.0 copy.60
  274.9 0.0 copy-done.7
  274.9 0.0 copy-start.3
  274.9 0.7 copy.61
  275.5 0.0 copy-done.6
  275.5 0.7 copy.62
  276.2 0.0 copy-done.5
  276.2 0.7 copy.63
  276.9 0.0 copy-done.4
  276.9 0.7 copy.64
  277.5 0.0 copy-done.2
  277.5 0.8 copy.65
  278.3 0.0 copy-done.1
  278.3 0.8 copy.66
  279.1 0.0 copy-done.3
  279.1 0.7 copy.67
Async XLA Ops:
  270.0 3.9 %copy-start = (bf16[512,1024]{1,0:T(8,128)(2,1)S(1)}, bf16[512,1024]{1,0:T(8,128)(2,1)}, u32[]{:S(2)}) copy-start(bf16[512,1024]{1,0:T(8,128)(2,1)} %get-tuple-element.66) | copy-start | bytes 3145732
  271.5 3.3 %copy-start.7 = (f32[128,256]{1,0:T(8,128)S(1)}, f32[128,256]{1,0:T(8,128)}, u32[]{:S(2)}) copy-start(f32[128,256]{1,0:T(8,128)} %get-tuple-element.118) | copy-start | bytes 393220
  271.6 4.0 %copy-start.6 = (f32[128,256]{1,0:T(8,128)S(1)}, f32[128,256]{1,0:T(8,128)}, u32[]{:S(2)}) copy-start(f32[128,256]{1,0:T(8,128)} %get-tuple-element.119) | copy-start | bytes 393220
  271.6 4.6 %copy-start.5 = (f32[128,256]{1,0:T(8,128)S(1)}, f32[128,256]{1,0:T(8,128)}, u32[]{:S(2)}) copy-start(f32[128,256]{1,0:T(8,128)} %get-tuple-element.120) | copy-start | bytes 393220
  271.6 5.3 %copy-start.4 = (f32[128,256]{1,0:T(8,128)S(1)}, f32[128,256]{1,0:T(8,128)}, u32[]{:S(2)}) copy-start(f32[128,256]{1,0:T(8,128)} %get-tuple-element.121) | copy-start | bytes 393220
  273.9 3.6 %copy-start.2 = (f32[128,1024]{1,0:T(8,128)S(1)}, f32[128,1024]{1,0:T(8,128)}, u32[]{:S(2)}) copy-start(f32[128,1024]{1,0:T(8,128)} %get-tuple-element.122) | copy-start | bytes 1572868
  273.9 4.4 %copy-start.1 = (f32[512,256]{1,0:T(8,128)S(1)}, f32[512,256]{1,0:T(8,128)}, u32[]{:S(2)}) copy-start(f32[512,256]{1,0:T(8,128)} %get-tuple-element.123) | copy-start | bytes 1572868
  274.9 4.2 %copy-start.3 = (f32[128,256]{1,0:T(8,128)S(1)}, f32[128,256]{1,0:T(8,128)}, u32[]{:S(2)}) copy-start(f32[128,256]{1,0:T(8,128)} %get-tuple-element.124) | copy-start | bytes 393220

commit v3 on v2

--- a/solution.py
+++ b/solution.py
@@ -15,287 +15,6 @@
 T = 512
 D = 1024
 SUB = T // 8
-
-
-def matmul_ref(out, a, b):
-    out[...] = jnp.dot(a[...], b[...], preferred_element_type=F32)
-
-
-def normalize(v, gain, bias):
-    mean = jnp.mean(v, axis=-1, keepdims=True)
-    cen = v - mean
-    var = jnp.mean(cen * cen, axis=-1, keepdims=True)
-    return cen * lax.rsqrt(var + 1e-5) * gain + bias
-
-
-def step_weights(delta):
-    e = jnp.exp(-jnp.abs(delta))
-    up = delta >= 0
-    return jnp.where(up, 1.0, e), jnp.where(up, e, 1.0)
-
-
-def join(early, late, span):
-    em, en, ed = early
-    lm, ln, ld = late
-    a, b = step_weights(em + span - lm)
-    return jnp.maximum(em + span, lm), a * en + b * ln, a * ed + b * ld
-
-
-def fwd_kernel(*refs):
-    (x_hbm, wk_h, wv_h, wr_h, wo_h, g1, b1, mk, mv, mr, td, tf, g2, b2, fmk, fmr, sn, sd, sm, pa, pf) = refs[:21]
-    (o_kin, o_vin, o_rin, o_gat, o_fk, o_fr, o_mid, o_k, o_v, o_r, o_mix, o_m, o_n, o_d, o_edge) = refs[21:36]
-    (xb, lanes, xf, xp, nb, kin, vin, rin, gat, fki, fri, wbuf, kb, vb, rb, mixb, mb, nmb, db,
-     es, er, fs, fr, ss, sr, cur, edges, insem, outsem, esem, fsem, ssem, rsem) = refs[36:]
-    s = lax.axis_index("seq")
-    b = lax.axis_index("batch")
-    bar = pltpu.get_barrier_semaphore()
-    for d in range(1, NS):
-        pl.semaphore_signal(bar, inc=1, device_id=(lax.rem(s + d, NS), b), device_id_type=MESH)
-    loads = [pltpu.make_async_copy(x_hbm, xb, insem.at[0])]
-    for i, w in enumerate((wk_h, wv_h, wr_h, wo_h)):
-        loads.append(pltpu.make_async_copy(w, wbuf.at[i], insem.at[1 + i]))
-    for cp in loads:
-        cp.start()
-    pending = []
-
-    def put(src, dst):
-        cp = pltpu.make_async_copy(src, dst, outsem.at[len(pending)])
-        cp.start()
-        pending.append(cp)
-
-    def edge(src, dst, i, sem):
-        return pltpu.make_async_remote_copy(src_ref=src, dst_ref=dst, send_sem=sem.at[0], recv_sem=sem.at[1], device_id=(i, b), device_id_type=MESH)
-
-    loads[0].wait()
-    es[...] = normalize(xb[T - 16:T, :].astype(F32), g1[...], b1[...])[8:16, :]
-    pl.semaphore_wait(bar, NS - 1)
-    to_next = edge(es, er, jnp.minimum(s + 1, NS - 1), esem)
-
-    @pl.when(s < NS - 1)
-    def _():
-        to_next.start()
-
-    def widen(i, _):
-        rows = pl.ds(pl.multiple_of(i * 64, 64), 64)
-        for g in range(8):
-            lanes[g, rows, :] = xb[rows, g * 128:g * 128 + 128].astype(F32)
-        return 0
-
-    lax.fori_loop(0, T // 64, widen, 0)
-
-    def norm1(j, _):
-        rows = pl.ds(pl.multiple_of(j * 8, 8), 8)
-        v = jnp.concatenate([lanes[g, pl.ds(j, 8, stride=SUB), :] for g in range(8)], axis=1)
-        xp[rows, :] = v
-        nb[pl.ds(pl.multiple_of(j * 8 + 8, 8), 8), :] = normalize(v, g1[...], b1[...])
-        return 0
-
-    lax.fori_loop(0, SUB, norm1, 0, unroll=4)
-    first_row = lax.broadcasted_iota(jnp.int32, (8, D), 0) == 0
-
-    def header(buf, start_row):
-        tail = pltpu.roll(buf[T:T + 8, :], 1, 0)
-        buf[0:8, :] = jnp.where(first_row, start_row, tail)
-
-    def mix(buf, pairs, i):
-        rows = pl.ds(pl.multiple_of(i * 32, 32), 32)
-        before = buf[rows, :]
-        now = buf[pl.ds(pl.multiple_of(i * 32 + 8, 8), 32), :]
-        for dst, w in pairs:
-            dst[rows, :] = (now * w[...] + before * (1.0 - w[...])).astype(BF)
-
-    @pl.when(s > 0)
-    def _():
-        to_next.wait_recv()
-
-    header(nb, jnp.where(s == 0, pa[...], er[7:8, :]))
-    edges[0:8, :] = nb[0:8, :]
-
-    def mix1(i, _):
-        mix(nb, ((kin, mk), (vin, mv), (rin, mr)), i)
-        return 0
-
-    lax.fori_loop(0, T // 32, mix1, 0)
-    put(kin, o_kin)
-    put(vin, o_vin)
-    put(rin, o_rin)
-    loads[1].wait()
-    matmul_ref(kb, kin, wbuf.at[0])
-    loads[2].wait()
-    matmul_ref(vb, vin, wbuf.at[1])
-    put(kb, o_k)
-    put(vb, o_v)
-    decay = -jnp.exp(td[...])
-
-    def own(h):
-        cols = pl.ds(h * 512, 512)
-        w = jnp.broadcast_to(decay[:, h * 512:h * 512 + 512], (8, 512))
-
-        def step(j, state):
-            rows = pl.ds(pl.multiple_of(j * 8, 8), 8)
-            m, n, d = state
-            k, v = kb[rows, cols], vb[rows, cols]
-            low = m + w
-            a, bb = step_weights(low - k)
-            return jnp.maximum(low, k), a * n + bb * v, a * d + bb
-
-        zero = jnp.zeros((8, 512), F32)
-        k, v = kb[0:8, cols], vb[0:8, cols]
-        return lax.fori_loop(1, SUB, step, (k, v, zero + 1.0), unroll=3)
-
-    halves = [own(h) for h in range(2)]
-    total = tuple(jnp.concatenate([halves[0][i], halves[1][i]], axis=1) for i in range(3))
-    row = lax.broadcasted_iota(jnp.int32, (8, D), 0)
-    span = SUB * decay
-
-    def earlier(state, dist):
-        m, n, d = (pltpu.roll(p, dist, 0) for p in state)
-        out = row < dist
-        return jnp.where(out, -1e30, m), jnp.where(out, 0.0, n), jnp.where(out, 0.0, d)
-
-    for dist in (1, 2, 4):
-        total = join(earlier(total, dist), total, dist * span)
-    before_own = earlier(total, 1)
-    m, n, d = (p[7:8, :] for p in total)
-    ss[...] = jnp.where(row == 0, m, jnp.where(row == 1, n, d))
-
-    def state_copy(src, dst):
-        return pltpu.make_async_remote_copy(src_ref=ss, dst_ref=sr.at[src], send_sem=ssem.at[dst], recv_sem=rsem.at[src], device_id=(dst, b), device_id_type=MESH)
-
-    for i in range(1, NS):
-        @pl.when(s < i)
-        def _(i=i):
-            state_copy(s, i).start()
-
-    loads[3].wait()
-    matmul_ref(rb, rin, wbuf.at[2])
-    put(rb, o_r)
-    cur[0:1, :] = sm[...]
-    cur[1:2, :] = sn[...]
-    cur[2:3, :] = sd[...]
-    for i in range(NS - 1):
-        @pl.when(i < s)
-        def _(i=i):
-            state_copy(i, NS - 1).wait_recv()
-            got = (sr[i, 0:1, :], sr[i, 1:2, :], sr[i, 2:3, :])
-            now = join((cur[0:1, :], cur[1:2, :], cur[2:3, :]), got, 8.0 * span)
-            for r in range(3):
-                cur[r:r + 1, :] = now[r]
-
-    lifted = cur[0:1, :] + row.astype(F32) * span
-    wide = tuple(jnp.broadcast_to(cur[r:r + 1, :], (8, D)) for r in (1, 2))
-    begin = join((lifted,) + wide, before_own, 0.0)
-
-    def outputs(h):
-        cols = pl.ds(h * 512, 512)
-        w = jnp.broadcast_to(decay[:, h * 512:h * 512 + 512], (8, 512))
-        bonus = jnp.broadcast_to(tf[:, h * 512:h * 512 + 512], (8, 512))
-
-        def one(j, state):
-            rows = pl.ds(pl.multiple_of(j * 8, 8), 8)
-            m, n, d = state
-            k, v = kb[rows, cols], vb[rows, cols]
-            mb[rows, cols] = m
-            nmb[rows, cols] = n
-            db[rows, cols] = d
-            p, u = step_weights(m - (bonus + k))
-            mixed = (p * n + u * v) / (p * d + u)
-            mixb[rows, cols] = mixed
-            low = m + w
-            a, bb = step_weights(low - k)
-            return (jnp.maximum(low, k), a * n + bb * v, a * d + bb), jax.nn.sigmoid(rb[rows, cols]) * mixed
-
-        def two(i, state):
-            state, ga = one(2 * i, state)
-            state, gb = one(2 * i + 1, state)
-            gat[pl.ds(pl.multiple_of(i * 16, 16), 16), cols] = jnp.concatenate([ga, gb], axis=0).astype(BF)
-            return state
-
-        lax.fori_loop(0, SUB // 2, two, tuple(p[:, h * 512:h * 512 + 512] for p in begin))
-
-    for h in range(2):
-        outputs(h)
-    put(gat, o_gat)
-    put(mixb, o_mix)
-    put(mb, o_m)
-    put(nmb, o_n)
-    put(db, o_d)
-    loads[4].wait()
-    matmul_ref(xf, gat, wbuf.at[3])
-
-    def norm2(i):
-        rows = pl.ds(pl.multiple_of(i * 32, 32), 32)
-        v = xp[rows, :] + xf[rows, :]
-        xp[rows, :] = v
-        nb[pl.ds(pl.multiple_of(i * 32 + 8, 8), 32), :] = normalize(v, g2[...], b2[...])
-
-    norm2(T // 32 - 1)
-    fs[...] = nb[T:T + 8, :]
-    to_next2 = edge(fs, fr, jnp.minimum(s + 1, NS - 1), fsem)
-
-    @pl.when(s < NS - 1)
-    def _():
-        to_next2.start()
-
-    def norm2_loop(i, _):
-        norm2(i)
-        return 0
-
-    lax.fori_loop(0, T // 32 - 1, norm2_loop, 0)
-    put(xp, o_mid)
-
-    def mix2(i, _):
-        mix(nb, ((fki, fmk), (fri, fmr)), i)
-        return 0
-
-    lax.fori_loop(1, T // 32, mix2, 0)
-
-    @pl.when(s > 0)
-    def _():
-        to_next2.wait_recv()
-
-    header(nb, jnp.where(s == 0, pf[...], fr[7:8, :]))
-    edges[8:16, :] = nb[0:8, :]
-    put(edges, o_edge)
-    mix2(0, 0)
-    put(fki, o_fk)
-    put(fri, o_fr)
-
-    @pl.when(s < NS - 1)
-    def _():
-        to_next.wait_send()
-        to_next2.wait_send()
-
-    for i in range(1, NS):
-        @pl.when(s < i)
-        def _(i=i):
-            state_copy(s, i).wait_send()
-    for cp in pending:
-        cp.wait()
-
-
-def fwd_call(x, wk, wv, wr, wo, vectors, states):
-    anyspec = pl.BlockSpec(memory_space=pl.ANY)
-    vm = pl.BlockSpec(memory_space=pltpu.VMEM)
-    low, full = jax.ShapeDtypeStruct((T, D), BF), jax.ShapeDtypeStruct((T, D), F32)
-    sem = pltpu.SemaphoreType.DMA
-    V = pltpu.VMEM
-    return pl.pallas_call(
-        fwd_kernel,
-        out_shape=[low] * 6 + [full] * 8 + [jax.ShapeDtypeStruct((16, D), F32)],
-        in_specs=[anyspec] * 5 + [vm] * 16,
-        out_specs=[anyspec] * 15,
-        scratch_shapes=[
-            V((T, D), BF), V((8, T, 128), F32), V((T, D), F32), V((T, D), F32), V((T + 8, D), F32),
-            V((T, D), BF), V((T, D), BF), V((T, D), BF), V((T, D), BF), V((T, D), BF), V((T, D), BF),
-            V((4, D, D), BF), V((T, D), F32), V((T, D), F32), V((T, D), F32), V((T, D), F32), V((T, D), F32), V((T, D), F32), V((T, D), F32),
-            V((8, D), F32), V((8, D), F32), V((8, D), F32), V((8, D), F32), V((8, D), F32), V((NS, 8, D), F32), V((8, D), F32), V((16, D), F32),
-            sem((5,)), sem((15,)), sem((2,)), sem((2,)), sem((NS,)), sem((NS,)),
-        ],
-        compiler_params=pltpu.CompilerParams(collective_id=1, has_side_effects=True, vmem_limit_bytes=67043328),
-        name="forward",
-    )(x, wk, wv, wr, wo, *vectors, *states)
-
 
 NZ = 4
 NM = 13
@@ -308,6 +27,26 @@
 RETIRE = 9
 
 
+def normalize(v, gain, bias):
+    mean = jnp.mean(v, axis=-1, keepdims=True)
+    cen = v - mean
+    var = jnp.mean(cen * cen, axis=-1, keepdims=True)
+    return cen * lax.rsqrt(var + 1e-5) * gain + bias
+
+
+def step_weights(delta):
+    e = jnp.exp(-jnp.abs(delta))
+    up = delta >= 0
+    return jnp.where(up, 1.0, e), jnp.where(up, e, 1.0)
+
+
+def join(early, late, span):
+    em, en, ed = early
+    lm, ln, ld = late
+    a, b = step_weights(em + span - lm)
+    return jnp.maximum(em + span, lm), a * en + b * ln, a * ed + b * ld
+
+
 def contract0(a, b):
     return lax.dot_general(a, b, (((0,), (0,)), ((), ())), preferred_element_type=F32)
 
@@ -345,17 +84,17 @@
     return pltpu.make_async_remote_copy(src_ref=src, dst_ref=dst, send_sem=ss, recv_sem=rs, device_id=dev, device_id_type=MESH)
 
 
-def bwd_kernel(*refs):
-    (cot_h, x_h, wfk_h, wfv_h, wfr_h, wo_h, wr_h, wv_h, wk_h,
-     kin_h, vin_h, rin_h, gat_h, fk_h, fr_h, mid_h, k_h, v_h, r_h, mix_h, m_h, n_h, d_h) = refs[:23]
-    (edges, g1, b1, mk, mv, mr, td, tf, g2, b2, fmk, fmr, sn, sd) = refs[23:37]
-    (o_blk, o_inp) = refs[37:39]
-    outs = refs[39:46]
-    sm_out = refs[46]
-    (ob, wbuf, G, V, K, X, lanes, lanes2, st, sums, RS, es, er, fs, fr, ws, wr,
+def block_kernel(*refs):
+    x_h, cot_h, wk_h, wv_h, wr_h, wo_h, wfk_h, wfv_h, wfr_h = refs[:9]
+    (g1, b1, mk, mv, mr, td, tf, g2, b2, fmk, fmr, sn, sd, sm, pa, pf) = refs[9:25]
+    o_blk, o_inp = refs[25:27]
+    outs = refs[27:34]
+    sm_out = refs[34]
+    kin_h, vin_h, rin_h, gat_h, k_h, v_h, r_h, mix_h, m_h, n_h, d_h = refs[35:46]
+    (ob, wbuf, Y, G, V, K, X, lanes, lanes2, st, sums, RS, es, er, fs, fr, ws, wr, edges, as_, ar, bs_, br_, us, ur,
      acc, sbuf, rF, rSA, rSE, rZA, rZE, smb, smr,
-     obsem, wsem, stsem, bigsem, outsem, esem, fsem, wssem, wrsem,
-     s0s, s0r, sFs, sFr, sSs, sSr, sZs, sZr, osem, msem, mss, msr) = refs[47:]
+     obsem, wsem, stsem, bigsem, outsem, spsem, esem, fsem, asem, bsem, wssem, wrsem, ussem, ursem,
+     s0s, s0r, sFs, sFr, sSs, sSr, sZs, sZr, osem, msem, mss, msr) = refs[46:]
     me = Place()
     z, x, y, c, s = me.z, me.x, me.y, me.c, me.s
     left, right = (jnp.maximum(s - 1, 0), me.b), (jnp.minimum(s + 1, NS - 1), me.b)
@@ -382,7 +121,7 @@
     def slab_rows(src, j, dst, sem):
         return [local(src.at[pl.ds(i * 512 + j * 128, 128), :], dst.at[pl.ds(i * 128, 128), :], sem) for i in range(8)]
 
-    weights = [("p", wfr_h)]
+    weights = [("p", wk_h), ("p", wv_h), ("p", wr_h), ("p", wo_h), ("p", wfr_h)]
     for j in range(4):
         weights += [("c", wfk_h, j), ("r", wfv_h, j)]
     weights += [("p", wfr_h), ("p", wo_h), ("p", wr_h), ("p", wv_h), ("p", wk_h)]
@@ -690,13 +429,13 @@
         tiles(2, 512, body)
 
     def gate_step():
-        w_wait(0)
+        w_wait(4)
 
         def mm(i, cols):
-            G[:, cols] = jnp.dot(ob[10], wbuf[0, :, cols], preferred_element_type=F32)
+            G[:, cols] = jnp.dot(ob[10], wbuf[4 % 3, :, cols], preferred_element_type=F32)
 
         halves(mm)
-        w_start(3)
+        w_start(7)
 
         def body(i, rows):
             gate = jax.nn.sigmoid(G[rows, :])
@@ -706,8 +445,8 @@
         tiles(T // 32, 32, body)
 
     def hid(j):
-        w_wait(1 + 2 * j)
-        slot = (1 + 2 * j) % 3
+        w_wait(5 + 2 * j)
+        slot = (5 + 2 * j) % 3
 
         def mm(i, cols):
             up = jnp.maximum(jnp.dot(ob[9], wbuf[slot, :, cols], preferred_element_type=F32), 0.0)
@@ -717,8 +456,8 @@
         halves(mm)
 
     def gpre(j):
-        w_wait(2 + 2 * j)
-        slot = (2 + 2 * j) % 3
+        w_wait(6 + 2 * j)
+        slot = (6 + 2 * j) % 3
 
         def mm(i, cols):
             back = contract1(ob[8], wbuf[slot, cols, :])
@@ -727,34 +466,32 @@
         halves(mm)
 
     def gk_step(j):
-        slot = (1 + 2 * j) % 3
+        slot = (5 + 2 * j) % 3
 
         def mm(i, cols):
             part = contract1(ob[4 + j], wbuf[slot, cols, :])
             K[pl.ds(0, T), cols] = part if j == 0 else K[pl.ds(0, T), cols] + part
 
         halves(mm)
-        w_start(1 + 2 * j + 3)
+        w_start(5 + 2 * j + 3)
 
     def ffv(j):
-        slot = (2 + 2 * j) % 3
+        slot = (6 + 2 * j) % 3
 
         def mm(i, cols):
             part = jnp.dot(ob[j], wbuf[slot, :, cols], preferred_element_type=F32)
             V[pl.ds(0, T), cols] = part if j == 0 else V[pl.ds(0, T), cols] + part
 
         halves(mm)
-        w_start(2 + 2 * j + 3)
+        w_start(6 + 2 * j + 3)
 
     def big_load(src, dst, i):
         return local(src, dst.at[pl.ds(0, T)], bigsem.at[i])
 
     def block_step():
-        big_load(mid_h, X, 0).wait()
-
         def body(i, rows):
             gate, values = G[rows, :], V[rows, :]
-            unspread(i, 4, X[rows, :] + gate * values)
+            unspread(i, 4, Y[rows, :] + gate * values)
             ob[0, rows, :] = (spread(i, 4) * values * gate * (1.0 - gate)).astype(BF)
 
         tiles(T // 32, 32, body)
@@ -769,13 +506,13 @@
         return rcopy(src, dst, sem.at[0], sem.at[1], dev)
 
     def recept_back():
-        w_wait(9)
+        w_wait(13)
 
         def mm(i, cols):
-            V[pl.ds(0, T), cols] = contract1(ob[0], wbuf[0, cols, :])
+            V[pl.ds(0, T), cols] = contract1(ob[0], wbuf[13 % 3, cols, :])
 
         halves(mm)
-        w_start(12)
+        w_start(16)
         tail(K)
         tail(V)
         es[...] = K[0:8, :] * (1.0 - fmk[...]) + V[0:8, :] * (1.0 - fmr[...])
@@ -823,7 +560,7 @@
 
         def body(i, _):
             rows = pl.ds(pl.multiple_of(i * 32, 32), 32)
-            n, inv = centre(X[rows, :])
+            n, inv = centre(Y[rows, :])
             grad = ln_tile(i, rows, n, g2, b2, ((K, fmk), (V, fmr)), arrived, (9, 10), (7, 8))
             gm = spread(i, 4) + ln_back(grad, n, inv, g2)
             G[rows, :] = gm
@@ -838,13 +575,13 @@
         sums[15, 0:1, :] = es[0:1, :]
 
     def gated_back():
-        w_wait(10)
+        w_wait(14)
 
         def mm(i, cols):
-            V[pl.ds(0, T), cols] = contract1(ob[1], wbuf[1, cols, :])
+            V[pl.ds(0, T), cols] = contract1(ob[1], wbuf[14 % 3, cols, :])
 
         halves(mm)
-        w_start(13)
+        w_start(17)
         big_load(r_h, X, 0).wait()
         big_load(mix_h, K, 1).wait()
 
@@ -1055,13 +792,13 @@
         3: [lambda: gk_step(1), lambda: hid(2)],
         4: [lambda: ffv(1), lambda: gpre(2)],
         5: [lambda: gk_step(2), lambda: hid(3), lambda: start_all(op_load(gat_h, 4))],
-        6: [lambda: ffv(2), lambda: gpre(3), lambda: big_load(mid_h, X, 0).start()],
+        6: [lambda: ffv(2), lambda: gpre(3)],
         7: [lambda: gk_step(3), lambda: ffv(3)],
         8: [block_step],
         9: [recept_back],
         10: [lambda: middle_back(0, 8)],
-        11: [lambda: wait_from_right(edge(es, er, esem, left)), lambda: middle_back(8, 16), middle_end,
-             lambda: start_all(big_load(r_h, X, 0), big_load(mix_h, K, 1)), lambda: st_start(7, 3),
+        11: [lambda: start_all(big_load(r_h, X, 0)), lambda: wait_from_right(edge(es, er, esem, left)), lambda: middle_back(8, 16), middle_end,
+             lambda: start_all(big_load(mix_h, K, 1)), lambda: st_start(7, 3),
              lambda: local(ob.at[5], o_blk, outsem.at[0]).wait(), lambda: start_all(op_load(rin_h, 5))],
         12: [gated_back],
         13: [lambda: first_pass(0)],
@@ -1069,8 +806,8 @@
         15: [second_start, lambda: second_pass(0, 2), lambda: start_all(op_load(vin_h, 8))],
         16: [lambda: second_pass(2, 3)],
         17: [lambda: second_pass(5, 3), second_end, lambda: start_all(op_load(kin_h, 7), op_load(x_h, 9))],
-        18: [lambda: input_mm(11, 2, X), lambda: input_mm(12, 3, V)],
-        19: [lambda: input_mm(13, 6, K), input_edge, lambda: op_load(x_h, 9).wait(), lambda: widen(9)],
+        18: [lambda: input_mm(15, 2, X), lambda: input_mm(16, 3, V)],
+        19: [lambda: input_mm(17, 6, K), input_edge, lambda: op_load(x_h, 9).wait(), lambda: widen(9)],
         20: [lambda: input_back(0, 8)],
         21: [lambda: wait_from_right(edge(fs, fr, fsem, left)), lambda: input_back(8, 16), input_end],
         23: [sm1],
@@ -1082,18 +819,196 @@
     }
     landed = {18: (gat_h, 4), 20: (rin_h, 5), 22: (vin_h, 8), 24: (kin_h, 7)}
 
-    start_all(op_load(fr_h, 10), op_load(cot_h, 1), op_load(fk_h, 9))
+    def spill(src, dst, i):
+        return local(src, dst, spsem.at[i])
+
+    kb, vb, rb, nb = G, V, X, K
+    to_next = rcopy(as_, ar, asem.at[0], asem.at[1], right)
+    to_next2 = rcopy(bs_, br_, bsem.at[0], bsem.at[1], right)
+
+    def wait_from_left(cp):
+        @pl.when(s > 0)
+        def _():
+            cp.wait_recv()
+
+    def send_right(cp):
+        @pl.when(s < NS - 1)
+        def _():
+            cp.start()
+
+    def norm1(j, _):
+        rows = pl.ds(pl.multiple_of(j * 8, 8), 8)
+        v = spread(j, 1)
+        Y[rows, :] = v
+        nb[pl.ds(pl.multiple_of(j * 8 + 8, 8), 8), :] = normalize(v, g1[...], b1[...])
+        return 0
+
+    def header(start_row):
+        nb[0:8, :] = jnp.where(row8 == 0, start_row, pltpu.roll(nb[T:T + 8, :], 1, 0))
+
+    def mix(pairs, i):
+        rows = pl.ds(pl.multiple_of(i * 32, 32), 32)
+        before = nb[rows, :]
+        now = nb[pl.ds(pl.multiple_of(i * 32 + 8, 8), 32), :]
+        for slot, w in pairs:
+            ob[slot, rows, :] = (now * w[...] + before * (1.0 - w[...])).astype(BF)
+
+    def project(i, slot, dst):
+        w_wait(i)
+        dst[pl.ds(0, T), :] = jnp.dot(ob[slot], wbuf[i % 3], preferred_element_type=F32)
+        w_start(i + 3)
+
+    start_all(op_load(x_h, 4), op_load(cot_h, 5))
     for i in range(3):
         w_start(i)
+    op_load(x_h, 4).wait()
+    as_[...] = normalize(ob[4, T - 16:T, :].astype(F32), g1[...], b1[...])[8:16, :]
+    pl.semaphore_wait(bar, NS + 1)
+    send_right(to_next)
+    widen(4)
+    lax.fori_loop(0, SUB, norm1, 0, unroll=4)
+    wait_from_left(to_next)
+    header(jnp.where(s == 0, pa[...], ar[7:8, :]))
+    edges[0:8, :] = nb[0:8, :]
+    tiles(T // 32, 32, lambda i, rows: mix(((0, mk), (1, mv), (2, mr)), i))
+    start_all(spill(ob.at[0], kin_h, 0), spill(ob.at[1], vin_h, 1), spill(ob.at[2], rin_h, 2))
+    project(0, 0, kb)
+    project(1, 1, vb)
+    start_all(spill(kb, k_h, 3), spill(vb.at[pl.ds(0, T)], v_h, 4))
+
+    def own_state(h):
+        cols = slice(h * 512, h * 512 + 512)
+        w = wide(decay, cols)
+
+        def step(j, state):
+            rows = pl.ds(pl.multiple_of(j * 8, 8), 8)
+            m, n, d = state
+            k, v = kb[rows, cols], vb[rows, cols]
+            low = m + w
+            a, b = step_weights(low - k)
+            return jnp.maximum(low, k), a * n + b * v, a * d + b
+
+        return lax.fori_loop(1, SUB, step, (kb[0:8, cols], vb[0:8, cols], jnp.ones((8, 512), F32)), unroll=3)
+
+    parts = [own_state(h) for h in range(2)]
+    total = tuple(jnp.concatenate([parts[0][i], parts[1][i]], axis=1) for i in range(3))
+
+    def earlier(state, dist):
+        m, n, d = (pltpu.roll(p, dist, 0) for p in state)
+        out = row8 < dist
+        return jnp.where(out, -1e30, m), jnp.where(out, 0.0, n), jnp.where(out, 0.0, d)
+
+    for dist in (1, 2, 4):
+        total = join(earlier(total, dist), total, dist * span)
+    before_own = earlier(total, 1)
+    us[...] = jnp.where(row8 == 0, total[0][7:8], jnp.where(row8 == 1, total[1][7:8], total[2][7:8]))
+
+    def reach_copy(src, dst):
+        return rcopy(us, ur.at[src], ussem.at[dst], ursem.at[src], (dst, me.b))
+
+    for i in range(1, NS):
+        @pl.when(s < i)
+        def _(i=i):
+            reach_copy(s, i).start()
+
+    project(2, 2, rb)
+    start_all(spill(rb.at[pl.ds(0, T)], r_h, 5))
+    op_load(cot_h, 5).wait()
+    widen(5)
+    RS[0, 0:1, :] = sm[...]
+    RS[1, 0:1, :] = sn[...]
+    RS[2, 0:1, :] = sd[...]
+    for i in range(NS - 1):
+        @pl.when(i < s)
+        def _(i=i):
+            reach_copy(i, NS - 1).wait_recv()
+            now = join(tuple(RS[r, 0:1, :] for r in range(3)), tuple(ur[i, r:r + 1, :] for r in range(3)), 8.0 * span)
+            for r in range(3):
+                RS[r, 0:1, :] = now[r]
+
+    base = tuple(RS[r, 0:1, :] for r in range(3))
+    lifted = (base[0] + row8.astype(F32) * span, jnp.broadcast_to(base[1], (8, D)), jnp.broadcast_to(base[2], (8, D)))
+    for r, v in enumerate(join(lifted, before_own, 0.0)):
+        RS[r] = v
+
+    def state_spills(blk, slot):
+        rows = pl.ds(pl.multiple_of(blk * 64, 64), 64)
+        return [local(st.at[slot, q], dst.at[rows, :], stsem.at[slot, q]) for q, dst in enumerate((mix_h, m_h, n_h, d_h))]
+
+    def outputs(blk, _):
+        slot = lax.rem(blk, 2)
+
+        @pl.when(blk >= 2)
+        def _():
+            for cp in state_spills(blk - 2, slot):
+                cp.wait()
+
+        for h in range(2):
+            cols = slice(h * 512, h * 512 + 512)
+            w, bonus = wide(decay, cols), wide(tf[...], cols)
+
+            def one(j, state):
+                at = pl.ds(pl.multiple_of(j * 8, 8), 8)
+                rows = pl.ds(pl.multiple_of(blk * 64 + j * 8, 8), 8)
+                m, n, d = state
+                k, v = kb[rows, cols], vb[rows, cols]
+                p, u = step_weights(m - (bonus + k))
+                mixed = (p * n + u * v) / (p * d + u)
+                for q, val in enumerate((mixed, m, n, d)):
+                    st[slot, q, at, cols] = val
+                low = m + w
+                a, b = step_weights(low - k)
+                return (jnp.maximum(low, k), a * n + b * v, a * d + b), jax.nn.sigmoid(rb[rows, cols]) * mixed
+
+            def two(i, state):
+                state, ga = one(2 * i, state)
+                state, gb = one(2 * i + 1, state)
+                ob[3, pl.ds(pl.multiple_of(blk * 64 + i * 16, 16), 16), cols] = jnp.concatenate([ga, gb], axis=0).astype(BF)
+                return state
+
+            for r, v in enumerate(lax.fori_loop(0, 4, two, tuple(RS[r, :, cols] for r in range(3)))):
+                RS[r, :, cols] = v
+        start_all(*state_spills(blk, slot))
+        return 0
+
+    lax.fori_loop(0, 8, outputs, 0)
+    start_all(spill(ob.at[3], gat_h, 6))
+    spill(kb, k_h, 3).wait()
+    project(3, 3, G)
+
+    def norm2(i, rows):
+        v = Y[rows, :] + G[rows, :]
+        Y[rows, :] = v
+        nb[pl.ds(pl.multiple_of(i * 32 + 8, 8), 32), :] = normalize(v, g2[...], b2[...])
+
+    norm2(T // 32 - 1, pl.ds(T - 32, 32))
+    bs_[...] = nb[T:T + 8, :]
+    send_right(to_next2)
+    tiles(T // 32 - 1, 32, norm2)
+
+    def mix2(i, _):
+        mix(((9, fmk), (10, fmr)), i)
+        return 0
+
+    lax.fori_loop(1, T // 32, mix2, 0)
+    wait_from_left(to_next2)
+    header(jnp.where(s == 0, pf[...], br_[7:8, :]))
+    edges[8:16, :] = nb[0:8, :]
+    mix2(0, 0)
+
     sums[...] = jnp.zeros_like(sums)
+    gate_step()
+    spill(ob.at[0], kin_h, 0).wait()
+    spill(rb.at[pl.ds(0, T)], r_h, 5).wait()
+    hid(0)
     RS[...] = jnp.zeros_like(RS)
-    op_load(cot_h, 1).wait()
-    widen(1)
-    op_load(fr_h, 10).wait()
-    gate_step()
-    op_load(fk_h, 9).wait()
-    hid(0)
-    pl.semaphore_wait(bar, NS + 1)
+    for i, (src, dst) in enumerate(((ob.at[1], vin_h), (ob.at[2], rin_h))):
+        spill(src, dst, 1 + i).wait()
+    spill(vb.at[pl.ds(0, T)], v_h, 4).wait()
+    spill(ob.at[3], gat_h, 6).wait()
+    for blk in (6, 7):
+        for cp in state_spills(blk, blk % 2):
+            cp.wait()
 
     def tick(t, _):
         for at, (src, slot) in landed.items():
@@ -1131,39 +1046,82 @@
         edge(es, er, esem, left).wait_send()
         edge(fs, fr, fsem, left).wait_send()
 
-    for i in range(NS - 1):
+    @pl.when(s < NS - 1)
+    def _():
+        to_next.wait_send()
+        to_next2.wait_send()
+
+    for i in range(NS):
         @pl.when(i < s)
         def _(i=i):
             state_copy(s, i).wait_send()
+
+        @pl.when(i > s)
+        def _(i=i):
+            reach_copy(s, i).wait_send()
     local(smb.at[1, x, z], sm_out, msem).wait()
     local(ob.at[0], o_inp, outsem.at[1]).wait()
 
 
-def bwd_call(cot, x, mats, acts, edges, vectors, sn, sd):
+def block_call(x, cot, mats, vectors, states):
     anyspec = pl.BlockSpec(memory_space=pl.ANY)
     vm = pl.BlockSpec(memory_space=pltpu.VMEM)
     S = jax.ShapeDtypeStruct
     sem = pltpu.SemaphoreType.DMA
     M = pltpu.VMEM
+    row = M((8, D), F32)
     return pl.pallas_call(
-        bwd_kernel,
-        out_shape=[S((T, D), BF)] * 2 + [S((128, 256), F32)] * 4 + [S((128, 1024), F32), S((512, 256), F32), S((128, 256), F32), S((16, 128), F32)],
-        in_specs=[anyspec] * 23 + [vm] * 14,
-        out_specs=[anyspec] * 10,
+        block_kernel,
+        out_shape=[S((T, D), BF)] * 2 + [S((128, 256), F32)] * 4 + [S((128, 1024), F32), S((512, 256), F32), S((128, 256), F32), S((16, 128), F32)]
+        + [S((T, D), BF)] * 4 + [S((T, D), F32)] * 7,
+        in_specs=[anyspec] * 9 + [vm] * 16,
+        out_specs=[anyspec] * 21,
         scratch_shapes=[
-            M((11, T, D), BF), M((3, D, D), BF), M((T, D), F32), M((T + 8, D), F32), M((T + 8, D), F32), M((T + 8, D), F32),
+            M((11, T, D), BF), M((3, D, D), BF), M((T, D), F32), M((T, D), F32), M((T + 8, D), F32), M((T + 8, D), F32), M((T + 8, D), F32),
             M((8, T, 128), F32), M((8, T, 128), F32), M((2, 5, 64, D), F32), M((16, 8, D), F32), M((7, 8, D), F32),
-            M((8, D), F32), M((8, D), F32), M((8, D), F32), M((8, D), F32), M((8, D), F32), M((NS, 8, D), F32),
+            row, row, row, row, row, M((NS, 8, D), F32), M((16, D), F32), row, row, row, row, row, M((NS, 8, D), F32),
             M((WIN, 2, 2, NZ, 128, 128), F32), M((2, 2, 2, NZ, 128, 128), F32), M((WINF, 2, NZ, 128, 128), F32),
             M((WIN, NZ, RA, 128), F32), M((WIN, RE, 128), F32), M((WIN, NZ + 1, RA, 128), F32), M((WIN, NZ + 1, 2, RE, 128), F32),
             M((3, 2, NZ, 16, 128), F32), M((4, 2, NZ, 16, 128), F32),
-            sem((11,)), sem((3,)), sem((2, 5)), sem((2,)), sem((2,)), sem((2,)), sem((2,)), sem((NS,)), sem((NS,)),
+            sem((11,)), sem((3,)), sem((2, 5)), sem((2,)), sem((2,)), sem((7,)), sem((2,)), sem((2,)), sem((2,)), sem((2,)), sem((NS,)), sem((NS,)), sem((NS,)), sem((NS,)),
             sem((NK,)), sem((NK,)), sem((NK,)), sem((NK,)), sem((NK, 2)), sem((NK, 2)),
             sem((NK, 2, NZ)), sem((NK, 2, NZ + 1)), sem((NK,)), sem, sem((3 + NZ,)), sem((3 + 2 * NZ,)),
         ],
         compiler_params=pltpu.CompilerParams(collective_id=0, has_side_effects=True, vmem_limit_bytes=67043328),
-        name="backward",
-    )(cot, x, *mats, *acts, edges, *vectors, sn, sd)
+        name="block",
+    )(x, cot, *mats, *vectors, *states)[:10]
+
+def finish_kernel(*refs):
+    ins, outs, (scratch, sems) = refs[:10], refs[10:35], (refs[35:-2], refs[-2:])
+    into, out = sems
+    loads = [pltpu.make_async_copy(src, buf, into.at[i]) for i, (src, buf) in enumerate(zip(ins, scratch))]
+    for cp in loads:
+        cp.start()
+    stores = []
+    for i in (9, 2, 3, 4, 5, 8, 6, 7, 0, 1):
+        loads[i].wait()
+        if i < 9:
+            stores.append(pltpu.make_async_copy(scratch[i], outs[i], out.at[i]))
+            stores[-1].start()
+        else:
+            for r in range(16):
+                stores.append(pltpu.make_async_copy(scratch[i].at[pl.ds(r, 1)], outs[9 + r], out.at[9 + r]))
+                stores[-1].start()
+    for cp in stores:
+        cp.wait()
+
+
+def finish_call(parts):
+    anyspec = pl.BlockSpec(memory_space=pl.ANY)
+    return pl.pallas_call(
+        finish_kernel,
+        out_shape=[jax.ShapeDtypeStruct(p.shape, p.dtype) for p in parts[:9]] + [jax.ShapeDtypeStruct((1, 128), F32)] * 16,
+        in_specs=[anyspec] * 10,
+        out_specs=[anyspec] * 25,
+        scratch_shapes=[pltpu.VMEM(p.shape, p.dtype) for p in parts] + [pltpu.SemaphoreType.DMA((10,)), pltpu.SemaphoreType.DMA((25,))],
+        name="finish",
+    )(*parts)
+
 
 def fits(mesh):
     return (mesh.shape["seq"], mesh.shape["batch"]) == (2 * NZ, 4)
@@ -1214,23 +1172,20 @@
         )
     ]
     states = [v.reshape(1, D) for v in (state_num, state_den, state_max, prev_att, prev_ffn)]
-    *acts, edges = fwd_call(rows, w_key, w_value, w_recept, w_output, vectors, states)
-    block_out, input_grad, *matrices, small = bwd_call(
+    parts = block_call(
+        rows,
         cotangent.reshape(T, D),
-        rows,
-        [w_ffn_key, w_ffn_value, w_ffn_recept, w_output, w_recept, w_value, w_key],
-        acts,
-        edges,
+        [w_key, w_value, w_recept, w_output, w_ffn_key, w_ffn_value, w_ffn_recept],
         vectors,
-        states[0],
-        states[1],
-    )
+        states,
+    )
+    block_out, input_grad, *rest = finish_call(parts)
     return (
         block_out.reshape(inputs.shape),
         input_grad.reshape(inputs.shape),
-        *matrices,
-        *[small[i] for i in range(11)],
-        *[small[i][:, None] for i in range(11, 16)],
+        *rest[:7],
+        *[v.reshape(128) for v in rest[7:18]],
+        *[v.reshape(128, 1) for v in rest[18:]],
     )
 
 

time: 280 us -> 271 us (0.968)
  local copies, waits for them, and re-layouts: 9.74 us -> 0 us
    unnamed x25 -> x0, local copies, waits for them, and re-layouts: 8.18 us -> none
where the time goes in v3:
time: 271 us; the launch traced here: 270 us
  Pallas kernels  270 us (100%)
    pallas_call x1, Pallas kernels, block_call(): pl.pallas_call(block_kernel, out_shape=[S((T, D), BF)] * 2 + [S((128, 256...  265 us

profile of v3, /device:TPU:0, one launch (start us, length us, event | category | flops | bytes accessed | tf_op | source)
XLA Modules:
  0.0 270.4 jit_solution(178053982264422460)
XLA Ops:
  0.7 265.4 %block.1 = (bf16[512,1024]{1,0:T(8,128)(2,1)}, bf16[512,1024]{1,0:T(8,128)(2,1)}, f32[128,256]{1,0:T(8,128)}, f32[128,256]{1,0:T(8,128)}, f32[128,256]{1,0:T(8,1...) custom-call(bf16[512,1024]{1,0:T(8,128)(2,1)} %bitcast.36, ...), custom_call_target="tpu_custom_call" | custom-call | tf_op jit(solution)/shard_map/block/pallas_call | solution.py:1073
  266.1 4.2 %finish.1 = (bf16[512,1024]{1,0:T(8,128)(2,1)}, bf16[512,1024]{1,0:T(8,128)(2,1)}, f32[128,256]{1,0:T(8,128)}, f32[128,256]{1,0:T(8,128)}, f32[128,256]{1,0:T(8,...) custom-call(bf16[512,1024]{1,0:T(8,128)(2,1)} %get-tuple-element.60., ...), custom_call_target="tpu_custom_call" | custom-call | tf_op jit(solution)/shard_map/finish/pallas_call | solution.py:1116

commit v4 on v3

--- a/solution.py
+++ b/solution.py
@@ -19,12 +19,14 @@
 NZ = 4
 NM = 13
 NK = 2 * NM
-WIN = 12
+WIN = 10
+WINZ = 8
 WINF = 4
 RA = 48
 RE = 128 - RA
 LAGS = [3, 5, 4, 5, 6, 6, 7, 8, 8]
 RETIRE = 9
+STOP = False
 
 
 def normalize(v, gain, bias):
@@ -86,15 +88,19 @@
 
 def block_kernel(*refs):
     x_h, cot_h, wk_h, wv_h, wr_h, wo_h, wfk_h, wfv_h, wfr_h = refs[:9]
-    (g1, b1, mk, mv, mr, td, tf, g2, b2, fmk, fmr, sn, sd, sm, pa, pf) = refs[9:25]
+    small_h = refs[9:25]
     o_blk, o_inp = refs[25:27]
     outs = refs[27:34]
     sm_out = refs[34]
     kin_h, vin_h, rin_h, gat_h, k_h, v_h, r_h, mix_h, m_h, n_h, d_h = refs[35:46]
     (ob, wbuf, Y, G, V, K, X, lanes, lanes2, st, sums, RS, es, er, fs, fr, ws, wr, edges, as_, ar, bs_, br_, us, ur,
      acc, sbuf, rF, rSA, rSE, rZA, rZE, smb, smr,
-     obsem, wsem, stsem, bigsem, outsem, spsem, esem, fsem, asem, bsem, wssem, wrsem, ussem, ursem,
-     s0s, s0r, sFs, sFr, sSs, sSr, sZs, sZr, osem, msem, mss, msr) = refs[46:]
+     obsem, wsem, stsem, bigsem, outsem, spsem, esem, fsem, asem, bsem, wssem, wrsem,
+     s0s, s0r, sFs, sFr, sSs, sSr, sZs, sZr, osem, msem, mss, msr, vsem) = refs[46:-16]
+    (g1, b1, mk, mv, mr, td, tf, g2, b2, fmk, fmr, sn, sd, sm, pa, pf) = refs[-16:]
+    small_loads = [pltpu.make_async_copy(src, dst, vsem) for src, dst in zip(small_h, refs[-16:])]
+    for cp in small_loads:
+        cp.start()
     me = Place()
     z, x, y, c, s = me.z, me.x, me.y, me.c, me.s
     left, right = (jnp.maximum(s - 1, 0), me.b), (jnp.minimum(s + 1, NS - 1), me.b)
@@ -149,21 +155,21 @@
         return (jnp.where(h == 0, a[0], b[0]), jnp.where(h == 0, a[1], b[1]))
 
     def copy0(k):
-        return rcopy(sbuf.at[lax.rem(k, 2)], acc.at[lax.rem(k, WIN)], s0s.at[k], s0r.at[k], me.at(c=1 - c))
+        return rcopy(sbuf.at[lax.rem(k, 2)], acc.at[lax.rem(k, WIN)], s0s.at[lax.rem(k, 2)], s0r.at[lax.rem(k, WIN)], me.at(c=1 - c))
 
     def copyF(k):
         f, _ = fs_of(k)
-        return rcopy(acc.at[lax.rem(k, WIN), 1 - f], rF.at[lax.rem(k, WINF)], sFs.at[k], sFr.at[k], partner(lax.rem(k, 2)))
+        return rcopy(acc.at[lax.rem(k, WIN), 1 - f], rF.at[lax.rem(k, WINF)], sFs.at[lax.rem(k, WIN)], sFr.at[lax.rem(k, WINF)], partner(lax.rem(k, 2)))
 
     def copySA(k):
         f, g = fs_of(k)
-        w = lax.rem(k, WIN)
-        return rcopy(acc.at[w, f, 1 - g, :, pl.ds(0, RA)], rSA.at[w], sSs.at[k, 0], sSr.at[k, 0], partner(1 - lax.rem(k, 2)))
+        w, v = lax.rem(k, WIN), lax.rem(k, WINZ)
+        return rcopy(acc.at[w, f, 1 - g, :, pl.ds(0, RA)], rSA.at[v], sSs.at[v, 0], sSr.at[v, 0], partner(1 - lax.rem(k, 2)))
 
     def copySE(k):
         f, g = fs_of(k)
-        w = lax.rem(k, WIN)
-        return rcopy(acc.at[w, f, 1 - g, z, pl.ds(RA, RE)], rSE.at[w], sSs.at[k, 1], sSr.at[k, 1], partner(1 - lax.rem(k, 2)))
+        w, v = lax.rem(k, WIN), lax.rem(k, WINZ)
+        return rcopy(acc.at[w, f, 1 - g, z, pl.ds(RA, RE)], rSE.at[v], sSs.at[v, 1], sSr.at[v, 1], partner(1 - lax.rem(k, 2)))
 
     def unit(k, q, late):
         f, g = fs_of(k)
@@ -171,15 +177,15 @@
         return acc.at[w, f, g, q, pl.ds(0, RA)] if late else acc.at[w, f, :, q, pl.ds(RA, RE)]
 
     def zbuf(k, slot, late):
-        return (rZA if late else rZE).at[lax.rem(k, WIN), slot]
+        return (rZA if late else rZE).at[lax.rem(k, WINZ), slot]
 
     def copyR(k, q, late):
         i = int(late)
-        return rcopy(unit(k, q, late), zbuf(k, q + 1, late), sZs.at[k, i, q], sZr.at[k, i, q + 1], me.at(z=z + 1))
+        return rcopy(unit(k, q, late), zbuf(k, q + 1, late), sZs.at[lax.rem(k, WINZ), i], sZr.at[lax.rem(k, WINZ), i, q + 1], me.at(z=z + 1))
 
     def copyL(k, q, late):
         i = int(late)
-        return rcopy(unit(k, q, late), zbuf(k, q, late), sZs.at[k, i, q], sZr.at[k, i, q], me.at(z=z - 1))
+        return rcopy(unit(k, q, late), zbuf(k, q, late), sZs.at[lax.rem(k, WINZ), i], sZr.at[lax.rem(k, WINZ), i, q], me.at(z=z - 1))
 
     def add_into(dst, src):
         dst[...] = dst[...] + src[...]
@@ -276,7 +282,7 @@
         copySA(k).wait_recv()
         f, g = fs_of(k)
         w = lax.rem(k, WIN)
-        add_into(acc.at[w, f, g, :, pl.ds(0, RA)], rSA.at[w])
+        add_into(acc.at[w, f, g, :, pl.ds(0, RA)], rSA.at[lax.rem(k, WINZ)])
         zsub(k, 0, True)
 
     def taskFinE(k):
@@ -287,33 +293,34 @@
         copySE(k).wait_recv()
         f, g = fs_of(k)
         w = lax.rem(k, WIN)
-        add_into(acc.at[w, f, g, z, pl.ds(RA, RE)], rSE.at[w])
+        add_into(acc.at[w, f, g, z, pl.ds(RA, RE)], rSE.at[lax.rem(k, WINZ)])
         src = acc.at[w, f, g, z]
         h, m = lax.rem(k, 2), k // 2
         half = pl.ds(pl.multiple_of(h * 128, 128), 128)
         for j in range(4):
             @pl.when(m == 2 * j)
             def _(j=j):
-                local(src, outs[5].at[pl.ds(j * 128, 128), half], osem.at[k]).start()
+                local(src, outs[5].at[pl.ds(j * 128, 128), half], osem.at[lax.rem(k, WIN)]).start()
 
             @pl.when(m == 2 * j + 1)
             def _(j=j):
-                local(src, outs[4].at[:, pl.ds(pl.multiple_of(h * 512 + j * 128, 128), 128)], osem.at[k]).start()
+                local(src, outs[4].at[:, pl.ds(pl.multiple_of(h * 512 + j * 128, 128), 128)], osem.at[lax.rem(k, WIN)]).start()
         for mm, i in ((8, 6), (9, 3), (10, 2), (11, 1), (12, 0)):
             @pl.when(m == mm)
             def _(i=i):
-                local(src, outs[i].at[:, half], osem.at[k]).start()
+                local(src, outs[i].at[:, half], osem.at[lax.rem(k, WIN)]).start()
 
     def retire(k):
         copyF(k).wait_send()
         copySA(k).wait_send()
         copySE(k).wait_send()
+        f, g = fs_of(k)
+        w, v = lax.rem(k, WIN), lax.rem(k, WINZ)
         for late in (False, True):
-            for q in range(NZ):
-                @pl.when(q != z)
-                def _(q=q, late=late):
-                    rcopy(unit(k, q, late), zbuf(k, q, late), sZs.at[k, int(late), q], sZr.at[k, int(late), q], me.at(c=1 - c)).wait_send()
-        local(acc.at[lax.rem(k, WIN), 0, 0, 0], outs[0].at[:, pl.ds(0, 128)], osem.at[k]).wait()
+            others = pl.ds(0, NZ - 1)
+            sent = acc.at[w, f, g, others, pl.ds(0, RA)] if late else acc.at[w, f, :, others, pl.ds(RA, RE)]
+            rcopy(sent, sent, sZs.at[v, int(late)], sZr.at[v, int(late), 0], me.at(c=1 - c)).wait_send()
+        local(acc.at[lax.rem(k, WIN), 0, 0, 0], outs[0].at[:, pl.ds(0, 128)], osem.at[lax.rem(k, WIN)]).wait()
 
     stages = [
         (RETIRE, retire),
@@ -611,7 +618,6 @@
         def _():
             st_start(blk - 1, count)
 
-    decay = -jnp.exp(td[...])
 
     def wide(v, cols):
         return jnp.broadcast_to(v[:, cols], (8, 512))
@@ -657,7 +663,6 @@
     def suffix(value, dist, fill):
         return jnp.where(row8 >= 8 - dist, fill, pltpu.roll(value, 8 - dist, 0))
 
-    span = SUB * decay
 
     def state_copy(src, dst):
         return rcopy(ws, wr.at[src], wssem.at[dst], wrsem.at[src], (dst, me.b))
@@ -786,8 +791,7 @@
             cp.start()
 
     compute = {
-        0: [lambda: gpre(0)],
-        1: [lambda: gk_step(0), lambda: hid(1)],
+        1: [lambda: gpre(0), lambda: gk_step(0), lambda: hid(1)],
         2: [lambda: ffv(0), lambda: gpre(1)],
         3: [lambda: gk_step(1), lambda: hid(2)],
         4: [lambda: ffv(1), lambda: gpre(2)],
@@ -836,20 +840,18 @@
         def _():
             cp.start()
 
-    def norm1(j, _):
-        rows = pl.ds(pl.multiple_of(j * 8, 8), 8)
-        v = spread(j, 1)
+    def norm1(i, rows):
+        v = spread(i, 8)
         Y[rows, :] = v
-        nb[pl.ds(pl.multiple_of(j * 8 + 8, 8), 8), :] = normalize(v, g1[...], b1[...])
-        return 0
+        nb[pl.ds(pl.multiple_of(i * 64 + 8, 8), 64), :] = normalize(v, g1[...], b1[...])
 
     def header(start_row):
         nb[0:8, :] = jnp.where(row8 == 0, start_row, pltpu.roll(nb[T:T + 8, :], 1, 0))
 
     def mix(pairs, i):
-        rows = pl.ds(pl.multiple_of(i * 32, 32), 32)
+        rows = pl.ds(pl.multiple_of(i * 64, 64), 64)
         before = nb[rows, :]
-        now = nb[pl.ds(pl.multiple_of(i * 32 + 8, 8), 32), :]
+        now = nb[pl.ds(pl.multiple_of(i * 64 + 8, 8), 64), :]
         for slot, w in pairs:
             ob[slot, rows, :] = (now * w[...] + before * (1.0 - w[...])).astype(BF)
 
@@ -861,37 +863,35 @@
     start_all(op_load(x_h, 4), op_load(cot_h, 5))
     for i in range(3):
         w_start(i)
+    local(K.at[pl.ds(0, 16)], V.at[pl.ds(0, 16)], vsem).wait()
+    decay = -jnp.exp(td[...])
+    span = SUB * decay
     op_load(x_h, 4).wait()
     as_[...] = normalize(ob[4, T - 16:T, :].astype(F32), g1[...], b1[...])[8:16, :]
     pl.semaphore_wait(bar, NS + 1)
     send_right(to_next)
     widen(4)
-    lax.fori_loop(0, SUB, norm1, 0, unroll=4)
+    tiles(T // 64, 64, norm1)
     wait_from_left(to_next)
     header(jnp.where(s == 0, pa[...], ar[7:8, :]))
     edges[0:8, :] = nb[0:8, :]
-    tiles(T // 32, 32, lambda i, rows: mix(((0, mk), (1, mv), (2, mr)), i))
+    tiles(T // 64, 64, lambda i, rows: mix(((0, mk), (1, mv), (2, mr)), i))
     start_all(spill(ob.at[0], kin_h, 0), spill(ob.at[1], vin_h, 1), spill(ob.at[2], rin_h, 2))
     project(0, 0, kb)
     project(1, 1, vb)
     start_all(spill(kb, k_h, 3), spill(vb.at[pl.ds(0, T)], v_h, 4))
 
-    def own_state(h):
-        cols = slice(h * 512, h * 512 + 512)
-        w = wide(decay, cols)
-
-        def step(j, state):
-            rows = pl.ds(pl.multiple_of(j * 8, 8), 8)
-            m, n, d = state
-            k, v = kb[rows, cols], vb[rows, cols]
-            low = m + w
-            a, b = step_weights(low - k)
-            return jnp.maximum(low, k), a * n + b * v, a * d + b
-
-        return lax.fori_loop(1, SUB, step, (kb[0:8, cols], vb[0:8, cols], jnp.ones((8, 512), F32)), unroll=3)
-
-    parts = [own_state(h) for h in range(2)]
-    total = tuple(jnp.concatenate([parts[0][i], parts[1][i]], axis=1) for i in range(3))
+    wide_decay = jnp.broadcast_to(decay, (8, D))
+
+    def own_step(j, state):
+        rows = pl.ds(pl.multiple_of(j * 8, 8), 8)
+        m, n, d = state
+        k, v = kb[rows, :], vb[rows, :]
+        low = m + wide_decay
+        a, b = step_weights(low - k)
+        return jnp.maximum(low, k), a * n + b * v, a * d + b
+
+    total = lax.fori_loop(1, SUB, own_step, (kb[0:8, :], vb[0:8, :], jnp.ones((8, D), F32)), unroll=7)
 
     def earlier(state, dist):
         m, n, d = (pltpu.roll(p, dist, 0) for p in state)
@@ -904,7 +904,7 @@
     us[...] = jnp.where(row8 == 0, total[0][7:8], jnp.where(row8 == 1, total[1][7:8], total[2][7:8]))
 
     def reach_copy(src, dst):
-        return rcopy(us, ur.at[src], ussem.at[dst], ursem.at[src], (dst, me.b))
+        return rcopy(us, ur.at[src], wssem.at[dst], wrsem.at[src], (dst, me.b))
 
     for i in range(1, NS):
         @pl.when(s < i)
@@ -966,7 +966,7 @@
                 ob[3, pl.ds(pl.multiple_of(blk * 64 + i * 16, 16), 16), cols] = jnp.concatenate([ga, gb], axis=0).astype(BF)
                 return state
 
-            for r, v in enumerate(lax.fori_loop(0, 4, two, tuple(RS[r, :, cols] for r in range(3)))):
+            for r, v in enumerate(lax.fori_loop(0, 4, two, tuple(RS[r, :, cols] for r in range(3)), unroll=4)):
                 RS[r, :, cols] = v
         start_all(*state_spills(blk, slot))
         return 0
@@ -979,18 +979,18 @@
     def norm2(i, rows):
         v = Y[rows, :] + G[rows, :]
         Y[rows, :] = v
-        nb[pl.ds(pl.multiple_of(i * 32 + 8, 8), 32), :] = normalize(v, g2[...], b2[...])
-
-    norm2(T // 32 - 1, pl.ds(T - 32, 32))
+        nb[pl.ds(pl.multiple_of(i * 64 + 8, 8), 64), :] = normalize(v, g2[...], b2[...])
+
+    norm2(T // 64 - 1, pl.ds(T - 64, 64))
     bs_[...] = nb[T:T + 8, :]
     send_right(to_next2)
-    tiles(T // 32 - 1, 32, norm2)
+    tiles(T // 64 - 1, 64, norm2)
 
     def mix2(i, _):
         mix(((9, fmk), (10, fmr)), i)
         return 0
 
-    lax.fori_loop(1, T // 32, mix2, 0)
+    lax.fori_loop(1, T // 64, mix2, 0)
     wait_from_left(to_next2)
     header(jnp.where(s == 0, pf[...], br_[7:8, :]))
     edges[8:16, :] = nb[0:8, :]
@@ -1019,7 +1019,7 @@
         for lag, task in stages:
             k = t - lag
 
-            @pl.when(jnp.logical_and(k >= 0, k < NK))
+            @pl.when(jnp.logical_and(k >= (2 if lag < 2 else 0), k < NK))
             def _(k=k, task=task):
                 task(k)
 
@@ -1030,7 +1030,11 @@
                     step()
         return 0
 
-    lax.fori_loop(0, NK + RETIRE, tick, 0)
+    for k in range(2):
+        taskP(jnp.int32(k))
+    for k in range(2):
+        task1(jnp.int32(k))
+    lax.fori_loop(1, NK + RETIRE, tick, 0)
 
     copy0(NK - 2).wait_send()
     copy0(NK - 1).wait_send()
@@ -1065,7 +1069,6 @@
 
 def block_call(x, cot, mats, vectors, states):
     anyspec = pl.BlockSpec(memory_space=pl.ANY)
-    vm = pl.BlockSpec(memory_space=pltpu.VMEM)
     S = jax.ShapeDtypeStruct
     sem = pltpu.SemaphoreType.DMA
     M = pltpu.VMEM
@@ -1074,19 +1077,19 @@
         block_kernel,
         out_shape=[S((T, D), BF)] * 2 + [S((128, 256), F32)] * 4 + [S((128, 1024), F32), S((512, 256), F32), S((128, 256), F32), S((16, 128), F32)]
         + [S((T, D), BF)] * 4 + [S((T, D), F32)] * 7,
-        in_specs=[anyspec] * 9 + [vm] * 16,
+        in_specs=[anyspec] * 25,
         out_specs=[anyspec] * 21,
         scratch_shapes=[
             M((11, T, D), BF), M((3, D, D), BF), M((T, D), F32), M((T, D), F32), M((T + 8, D), F32), M((T + 8, D), F32), M((T + 8, D), F32),
             M((8, T, 128), F32), M((8, T, 128), F32), M((2, 5, 64, D), F32), M((16, 8, D), F32), M((7, 8, D), F32),
             row, row, row, row, row, M((NS, 8, D), F32), M((16, D), F32), row, row, row, row, row, M((NS, 8, D), F32),
             M((WIN, 2, 2, NZ, 128, 128), F32), M((2, 2, 2, NZ, 128, 128), F32), M((WINF, 2, NZ, 128, 128), F32),
-            M((WIN, NZ, RA, 128), F32), M((WIN, RE, 128), F32), M((WIN, NZ + 1, RA, 128), F32), M((WIN, NZ + 1, 2, RE, 128), F32),
+            M((WINZ, NZ, RA, 128), F32), M((WINZ, RE, 128), F32), M((WINZ, NZ + 1, RA, 128), F32), M((WINZ, NZ + 1, 2, RE, 128), F32),
             M((3, 2, NZ, 16, 128), F32), M((4, 2, NZ, 16, 128), F32),
-            sem((11,)), sem((3,)), sem((2, 5)), sem((2,)), sem((2,)), sem((7,)), sem((2,)), sem((2,)), sem((2,)), sem((2,)), sem((NS,)), sem((NS,)), sem((NS,)), sem((NS,)),
-            sem((NK,)), sem((NK,)), sem((NK,)), sem((NK,)), sem((NK, 2)), sem((NK, 2)),
-            sem((NK, 2, NZ)), sem((NK, 2, NZ + 1)), sem((NK,)), sem, sem((3 + NZ,)), sem((3 + 2 * NZ,)),
-        ],
+            sem((11,)), sem((3,)), sem((2, 5)), sem((2,)), sem((2,)), sem((7,)), sem((2,)), sem((2,)), sem((2,)), sem((2,)), sem((NS,)), sem((NS,)),
+            sem((2,)), sem((WIN,)), sem((WIN,)), sem((WINF,)), sem((WINZ, 2)), sem((WINZ, 2)),
+            sem((WINZ, 2)), sem((WINZ, 2, NZ + 1)), sem((WIN,)), sem, sem((3 + NZ,)), sem((3 + 2 * NZ,)), sem,
+        ] + [M((1, D), F32)] * 16,
         compiler_params=pltpu.CompilerParams(collective_id=0, has_side_effects=True, vmem_limit_bytes=67043328),
         name="block",
     )(x, cot, *mats, *vectors, *states)[:10]

time: 271 us -> 260 us (0.959)
  Pallas kernels: 270 us -> 259 us
    pallas_call x1, Pallas kernels: 265 us -> 255 us  [block_call(): pl.pallas_call(block_kernel, out_shape=[S((T, D), BF)] * 2 + [S((128, 256...]
where the time goes in v4:
time: 260 us
  Pallas kernels  259 us (100%)
    pallas_call x1, Pallas kernels, block_call(): pl.pallas_call(block_kernel, out_shape=[S((T, D), BF)] * 2 + [S((128, 256...  255 us

profile of v4, /device:TPU:0, one launch (start us, length us, event | category | flops | bytes accessed | tf_op | source)
XLA Modules:
  0.0 259.7 jit_solution(18128447282403867354)
XLA Ops:
  0.7 254.7 %block.1 = (bf16[512,1024]{1,0:T(8,128)(2,1)}, bf16[512,1024]{1,0:T(8,128)(2,1)}, f32[128,256]{1,0:T(8,128)}, f32[128,256]{1,0:T(8,128)}, f32[128,256]{1,0:T(8,1...) custom-call(bf16[512,1024]{1,0:T(8,128)(2,1)} %bitcast.36, ...), custom_call_target="tpu_custom_call" | custom-call | tf_op jit(solution)/shard_map/block/pallas_call | solution.py:1076
  255.4 4.2 %finish.1 = (bf16[512,1024]{1,0:T(8,128)(2,1)}, bf16[512,1024]{1,0:T(8,128)(2,1)}, f32[128,256]{1,0:T(8,128)}, f32[128,256]{1,0:T(8,128)}, f32[128,256]{1,0:T(8,...) custom-call(bf16[512,1024]{1,0:T(8,128)(2,1)} %get-tuple-element.60., ...), custom_call_target="tpu_custom_call" | custom-call | tf_op jit(solution)/shard_map/finish/pallas_call | solution.py:1119

commit v5 on v4

--- a/solution.py
+++ b/solution.py
@@ -21,12 +21,12 @@
 NK = 2 * NM
 WIN = 10
 WINZ = 8
-WINF = 4
+WINF = 8
 RA = 48
 RE = 128 - RA
 LAGS = [3, 5, 4, 5, 6, 6, 7, 8, 8]
 RETIRE = 9
-STOP = False
+ROWS = 64
 
 
 def normalize(v, gain, bias):
@@ -332,8 +332,8 @@
         (LAGS[3], lambda k: zsub(k, 2, False)),
         (LAGS[2], lambda k: zsub(k, 1, False)),
         (LAGS[1], taskSA),
+        (1, task1),
         (LAGS[0], task2),
-        (1, task1),
         (0, taskP),
     ]
 
@@ -529,9 +529,9 @@
             edge(es, er, esem, left).start()
 
     def fold(v):
-        return v[0:8] + v[8:16] + v[16:24] + v[24:32]
-
-    row32 = lax.broadcasted_iota(jnp.int32, (32, D), 0)
+        return sum(v[i:i + 8] for i in range(8, ROWS, 8)) + v[0:8]
+
+    row_of = lax.broadcasted_iota(jnp.int32, (ROWS, D), 0)
 
     def centre(v):
         mean = jnp.mean(v, axis=-1, keepdims=True)
@@ -544,11 +544,11 @@
         return inv * (h - jnp.mean(h, axis=-1, keepdims=True) - n * jnp.mean(h * n, axis=-1, keepdims=True))
 
     def ln_tile(i, rows, n, gain, bias, parts, arrived, sum_rows, ln_sums):
-        later = pl.ds(pl.multiple_of(i * 32 + 8, 8), 32)
+        later = pl.ds(pl.multiple_of(i * ROWS + 8, 8), ROWS)
         normed = n * gain[...] + bias[...]
         grad = 0.0
         if arrived is not None:
-            grad = jnp.where(jnp.logical_and(row32 == 31, i == T // 32 - 1), arrived, 0.0)
+            grad = jnp.where(jnp.logical_and(row_of == ROWS - 1, i == T // ROWS - 1), arrived, 0.0)
         for (buf, w), r in zip(parts, sum_rows):
             now, nxt = buf[rows, :], buf[later, :]
             grad = grad + now * w[...] + nxt * (1.0 - w[...])
@@ -563,13 +563,13 @@
             cp.wait_recv()
 
     def middle_back(lo, hi):
-        arrived = jnp.where(s == NS - 1, 0.0, er[0:1, :]) if hi == T // 32 else None
+        arrived = jnp.where(s == NS - 1, 0.0, er[0:1, :]) if hi == T // ROWS else None
 
         def body(i, _):
-            rows = pl.ds(pl.multiple_of(i * 32, 32), 32)
+            rows = pl.ds(pl.multiple_of(i * ROWS, ROWS), ROWS)
             n, inv = centre(Y[rows, :])
             grad = ln_tile(i, rows, n, g2, b2, ((K, fmk), (V, fmr)), arrived, (9, 10), (7, 8))
-            gm = spread(i, 4) + ln_back(grad, n, inv, g2)
+            gm = spread(i, ROWS // 8) + ln_back(grad, n, inv, g2)
             G[rows, :] = gm
             ob[1, rows, :] = gm.astype(BF)
             return 0
@@ -763,13 +763,13 @@
             edge(fs, fr, fsem, left).start()
 
     def input_back(lo, hi):
-        arrived = jnp.where(s == NS - 1, 0.0, fr[0:1, :]) if hi == T // 32 else None
+        arrived = jnp.where(s == NS - 1, 0.0, fr[0:1, :]) if hi == T // ROWS else None
 
         def body(i, _):
-            rows = pl.ds(pl.multiple_of(i * 32, 32), 32)
-            n, inv = centre(spread(i, 4))
+            rows = pl.ds(pl.multiple_of(i * ROWS, ROWS), ROWS)
+            n, inv = centre(spread(i, ROWS // 8))
             grad = ln_tile(i, rows, n, g1, b1, ((K, mk), (V, mv), (X, mr)), arrived, (2, 3, 4), (0, 1))
-            unspread(i, 4, G[rows, :] + ln_back(grad, n, inv, g1))
+            unspread(i, ROWS // 8, G[rows, :] + ln_back(grad, n, inv, g1))
             return 0
 
         lax.fori_loop(lo, hi, body, 0)
@@ -800,8 +800,8 @@
         7: [lambda: gk_step(3), lambda: ffv(3)],
         8: [block_step],
         9: [recept_back],
-        10: [lambda: middle_back(0, 8)],
-        11: [lambda: start_all(big_load(r_h, X, 0)), lambda: wait_from_right(edge(es, er, esem, left)), lambda: middle_back(8, 16), middle_end,
+        10: [lambda: middle_back(0, 4)],
+        11: [lambda: start_all(big_load(r_h, X, 0)), lambda: wait_from_right(edge(es, er, esem, left)), lambda: middle_back(4, 8), middle_end,
              lambda: start_all(big_load(mix_h, K, 1)), lambda: st_start(7, 3),
              lambda: local(ob.at[5], o_blk, outsem.at[0]).wait(), lambda: start_all(op_load(rin_h, 5))],
         12: [gated_back],
@@ -812,14 +812,14 @@
         17: [lambda: second_pass(5, 3), second_end, lambda: start_all(op_load(kin_h, 7), op_load(x_h, 9))],
         18: [lambda: input_mm(15, 2, X), lambda: input_mm(16, 3, V)],
         19: [lambda: input_mm(17, 6, K), input_edge, lambda: op_load(x_h, 9).wait(), lambda: widen(9)],
-        20: [lambda: input_back(0, 8)],
-        21: [lambda: wait_from_right(edge(fs, fr, fsem, left)), lambda: input_back(8, 16), input_end],
+        20: [lambda: input_back(0, 4)],
+        21: [lambda: wait_from_right(edge(fs, fr, fsem, left)), lambda: input_back(4, 8), input_end],
         23: [sm1],
         24: [sm2],
         25: [sm3, lambda: smz(0)],
-        27: [lambda: smz(1)],
-        29: [lambda: smz(2)],
-        31: [sm_fin],
+        26: [lambda: smz(1)],
+        27: [lambda: smz(2)],
+        28: [sm_fin],
     }
     landed = {18: (gat_h, 4), 20: (rin_h, 5), 22: (vin_h, 8), 24: (kin_h, 7)}
 
@@ -1101,7 +1101,7 @@
     for cp in loads:
         cp.start()
     stores = []
-    for i in (9, 2, 3, 4, 5, 8, 6, 7, 0, 1):
+    for i in range(10):
         loads[i].wait()
         if i < 9:
             stores.append(pltpu.make_async_copy(scratch[i], outs[i], out.at[i]))

time: 260 us -> 256 us (0.985)
  Pallas kernels: 259 us -> 255 us
    pallas_call x1, Pallas kernels: 255 us -> 252 us  [block_call(): pl.pallas_call(block_kernel, out_shape=[S((T, D), BF)] * 2 + [S((128, 256...]
where the time goes in v5:
time: 256 us
  Pallas kernels  255 us (100%)
    pallas_call x1, Pallas kernels, block_call(): pl.pallas_call(block_kernel, out_shape=[S((T, D), BF)] * 2 + [S((128, 256...  252 us

profile of v5, /device:TPU:0, one launch (start us, length us, event | category | flops | bytes accessed | tf_op | source)
XLA Modules:
  0.0 256.1 jit_solution(18164845171028871448)
XLA Ops:
  0.7 251.7 %block.1 = (bf16[512,1024]{1,0:T(8,128)(2,1)}, bf16[512,1024]{1,0:T(8,128)(2,1)}, f32[128,256]{1,0:T(8,128)}, f32[128,256]{1,0:T(8,128)}, f32[128,256]{1,0:T(8,1...) custom-call(bf16[512,1024]{1,0:T(8,128)(2,1)} %bitcast.36, ...), custom_call_target="tpu_custom_call" | custom-call | tf_op jit(solution)/shard_map/block/pallas_call | solution.py:1076
  252.4 3.5 %finish.1 = (bf16[512,1024]{1,0:T(8,128)(2,1)}, bf16[512,1024]{1,0:T(8,128)(2,1)}, f32[128,256]{1,0:T(8,128)}, f32[128,256]{1,0:T(8,128)}, f32[128,256]{1,0:T(8,...) custom-call(bf16[512,1024]{1,0:T(8,128)(2,1)} %get-tuple-element.60., ...), custom_call_target="tpu_custom_call" | custom-call | tf_op jit(solution)/shard_map/finish/pallas_call | solution.py:1119

commit v6 on v5

--- a/solution.py
+++ b/solution.py
@@ -324,14 +324,14 @@
 
     stages = [
         (RETIRE, retire),
-        (LAGS[7], lambda k: zfin(k, True)),
-        (LAGS[8], taskSE),
-        (LAGS[6], lambda k: zsub(k, 2, True)),
-        (LAGS[5], lambda k: zsub(k, 1, True)),
+        (LAGS[7], lambda k: zfin(k, True), True),
+        (LAGS[8], taskSE, True),
+        (LAGS[6], lambda k: zsub(k, 2, True), True),
+        (LAGS[5], lambda k: zsub(k, 1, True), True),
         (LAGS[4], taskFinE),
         (LAGS[3], lambda k: zsub(k, 2, False)),
         (LAGS[2], lambda k: zsub(k, 1, False)),
-        (LAGS[1], taskSA),
+        (LAGS[1], taskSA, True),
         (1, task1),
         (LAGS[0], task2),
         (0, taskP),
@@ -438,29 +438,23 @@
     def gate_step():
         w_wait(4)
 
-        def mm(i, cols):
-            G[:, cols] = jnp.dot(ob[10], wbuf[4 % 3, :, cols], preferred_element_type=F32)
-
-        halves(mm)
+        G[...] = jnp.dot(ob[10], wbuf[4 % 3], preferred_element_type=F32)
         w_start(7)
 
         def body(i, rows):
             gate = jax.nn.sigmoid(G[rows, :])
             G[rows, :] = gate
-            ob[8, rows, :] = (spread(i, 4) * gate).astype(BF)
-
-        tiles(T // 32, 32, body)
+            ob[8, rows, :] = (spread(i, 8) * gate).astype(BF)
+
+        tiles(T // 64, 64, body)
 
     def hid(j):
         w_wait(5 + 2 * j)
         slot = (5 + 2 * j) % 3
 
-        def mm(i, cols):
-            up = jnp.maximum(jnp.dot(ob[9], wbuf[slot, :, cols], preferred_element_type=F32), 0.0)
-            X[pl.ds(0, T), cols] = up
-            ob[j, :, cols] = (up * up).astype(BF)
-
-        halves(mm)
+        up = jnp.maximum(jnp.dot(ob[9], wbuf[slot], preferred_element_type=F32), 0.0)
+        X[pl.ds(0, T), :] = up
+        ob[j] = (up * up).astype(BF)
 
     def gpre(j):
         w_wait(6 + 2 * j)
@@ -1016,8 +1010,17 @@
             def _(src=src, slot=slot):
                 op_load(src, slot).wait()
 
-        for lag, task in stages:
+        for lag, task, *early in stages:
             k = t - lag
+
+            if early:
+                def later(k, _, task=task):
+                    task(k)
+                    return 0
+
+                hurry = jnp.where(k >= NK - 3, 1, 0), jnp.where(k > NK - 3, 1, 0)
+                lax.fori_loop(jnp.clip(k + hurry[1], 0, NK), jnp.clip(k + 1 + hurry[0], 0, NK), later, 0)
+                continue
 
             @pl.when(jnp.logical_and(k >= (2 if lag < 2 else 0), k < NK))
             def _(k=k, task=task):

time: 256 us -> 255 us (level)
  no operation moved by 1% of the time
where the time goes in v6:
time: 255 us; the launch traced here: 254 us
  Pallas kernels  253 us (99%)
    pallas_call x1, Pallas kernels, block_call(): pl.pallas_call(block_kernel, out_shape=[S((T, D), BF)] * 2 + [S((128, 256...  250 us

profile of v6, /device:TPU:0, one launch (start us, length us, event | category | flops | bytes accessed | tf_op | source)
XLA Modules:
  0.0 254.1 jit_solution(6676100932306281070)
XLA Ops:
  0.7 249.8 %block.1 = (bf16[512,1024]{1,0:T(8,128)(2,1)}, bf16[512,1024]{1,0:T(8,128)(2,1)}, f32[128,256]{1,0:T(8,128)}, f32[128,256]{1,0:T(8,128)}, f32[128,256]{1,0:T(8,1...) custom-call(bf16[512,1024]{1,0:T(8,128)(2,1)} %bitcast.36, ...), custom_call_target="tpu_custom_call" | custom-call | tf_op jit(solution)/shard_map/block/pallas_call | solution.py:1079
  250.5 3.5 %finish.1 = (bf16[512,1024]{1,0:T(8,128)(2,1)}, bf16[512,1024]{1,0:T(8,128)(2,1)}, f32[128,256]{1,0:T(8,128)}, f32[128,256]{1,0:T(8,128)}, f32[128,256]{1,0:T(8,...) custom-call(bf16[512,1024]{1,0:T(8,128)(2,1)} %get-tuple-element.60., ...), custom_call_target="tpu_custom_call" | custom-call | tf_op jit(solution)/shard_map/finish/pallas_call | solution.py:1122
